TPU v7x, 256 devices: a whole 4x4x8 slice. The times are simulated.
256 devices in a mesh: grp: 4 (over x), dev: 64 (over z, y, core).
Axes of the slice: x: 4, y: 4, z: 8, core: 2. Of those that a mesh axis runs over, the one named last changes fastest.
Arguments:
- block_values: bfloat16 [3072, 9, 128, 128], P(('grp', 'dev')), may hold values from -0.1875 to 0.1875
- block_columns: int32 [3072, 9], P(('grp', 'dev')), may hold values from 0 to 17, as said below
- tentative: bfloat16 [3072, 128, 128], P(('grp', 'dev')), may hold values from -1.1953125 to 1.1953125
- inverse_diagonal: bfloat16 [3072, 128, 128], P(('grp', 'dev')), may hold values from -0.5 to 0.5
- aggregate: int32 [3072], P(('grp', 'dev')), may hold values from 0 to 1, as said below
- ghost_rows: int32 [256, 2, 3], P(('grp', 'dev')), may hold values from 0 to 11, as said below
- damping: float32 [1], replicated, may hold values from 0.5 to 0.8
Outputs:
- coarse_op: bfloat16 [512, 128, 1792], P(('grp', 'dev'))
Inputs may be any that keep to these rules, and one draw needn't show every extreme that they name: `block_columns`: in part n, row r names its own row r first; the 9 entries of a row differ; entries from 12 to 14 never stand in the first part, entries from 15 on never in the last. `aggregate`: each of the 2 aggregates of a part holds one or more of its rows. `ghost_rows`: the 3 rows of each list differ.
All inputs are finite; a program needn't handle non-finite values.
Results may differ from a plain program's by a relative error of at most 0.0068.
Values may be sent and summed in bfloat16 or wider, within the bound.
No kernel may reach another device: no remote copies, remote signals or barrier semaphores. Data moves between devices by JAX's collectives and lax.ppermute only.
A program may use at most 64 MiB of HBM per device.

v0:
```python
import jax
import jax.numpy as jnp
from jax import lax
from jax.sharding import PartitionSpec as P

CA = 2


def from_behind(block, axis, distance):
    devices = range(lax.axis_size(axis))
    route = [(i - distance, i) for i in devices if i - distance in devices]
    return lax.ppermute(block, axis, route)


def place_own(tentative, aggregate):
    aggregate_mask = aggregate[:, None] == jnp.arange(CA, dtype=jnp.int32)[None, :]
    spread = jnp.where(
        aggregate_mask[:, None, :, None], tentative[:, :, None, :], jnp.zeros((), tentative.dtype)
    )
    return spread.reshape(tentative.shape[0], tentative.shape[1], CA * tentative.shape[2])


def dense_rows(values, columns, lookup_rows):
    selector = (
        columns[:, :, None] == jnp.arange(lookup_rows, dtype=jnp.int32)[None, None, :]
    ).astype(values.dtype)
    return jnp.einsum(
        "rkl,rkab->rlab", selector, values, preferred_element_type=jnp.float32
    ).astype(values.dtype)


def assemble(dense, own_count, ghost_count, lookup, block_span):
    width = lookup.shape[2]
    middle = jnp.einsum(
        "rlab,lbc->rac",
        dense[:, :own_count],
        lookup[:own_count],
        preferred_element_type=jnp.float32,
    )
    left = jnp.einsum(
        "rlab,lbc->rac",
        dense[:, own_count : own_count + ghost_count],
        lookup[own_count : own_count + ghost_count],
        preferred_element_type=jnp.float32,
    )
    right = jnp.einsum(
        "rlab,lbc->rac",
        dense[:, own_count + ghost_count :],
        lookup[own_count + ghost_count :],
        preferred_element_type=jnp.float32,
    )
    total = jnp.pad(middle, ((0, 0), (0, 0), (block_span, block_span)))
    total = total.at[:, :, :width].add(left)
    total = total.at[:, :, 2 * block_span :].add(right)
    return total


def wanted_list(payload, offset):
    return from_behind(payload, ("grp", "dev"), offset)


def rim_tentative(payload, offset):
    return from_behind(payload, ("grp", "dev"), offset)


def rim_smoothed(payload, offset):
    return from_behind(payload, ("grp", "dev"), offset)


def coarse_part(payload, offset):
    return from_behind(payload.astype(jnp.bfloat16), ("grp", "dev"), offset).astype(payload.dtype)


def shards(
    block_values, block_columns, tentative, inverse_diagonal, aggregate, ghost_rows, damping
):
    row_count = block_columns.shape[0]
    block_width = tentative.shape[1]
    list_length = ghost_rows.shape[2]
    block_span = CA * block_width
    ghost_lists = ghost_rows[0]
    own_rows = place_own(tentative, aggregate)
    dense = dense_rows(block_values, block_columns, row_count + 2 * list_length)
    wanted_left = wanted_list(ghost_lists[1], 1)
    wanted_right = wanted_list(ghost_lists[0], -1)
    left_ghosts = rim_tentative(jnp.take(own_rows, wanted_right, axis=0), 1)
    right_ghosts = rim_tentative(jnp.take(own_rows, wanted_left, axis=0), -1)
    lookup = jnp.concatenate([own_rows, left_ghosts, right_ghosts], axis=0)
    smooth_sum = assemble(dense, row_count, list_length, lookup, block_span)
    smooth_half = smooth_sum.astype(jnp.bfloat16)
    scaled = jnp.einsum(
        "rab,rbc->rac", inverse_diagonal, smooth_half, preferred_element_type=jnp.float32
    )
    own_wide = jnp.pad(own_rows, ((0, 0), (0, 0), (block_span, block_span))).astype(jnp.float32)
    prolong = (own_wide - damping[0] * scaled).astype(jnp.bfloat16)
    left_smoothed = rim_smoothed(jnp.take(prolong, wanted_right, axis=0), 1)
    right_smoothed = rim_smoothed(jnp.take(prolong, wanted_left, axis=0), -1)
    prolong_lookup = jnp.concatenate([prolong, left_smoothed, right_smoothed], axis=0)
    applied = assemble(dense, row_count, list_length, prolong_lookup, block_span).astype(
        jnp.bfloat16
    )
    flat_prolong = prolong.reshape(row_count * block_width, 3 * block_span)
    flat_applied = applied.reshape(row_count * block_width, 5 * block_span)
    galerkin = lax.dot_general(
        flat_prolong, flat_applied, (((0,), (0,)), ((), ())), preferred_element_type=jnp.float32
    )
    from_right = coarse_part(galerkin[:block_span], -1)
    from_left = coarse_part(galerkin[2 * block_span :], 1)
    result = jnp.pad(galerkin[block_span : 2 * block_span], ((0, 0), (block_span, block_span)))
    result = result + jnp.pad(from_right, ((0, 0), (2 * block_span, 0)))
    result = result + jnp.pad(from_left, ((0, 0), (0, 2 * block_span)))
    return result.reshape(CA, block_width, 7 * block_span).astype(jnp.bfloat16)


def solution(mesh):
    return jax.shard_map(
        shards,
        mesh=mesh,
        in_specs=(
            P(("grp", "dev"), None, None, None),
            P(("grp", "dev"), None),
            P(("grp", "dev"), None, None),
            P(("grp", "dev"), None, None),
            P(("grp", "dev")),
            P(("grp", "dev"), None, None),
            P(),
        ),
        out_specs=P(("grp", "dev"), None, None),
        check_vma=False,
    )
```

profile of v0, /device:TPU:6, one launch (start us, length us, event | category | flops | bytes accessed | tf_op | source)
XLA Modules:
  0.0 126.0 jit_solution(15778285988902130582)
XLA Ops:
  0.0 1.4 %slice_bitcast_fusion = (s32[3]{0:T(128)}, s32[3]{0:T(128)S(1)}) fusion(s32[1,2,3]{2,1,0:T(2,128)} %param.24), kind=kLoop, calls=%fused_computation.52 | loop fusion | bytes 48 | tf_op jit(solution)/shard_map/squeeze | solution.py:84
  1.4 1.9 %collective-permute-start.2 = (s32[3]{0:T(128)}, s32[3]{0:T(128)S(1)}, u32[]{:S(2)}, u32[]{:S(2)}) collective-permute-start(s32[3]{0:T(128)} %get-tuple-element.59), channel_id=1, source_target_pairs={{0,1},{1,2},{2,3},{3,4},{4,5},{5,6},{6,7},{7,8},{8,9},{9,10},{10,1... | collective-permute-start | bytes 44 | tf_op jit(solution)/shard_map/ppermute | solution.py:12
  3.3 9.9 %collective-permute-start = (s32[3]{0:T(128)S(1)}, s32[3]{0:T(128)S(1)}, u32[]{:S(2)}, u32[]{:S(2)}) collective-permute-start(s32[3]{0:T(128)S(1)} %get-tuple-element.60), channel_id=1, source_target_pairs={{1,0},{2,1},{3,2},{4,3},{5,4},{6,5},{7,6},{8,7},{9,8},{10,9},{11,1... | collective-permute-start | bytes 44 | tf_op jit(solution)/shard_map/ppermute | solution.py:12
  13.3 5.1 %convolution_convert_fusion = bf16[12,18,128,128]{3,1,2,0:T(8,128)(2,1)S(1)} fusion(bf16[12,9,128,128]{3,2,1,0:T(8,128)(2,1)S(1)} %copy-done, s32[12,9]{1,0:T(8,128)} %param.20), kind=kOutput, calls=%fused_computation.4 | convolution fusion | flops 67241880 | bytes 10617264 | tf_op jit(solution)/shard_map/rkl,rkab->rlab/dot_general | solution.py:27
  18.4 3.4 %fusion.39 = (bf16[12,3,128,128]{3,1,2,0:T(4,128)(2,1)}, bf16[12,3,128,128]{3,1,2,0:T(4,128)(2,1)}) fusion(bf16[12,18,128,128]{3,1,2,0:T(8,128)(2,1)S(1)} %convolution_convert_fusion), kind=kLoop, calls=%fused_computation.54 | loop fusion | bytes 4718592 | tf_op jit(solution)/shard_map/slice | solution.py:48
  21.8 3.8 %slice.144 = bf16[12,12,128,128]{3,1,2,0:T(8,128)(2,1)} slice(bf16[12,18,128,128]{3,1,2,0:T(8,128)(2,1)S(1)} %convolution_convert_fusion), slice={[0:12], [0:12], [0:128], [0:128]} | slice | bytes 9437184 | tf_op jit(solution)/shard_map/slice | solution.py:36
  26.4 1.9 %copy.18 = bf16[12,128,128]{1,2,0:T(8,128)(2,1)} copy(bf16[12,128,128]{2,1,0:T(8,128)(2,1)} %param.21) | data formatting | bytes 786432 | tf_op args[2]
  28.3 2.2 %bitcast_select_fusion = bf16[12,128,256]{1,2,0:T(8,128)(2,1)} fusion(pred[12,256]{1,0:T(8,128)(4,1)S(1)} %bitcast.66, bf16[12,128,128]{1,2,0:T(8,128)(2,1)} %copy.18), kind=kLoop, calls=%fused_computation.33 | loop fusion | flops 393216 | bytes 1182720 | tf_op jit(solution)/shard_map/jit(_where)/select_n | solution.py:17
  30.6 2.3 %copy.22 = bf16[12,128,256]{2,1,0:T(8,128)(2,1)} copy(bf16[12,128,256]{1,2,0:T(8,128)(2,1)} %bitcast_select_fusion) | data formatting | bytes 1572864 | tf_op jit(solution)/shard_map/jit(_where)/select_n | solution.py:17
  32.9 4.4 %fusion.24 = f32[12,128,256]{2,1,0:T(8,128)S(1)} fusion(bf16[12,12,128,128]{3,1,2,0:T(8,128)(2,1)} %slice.144, bf16[12,128,256]{1,2,0:T(8,128)(2,1)} %bitcast_select_fusion), kind=kOutput, calls=%fused_computation.27 | convolution fusion | flops 1207959552 | bytes 7077888 | tf_op jit(solution)/shard_map/rlab,lbc->rac/dot_general | solution.py:34
  37.3 2.7 %pad.39 = f32[12,128,768]{2,1,0:T(8,128)} pad(f32[12,128,256]{2,1,0:T(8,128)S(1)} %fusion.24, f32[]{:T(128)} %constant.119.clone.1), padding=0_0x0_0x256_256 | pad | bytes 6291460 | tf_op jit(solution)/shard_map/jit(_pad)/pad | solution.py:52
  40.6 2.4 %gather_fusion.1 = bf16[3,128,256]{1,2,0:T(8,128)(2,1)} fusion(bf16[12,128,256]{1,2,0:T(8,128)(2,1)} %bitcast_select_fusion, s32[1024]{0:T(1024)S(1)} %pad_clamp_fusion), kind=kCustom, calls=%fused_computation.2.clone | custom fusion | bytes 393228 | tf_op jit(solution)/shard_map/jit(_take)/gather | solution.py:87
  43.0 2.4 %gather_fusion = bf16[3,128,256]{2,1,0:T(8,128)(2,1)} fusion(bf16[12,128,256]{2,1,0:T(8,128)(2,1)} %copy.22, s32[1024]{0:T(1024)S(1)} %pad_clamp_fusion.1), kind=kCustom, calls=%fused_computation.clone | custom fusion | bytes 393228 | tf_op jit(solution)/shard_map/jit(_take)/gather | solution.py:86
  47.2 1.9 %collective-permute-start.1 = (bf16[3,128,256]{2,1,0:T(8,128)(2,1)S(1)}, bf16[3,128,256]{2,1,0:T(8,128)(2,1)S(1)}, u32[]{:S(2)}, u32[]{:S(2)}) collective-permute-start(bf16[3,128,256]{2,1,0:T(8,128)(2,1)S(1)} %broadcast_select_fusion.3), channel_id=1, source_target_pairs={{0,1},{1,2},{2,3},{3,4},{4,5},{5,6},{6,7},{7,8},{8,9},{9,10},{10,1... | collective-permute-start | bytes 589832 | tf_op jit(solution)/shard_map/ppermute | solution.py:12
  50.1 7.9 %collective-permute-start.3 = (bf16[3,128,256]{1,2,0:T(8,128)(2,1)S(1)}, bf16[3,128,256]{1,2,0:T(8,128)(2,1)S(1)}, u32[]{:S(2)}, u32[]{:S(2)}) collective-permute-start(bf16[3,128,256]{1,2,0:T(8,128)(2,1)S(1)} %broadcast_select_fusion.2), channel_id=1, source_target_pairs={{1,0},{2,1},{3,2},{4,3},{5,4},{6,5},{7,6},{8,7},{9,8},{10,9},{11,1... | collective-permute-start | bytes 589832 | tf_op jit(solution)/shard_map/ppermute | solution.py:12
  58.4 3.3 %bitcast_dynamic-update-slice_fusion = f32[12,128,768]{2,1,0:T(8,128)} fusion(f32[12,128,768]{2,1,0:T(8,128)} %pad.39, bf16[12,3,128,128]{3,1,2,0:T(4,128)(2,1)} %get-tuple-element.56, bf16[3,128,256]{2,1,0:T(8,128)(2,1)S(1)} %collective-permute-done.1), kind=kOutput, calls=%fused_computation.26 | convolution fusion | flops 301989888 | bytes 3342336 | tf_op jit(solution)/shard_map/rlab,lbc->rac/dot_general | solution.py:40
  61.7 3.3 %fusion.23 = f32[12,128,768]{2,1,0:T(8,128)} fusion(f32[12,128,768]{2,1,0:T(8,128)} %bitcast_dynamic-update-slice_fusion, bf16[12,3,128,128]{3,1,2,0:T(4,128)(2,1)S(1)} %copy-done.1, bf16[3,128,256]{1,2,0:T(8,128)(2,1)S(1)} %collective-permute-done.3), kind=kOutput, calls=%fused_computation.25 | convolution fusion | flops 302383104 | bytes 4521984 | tf_op jit(solution)/shard_map/rlab,lbc->rac/dot_general | solution.py:46
  65.0 4.9 %fusion.3 = bf16[12,128,768]{1,2,0:T(8,128)(2,1)} fusion(f32[]{:T(128)} %bitcast.64, bf16[12,128,256]{1,2,0:T(8,128)(2,1)S(1)} %copy-done.4, bf16[12,128,128]{2,1,0:T(8,128)(2,1)S(1)} %copy-done.6, f32[12,128,768]{2,1,0:T(8,128)} %fusion.23), kind=kOutput, calls=%fused_computation.11 | convolution fusion | flops 307888128 | bytes 8257540 | tf_op jit(solution)/shard_map/rab,rbc->rac/dot_general | solution.py:91
  69.9 3.1 %gather_fusion.3 = bf16[3,128,768]{1,2,0:T(8,128)(2,1)} fusion(bf16[12,128,768]{1,2,0:T(8,128)(2,1)} %fusion.3, s32[1024]{0:T(1024)S(1)} %pad_clamp_fusion), kind=kCustom, calls=%fused_computation.3.clone | custom fusion | bytes 1179660 | tf_op jit(solution)/shard_map/jit(_take)/gather | solution.py:97
  73.0 3.1 %gather_fusion.2 = bf16[3,128,768]{1,2,0:T(8,128)(2,1)} fusion(bf16[12,128,768]{1,2,0:T(8,128)(2,1)} %fusion.3, s32[1024]{0:T(1024)S(1)} %pad_clamp_fusion.1), kind=kCustom, calls=%fused_computation.1.clone | custom fusion | bytes 1179660 | tf_op jit(solution)/shard_map/jit(_take)/gather | solution.py:96
  76.2 1.2 broadcast_select_fusion
  77.3 1.2 broadcast_select_fusion.1
  78.5 1.9 %collective-permute-start.4 = (bf16[3,128,768]{1,2,0:T(8,128)(2,1)S(1)}, bf16[3,128,768]{1,2,0:T(8,128)(2,1)S(1)}, u32[]{:S(2)}, u32[]{:S(2)}) collective-permute-start(bf16[3,128,768]{1,2,0:T(8,128)(2,1)S(1)} %broadcast_select_fusion.1), channel_id=1, source_target_pairs={{0,1},{1,2},{2,3},{3,4},{4,5},{5,6},{6,7},{7,8},{8,9},{9,10},{10,1... | collective-permute-start | bytes 1769480 | tf_op jit(solution)/shard_map/ppermute | solution.py:12
  80.5 8.0 %collective-permute-start.5 = (bf16[3,128,768]{1,2,0:T(8,128)(2,1)S(1)}, bf16[3,128,768]{1,2,0:T(8,128)(2,1)S(1)}, u32[]{:S(2)}, u32[]{:S(2)}) collective-permute-start(bf16[3,128,768]{1,2,0:T(8,128)(2,1)S(1)} %broadcast_select_fusion), channel_id=1, source_target_pairs={{1,0},{2,1},{3,2},{4,3},{5,4},{6,5},{7,6},{8,7},{9,8},{10,9},{11,1... | collective-permute-start | bytes 1769480 | tf_op jit(solution)/shard_map/ppermute | solution.py:12
  88.5 7.3 %fusion.16 = f32[12,128,768]{2,1,0:T(8,128)S(1)} fusion(bf16[12,128,768]{1,2,0:T(8,128)(2,1)} %fusion.3, bf16[12,12,128,128]{3,1,2,0:T(8,128)(2,1)} %slice.144), kind=kOutput, calls=%fused_computation.22 | convolution fusion | flops 3623878656 | bytes 11796480 | tf_op jit(solution)/shard_map/rlab,lbc->rac/dot_general | solution.py:34
  97.2 1.6 %fusion.2 = f32[12,128,1280]{2,1,0:T(8,128)S(1)} fusion(f32[12,128,1280]{2,1,0:T(8,128)S(1)} %pad.40, bf16[12,3,128,128]{3,1,2,0:T(4,128)(2,1)S(1)} %copy-done.3, bf16[3,128,768]{1,2,0:T(8,128)(2,1)S(1)} %collective-permute-done.4), kind=kOutput, calls=%fused_computation.9 | convolution fusion | flops 907149312 | bytes 11599872 | tf_op jit(solution)/shard_map/rlab,lbc->rac/dot_general | solution.py:40
  98.9 1.6 %fusion.1 = f32[12,128,1280]{2,1,0:T(8,128)S(1)} fusion(f32[12,128,1280]{2,1,0:T(8,128)S(1)} %fusion.2, bf16[12,3,128,128]{3,1,2,0:T(4,128)(2,1)S(1)} %copy-done.2, bf16[3,128,768]{1,2,0:T(8,128)(2,1)S(1)} %collective-permute-done.5), kind=kOutput, calls=%fused_computation.7 | convolution fusion | flops 907149312 | bytes 11599872 | tf_op jit(solution)/shard_map/rlab,lbc->rac/dot_general | solution.py:46
  100.6 3.3 %fusion.41 = (bf16[768,1280]{1,0:T(8,128)(2,1)S(1)}, f32[768,1280]{1,0:T(8,128)S(1)}) fusion(bf16[12,128,768]{1,2,0:T(8,128)(2,1)S(1)} %copy-done.5, f32[12,128,1280]{2,1,0:T(8,128)S(1)} %fusion.1), kind=kOutput, calls=%fused_computation.56 | convolution fusion | flops 3022848000 | bytes 16121856 | tf_op jit(solution)/shard_map/dot_general | solution.py:104
  103.9 4.8 %collective-permute-start.6 = (bf16[256,1280]{1,0:T(8,128)(2,1)S(1)}, bf16[256,1280]{1,0:T(8,128)(2,1)S(1)}, u32[]{:S(2)}, u32[]{:S(2)}) collective-permute-start(bf16[256,1280]{1,0:T(8,128)(2,1)S(1)} %get-tuple-element.57), channel_id=1, source_target_pairs={{1,0},{2,1},{3,2},{4,3},{5,4},{6,5},{7,6},{8,7},{9,8},{10,9},{11,1... | collective-permute-start | bytes 1966088 | tf_op jit(solution)/shard_map/ppermute | solution.py:12
  108.8 1.9 %collective-permute-start.7 = (bf16[256,1280]{1,0:T(8,128)(2,1)S(1)}, bf16[256,1280]{1,0:T(8,128)(2,1)S(1)}, u32[]{:S(2)}, u32[]{:S(2)}) collective-permute-start(bf16[256,1280]{1,0:T(8,128)(2,1)S(1)} %get-tuple-element.58), channel_id=1, source_target_pairs={{0,1},{1,2},{2,3},{3,4},{4,5},{5,6},{6,7},{7,8},{8,9},{9,10},{10,1... | collective-permute-start | bytes 1966088 | tf_op jit(solution)/shard_map/ppermute | solution.py:12
  110.8 6.1 %collective-permute-done.6 = bf16[256,1280]{1,0:T(8,128)(2,1)S(1)} collective-permute-done((bf16[256,1280]{1,0:T(8,128)(2,1)S(1)}, bf16[256,1280]{1,0:T(8,128)(2,1)S(1)}, u32[]{:S(2)}, u32[]{:S(2)}) %collective-permute-start.6) | collective-permute-done | bytes 655392 | tf_op jit(solution)/shard_map/ppermute | solution.py:12
  116.9 8.0 %collective-permute-done.7 = bf16[256,1280]{1,0:T(8,128)(2,1)S(1)} collective-permute-done((bf16[256,1280]{1,0:T(8,128)(2,1)S(1)}, bf16[256,1280]{1,0:T(8,128)(2,1)S(1)}, u32[]{:S(2)}, u32[]{:S(2)}) %collective-permute-start.7) | collective-permute-done | bytes 655392 | tf_op jit(solution)/shard_map/ppermute | solution.py:12
  (41 shorter events, 6.6 us)
Async XLA Ops:
  0.0 13.3 %copy-start = (bf16[12,9,128,128]{3,2,1,0:T(8,128)(2,1)S(1)}, bf16[12,9,128,128]{3,2,1,0:T(8,128)(2,1)}, u32[]{:S(2)}) copy-start(bf16[12,9,128,128]{3,2,1,0:T(8,128)(2,1)} %param.19) | copy-start | bytes 10616836
  1.4 38.5 %collective-permute-start.2 = (s32[3]{0:T(128)}, s32[3]{0:T(128)S(1)}, u32[]{:S(2)}, u32[]{:S(2)}) collective-permute-start(s32[3]{0:T(128)} %get-tuple-element.59), channel_id=1, source_target_pairs={{0,1},{1,2},{2,3},{3,4},{4,5},{5,6},{6,7},{7,8},{8,9},{9,10},{10,1... | collective-permute-start | bytes 44 | tf_op jit(solution)/shard_map/ppermute | solution.py:12
  3.3 36.7 %collective-permute-start = (s32[3]{0:T(128)S(1)}, s32[3]{0:T(128)S(1)}, u32[]{:S(2)}, u32[]{:S(2)}) collective-permute-start(s32[3]{0:T(128)S(1)} %get-tuple-element.60), channel_id=1, source_target_pairs={{1,0},{2,1},{3,2},{4,3},{5,4},{6,5},{7,6},{8,7},{9,8},{10,9},{11,1... | collective-permute-start | bytes 44 | tf_op jit(solution)/shard_map/ppermute | solution.py:12
  21.8 4.4 %copy-start.7 = (s32[12]{0:T(128)S(1)}, s32[12]{0:T(128)}, u32[]{:S(2)}) copy-start(s32[12]{0:T(128)} %param.23) | copy-start | bytes 148
  40.0 0.6 copy-start.8
  40.6 2.4 %copy-start.9 = (s32[3]{0:T(128)}, s32[3]{0:T(128)S(1)}, u32[]{:S(2)}) copy-start(s32[3]{0:T(128)S(1)} %collective-permute-done) | copy-start | bytes 40
  45.4 16.3 %copy-start.1 = (bf16[12,3,128,128]{3,1,2,0:T(4,128)(2,1)S(1)}, bf16[12,3,128,128]{3,1,2,0:T(4,128)(2,1)}, u32[]{:S(2)}) copy-start(bf16[12,3,128,128]{3,1,2,0:T(4,128)(2,1)} %get-tuple-element.55) | copy-start | bytes 3538948
  47.2 11.2 %collective-permute-start.1 = (bf16[3,128,256]{2,1,0:T(8,128)(2,1)S(1)}, bf16[3,128,256]{2,1,0:T(8,128)(2,1)S(1)}, u32[]{:S(2)}, u32[]{:S(2)}) collective-permute-start(bf16[3,128,256]{2,1,0:T(8,128)(2,1)S(1)} %broadcast_select_fusion.3), channel_id=1, source_target_pairs={{0,1},{1,2},{2,3},{3,4},{4,5},{5,6},{6,7},{7,8},{8,9},{9,10},{10,1... | collective-permute-start | bytes 589832 | tf_op jit(solution)/shard_map/ppermute | solution.py:12
  50.1 11.6 %collective-permute-start.3 = (bf16[3,128,256]{1,2,0:T(8,128)(2,1)S(1)}, bf16[3,128,256]{1,2,0:T(8,128)(2,1)S(1)}, u32[]{:S(2)}, u32[]{:S(2)}) collective-permute-start(bf16[3,128,256]{1,2,0:T(8,128)(2,1)S(1)} %broadcast_select_fusion.2), channel_id=1, source_target_pairs={{1,0},{2,1},{3,2},{4,3},{5,4},{6,5},{7,6},{8,7},{9,8},{10,9},{11,1... | collective-permute-start | bytes 589832 | tf_op jit(solution)/shard_map/ppermute | solution.py:12
  58.4 6.6 %copy-start.4 = (bf16[12,128,256]{1,2,0:T(8,128)(2,1)S(1)}, bf16[12,128,256]{1,2,0:T(8,128)(2,1)}, u32[]{:S(2)}) copy-start(bf16[12,128,256]{1,2,0:T(8,128)(2,1)} %bitcast_select_fusion) | copy-start | bytes 2359300
  58.4 6.6 %copy-start.6 = (bf16[12,128,128]{2,1,0:T(8,128)(2,1)S(1)}, bf16[12,128,128]{2,1,0:T(8,128)(2,1)}, u32[]{:S(2)}) copy-start(bf16[12,128,128]{2,1,0:T(8,128)(2,1)} %param.22) | copy-start | bytes 1179652
  78.5 18.1 %collective-permute-start.4 = (bf16[3,128,768]{1,2,0:T(8,128)(2,1)S(1)}, bf16[3,128,768]{1,2,0:T(8,128)(2,1)S(1)}, u32[]{:S(2)}, u32[]{:S(2)}) collective-permute-start(bf16[3,128,768]{1,2,0:T(8,128)(2,1)S(1)} %broadcast_select_fusion.1), channel_id=1, source_target_pairs={{0,1},{1,2},{2,3},{3,4},{4,5},{5,6},{6,7},{7,8},{8,9},{9,10},{10,1... | collective-permute-start | bytes 1769480 | tf_op jit(solution)/shard_map/ppermute | solution.py:12
  80.5 18.4 %collective-permute-start.5 = (bf16[3,128,768]{1,2,0:T(8,128)(2,1)S(1)}, bf16[3,128,768]{1,2,0:T(8,128)(2,1)S(1)}, u32[]{:S(2)}, u32[]{:S(2)}) collective-permute-start(bf16[3,128,768]{1,2,0:T(8,128)(2,1)S(1)} %broadcast_select_fusion), channel_id=1, source_target_pairs={{1,0},{2,1},{3,2},{4,3},{5,4},{6,5},{7,6},{8,7},{9,8},{10,9},{11,1... | collective-permute-start | bytes 1769480 | tf_op jit(solution)/shard_map/ppermute | solution.py:12
  95.8 1.4 %copy-start.3 = (bf16[12,3,128,128]{3,1,2,0:T(4,128)(2,1)S(1)}, bf16[12,3,128,128]{3,1,2,0:T(4,128)(2,1)}, u32[]{:S(2)}) copy-start(bf16[12,3,128,128]{3,1,2,0:T(4,128)(2,1)} %get-tuple-element.56) | copy-start | bytes 3538948
  96.6 2.3 %copy-start.2 = (bf16[12,3,128,128]{3,1,2,0:T(4,128)(2,1)S(1)}, bf16[12,3,128,128]{3,1,2,0:T(4,128)(2,1)}, u32[]{:S(2)}) copy-start(bf16[12,3,128,128]{3,1,2,0:T(4,128)(2,1)} %get-tuple-element.55) | copy-start | bytes 3538948
  98.9 1.7 %copy-start.5 = (bf16[12,128,768]{1,2,0:T(8,128)(2,1)S(1)}, bf16[12,128,768]{1,2,0:T(8,128)(2,1)}, u32[]{:S(2)}) copy-start(bf16[12,128,768]{1,2,0:T(8,128)(2,1)} %fusion.3) | copy-start | bytes 7077892
  103.9 12.9 %collective-permute-start.6 = (bf16[256,1280]{1,0:T(8,128)(2,1)S(1)}, bf16[256,1280]{1,0:T(8,128)(2,1)S(1)}, u32[]{:S(2)}, u32[]{:S(2)}) collective-permute-start(bf16[256,1280]{1,0:T(8,128)(2,1)S(1)} %get-tuple-element.57), channel_id=1, source_target_pairs={{1,0},{2,1},{3,2},{4,3},{5,4},{6,5},{7,6},{8,7},{9,8},{10,9},{11,1... | collective-permute-start | bytes 1966088 | tf_op jit(solution)/shard_map/ppermute | solution.py:12
  108.8 16.1 %collective-permute-start.7 = (bf16[256,1280]{1,0:T(8,128)(2,1)S(1)}, bf16[256,1280]{1,0:T(8,128)(2,1)S(1)}, u32[]{:S(2)}, u32[]{:S(2)}) collective-permute-start(bf16[256,1280]{1,0:T(8,128)(2,1)S(1)} %get-tuple-element.58), channel_id=1, source_target_pairs={{0,1},{1,2},{2,3},{3,4},{4,5},{5,6},{6,7},{7,8},{8,9},{9,10},{10,1... | collective-permute-start | bytes 1966088 | tf_op jit(solution)/shard_map/ppermute | solution.py:12
where the time goes:
time: 127 us; the launch traced here: 126 us
  starting transfers between devices  38.3 us (30%)
  matrix products  34.8 us (27%)
  local copies, waits for them, and re-layouts  28.8 us (23%)
  waiting for transfers between devices  14.5 us (11%)
  other arithmetic  8.63 us (7%)
    ppermute x8, starting transfers between devices, from_behind(): return lax.ppermute(block, axis, route)  38.3 us
    ppermute x8, waiting for transfers between devices, from_behind(): return lax.ppermute(block, axis, route)  14.5 us
    dot_general x2, matrix products, assemble(): jnp.einsum('rlab,lbc->rac', dense[:, :own_count], lookup[:own_count], pre...  11.7 us
    dot_general x1, matrix products, dense_rows(): jnp.einsum('rkl,rkab->rlab', selector, values, preferred_element_type=jnp...  5.07 us
    dot_general x1, matrix products, shards(): jnp.einsum('rab,rbc->rac', inverse_diagonal, smooth_half, preferred_eleme...  4.94 us
    dot_general x2, matrix products, assemble(): jnp.einsum('rlab,lbc->rac', dense[:, own_count:own_count + ghost_count],...  4.94 us
    dot_general x2, matrix products, assemble(): jnp.einsum('rlab,lbc->rac', dense[:, own_count + ghost_count:], lookup[ow...  4.9 us
    slice x1, local copies, waits for them, and re-layouts, assemble(): dense[:, :own_count]  3.76 us
  transfers between devices with their start and end apart: 8, of which 3 were waited for; matrix products, arithmetic and copies ran while one was open for 32% of the time, Pallas kernels for 0%

commit v1 on v0

v1 whole, which is shorter than its diff:
```python
import functools

import jax
import jax.numpy as jnp
from jax import lax
from jax.experimental import pallas as pl
from jax.experimental.pallas import tpu as pltpu
from jax.sharding import PartitionSpec as P

CA = 2
META = 32
AXES = ("grp", "dev")
VMEM = pltpu.VMEM
SMEM = pltpu.SMEM
F32 = jnp.float32
BF16 = jnp.bfloat16


SPACES = {"v": VMEM, "s": SMEM, "h": pltpu.HBM}


def call(kernel, args, spaces, outs, scratch=(), flops=1, limit=None):
    nbytes = sum(a.size * a.dtype.itemsize for a in args)
    in_specs = [pl.BlockSpec(memory_space=SPACES[c]) for c in spaces]
    return pl.pallas_call(
        kernel,
        out_shape=[jax.ShapeDtypeStruct(*o) for o in outs],
        in_specs=in_specs,
        out_specs=[pl.BlockSpec(memory_space=VMEM) for _ in outs],
        scratch_shapes=list(scratch),
        cost_estimate=pl.CostEstimate(flops=flops, bytes_accessed=nbytes, transcendentals=0),
        compiler_params=pltpu.CompilerParams(vmem_limit_bytes=limit),
    )(*[pltpu.with_memory_space_constraint(a, pltpu.HBM) if c == "h" else a for a, c in zip(args, spaces)])


def rows(index, size):
    return pl.ds(pl.multiple_of(index * size, size), size)


def dot(a, b):
    return jnp.dot(a, b, preferred_element_type=F32)


def pack_kernel(r, b, s, agg_hbm, ghost_hbm, tent_hbm, out, agg, ghost, sems):
    copies = [
        pltpu.make_async_copy(agg_hbm, agg, sems.at[0]),
        pltpu.make_async_copy(ghost_hbm, ghost, sems.at[1]),
        pltpu.make_async_copy(tent_hbm, out.at[: r * b, :], sems.at[2]),
    ]
    for copy in copies:
        copy.start()
    copies[0].wait()
    copies[1].wait()
    sub = lax.broadcasted_iota(jnp.int32, (META, b), 0)
    meta = jnp.zeros((META, b), F32)
    for j in range(r):
        meta = jnp.where(sub == j, agg[j].astype(F32), meta)
    for side in range(2):
        for j in range(s):
            meta = jnp.where(sub == 16 + 8 * side + j, ghost[0, side, j].astype(F32), meta)
    out[r * b :, :] = meta.astype(BF16)
    copies[2].wait()


def own_kernel(
    r, k, b, s, cols_hbm, agg_hbm, par, damp, vals_hbm, inv_hbm, pay, dense, inv, p_own, cols, agg, vals, placed, sems
):
    def fetch(j):
        return pltpu.make_async_copy(vals_hbm.at[j], vals.at[j], sems.at[j])

    others = [
        pltpu.make_async_copy(cols_hbm, cols, sems.at[r]),
        pltpu.make_async_copy(agg_hbm, agg, sems.at[r + 1]),
        pltpu.make_async_copy(inv_hbm, inv, sems.at[r + 2]),
    ]
    others[0].start()
    others[1].start()
    for j in range(r):
        fetch(j).start()
    others[2].start()

    def clear(j, carry):
        dense[rows(j, b), :] = jnp.zeros((b, (r + 2 * s) * b), BF16)
        return carry

    lax.fori_loop(0, r, clear, 0)
    others[0].wait()
    others[1].wait()
    zero = jnp.zeros((b, b), BF16)
    for j in range(r):
        own = slice(j * b, (j + 1) * b)
        block = pay[own, :]
        here = agg[j]
        for c in range(CA):
            placed[own, c * b : (c + 1) * b] = jnp.where(here == c, block, zero)
    odd = par[0]
    left = s * (1 - odd)

    def row(j, carry):
        fetch(j).wait()
        at = rows(j, b)
        for e in range(k):
            c = cols[j, e]
            c = jnp.where(c < r, c, jnp.where(c < r + s, c + left, c - left))
            dense[at, rows(c, b)] = vals[j, e]
        return carry

    lax.fori_loop(0, r, row, 0)
    others[2].wait()
    step = 4

    def smooth(t, carry):
        half = dot(dense[rows(t, step * b), : r * b], placed[...]).astype(BF16)
        for q in range(step):
            at = rows(t * step + q, b)
            scaled = dot(inv[at, :], half[q * b : (q + 1) * b, :])
            p_own[at, :] = (placed[at, :].astype(F32) - damp[0] * scaled).astype(BF16)
        return carry

    lax.fori_loop(0, r // step, smooth, 0)


def ghost_kernel(r, b, s, ghost, par, damp, dense, inv, p_own, pay_s, pay_x, p_s, p_x, out_s, out_x, meta, placed):
    odd = par[0]
    sides = ((pay_s, 1 - odd, odd), (pay_x, odd, 1 - odd))
    for d, (pay, mine, _) in enumerate(sides):
        meta[d] = pay[r * b :, :].astype(F32)
        for j in range(s):
            row = jnp.clip(ghost[0, mine, j], 0, r - 1)
            block = pay[rows(row, b), :]
            here = jnp.broadcast_to(meta[d, pl.ds(row, 1), :], (b, b))
            at = slice((d * s + j) * b, (d * s + j + 1) * b)
            for c in range(CA):
                placed[at, c * b : (c + 1) * b] = jnp.where(here == c, block.astype(F32), 0.0).astype(BF16)
    step = 4
    for d, target in enumerate((p_s, p_x)):
        span = slice(d * s * b, (d + 1) * s * b)
        cols = slice((r + d * s) * b, (r + d * s + s) * b)

        def smooth(t, carry):
            half = dot(dense[rows(t, step * b), cols], placed[span, :]).astype(BF16)
            for q in range(step):
                at = rows(t * step + q, b)
                scaled = dot(inv[at, :], half[q * b : (q + 1) * b, :])
                target[at, :] = (-damp[0] * scaled).astype(BF16)
            return carry

        lax.fori_loop(0, r // step, smooth, 0)
    w = CA * b
    for d, (_, mine, theirs) in enumerate(sides):
        out = (out_s, out_x)[d]
        for j in range(s):
            wanted = meta[d, pl.ds(16 + 8 * theirs + j, 1), :]
            row = jnp.clip(jnp.max(wanted).astype(jnp.int32), 0, r - 1)
            at = rows(row, b)
            to = slice(j * b, (j + 1) * b)
            out[to, :w] = p_s[at, :]
            out[to, w : 2 * w] = p_own[at, :]
            out[to, 2 * w :] = p_x[at, :]


def middle_kernel(r, b, w, dense, p_s, p_own, p_x, gal, wide, flipped, applied):
    parts = (p_s, p_own, p_x)
    for d, p in enumerate(parts):
        for j in range(r):
            at = slice(j * b, (j + 1) * b)
            flipped[d * w : (d + 1) * w, at] = p[at, :].T
    step = 4

    def apply(t, carry):
        at = rows(t, step * b)
        block = dense[at, : r * b]
        for d, p in enumerate(parts):
            applied[at, d * w : (d + 1) * w] = dot(block, p[...]).astype(BF16)
        return carry

    lax.fori_loop(0, r // step, apply, 0)

    def galerkin(t, carry):
        at = rows(t, w)
        left = flipped[at, :]
        gal[at, :] = dot(left, applied[...])
        wide[at, :] = dot(left, dense[:, r * b :]).astype(BF16)
        return carry

    lax.fori_loop(0, 3, galerkin, 0)


def galerkin_rows(index, w, span, gal, wide, far_s, far_x, write):
    at = slice(index * w, (index + 1) * w)
    left_s = wide[at, :span]
    left_x = wide[at, span:]
    by_s = dot(left_s, far_s[...])
    by_x = dot(left_x, far_x[...])
    write(0, by_s[:, 2 * w :])
    write(1, gal[at, :w] + by_s[:, w : 2 * w])
    write(2, gal[at, w : 2 * w] + by_s[:, :w] + by_x[:, 2 * w :])
    write(3, gal[at, 2 * w :] + by_x[:, w : 2 * w])
    write(4, by_x[:, :w])


def outer_kernel(w, span, gal, wide, far_s, far_x, out_x, out_s):
    for index, out in ((2, out_x), (0, out_s)):
        def write(c, value, out=out):
            out[:, c * w : (c + 1) * w] = value.astype(BF16)

        galerkin_rows(index, w, span, gal, wide, far_s, far_x, write)


def inner_kernel(w, span, gal, wide, far_s, far_x, out):
    def write(c, value):
        out[:, c * w : (c + 1) * w] = value

    galerkin_rows(1, w, span, gal, wide, far_s, far_x, write)


def final_kernel(w, par, mine, from_s, from_x, out):
    sign = 1 - 2 * par[0]
    for u in range(-3, 4):
        total = None
        for ref, at in ((mine, 2 - u), (from_s, 1 + u), (from_x, 3 + u)):
            if 0 <= at < 5:
                term = ref[:, at * w : (at + 1) * w].astype(F32)
                total = term if total is None else total + term
        out[:, rows(3 + sign * u, w)] = total.astype(BF16)


def swap(x, route):
    return lax.ppermute(x, AXES, route)


def shards(block_values, block_columns, tentative, inverse_diagonal, aggregate, ghost_rows, damping):
    r, k = block_columns.shape
    b = tentative.shape[1]
    s = ghost_rows.shape[2]
    w = CA * b
    span = s * b
    devices = lax.axis_size(AXES)
    chip = [(i, i ^ 1) for i in range(devices) if i ^ 1 < devices]
    cross = []
    for i in range(1, devices - 1, 2):
        cross += [(i, i + 1), (i + 1, i)]
    par = (lax.axis_index(AXES) % 2).astype(jnp.int32).reshape(1)
    tent = tentative.reshape(r * b, b)
    inv = inverse_diagonal.reshape(r * b, b)
    dma = pltpu.SemaphoreType.DMA

    (pay,) = call(
        functools.partial(pack_kernel, r, b, s), (aggregate, ghost_rows, tent), "hhh",
        [((r * b + META, b), BF16)],
        scratch=[SMEM((r,), jnp.int32), SMEM((1, 2, s), jnp.int32), dma((3,))], limit=2 << 20,
    )
    pay_x = swap(pay, cross)
    pay_s = swap(pay, chip)
    dense, inv, p_own = call(
        functools.partial(own_kernel, r, k, b, s),
        (block_columns, aggregate, par, damping, block_values, inv, pay), "hhsshhv",
        [((r * b, (r + 2 * s) * b), BF16), ((r * b, b), BF16), ((r * b, w), BF16)],
        scratch=[
            SMEM((r, k), jnp.int32), SMEM((r,), jnp.int32), VMEM((r, k, b, b), BF16), VMEM((r * b, w), BF16),
            dma((r + 3,)),
        ],
        flops=2 * r * b * r * b * w, limit=24 << 20,
    )
    p_s, p_x, out_s, out_x = call(
        functools.partial(ghost_kernel, r, b, s),
        (ghost_rows, par, damping, dense, inv, p_own, pay_s, pay_x), "sssvvvvv",
        [((r * b, w), BF16), ((r * b, w), BF16), ((span, 3 * w), BF16), ((span, 3 * w), BF16)],
        scratch=[VMEM((2, META, b), F32), VMEM((2 * span, w), BF16)],
        flops=2 * r * b * 2 * span * w, limit=24 << 20,
    )
    far_x = swap(out_x, cross)
    far_s = swap(out_s, chip)
    gal, wide = call(
        functools.partial(middle_kernel, r, b, w), (dense, p_s, p_own, p_x), "vvvv",
        [((3 * w, 3 * w), F32), ((3 * w, 2 * span), BF16)],
        scratch=[VMEM((3 * w, r * b), BF16), VMEM((r * b, 3 * w), BF16)],
        flops=6 * r * b * r * b * w, limit=24 << 20,
    )
    sum_x, sum_s = call(
        functools.partial(outer_kernel, w, span), (gal, wide, far_s, far_x), "vvvv",
        [((w, 5 * w), BF16), ((w, 5 * w), BF16)], flops=8 * w * span * 3 * w, limit=16 << 20,
    )
    from_x = swap(sum_x, cross)
    from_s = swap(sum_s, chip)
    (mine,) = call(
        functools.partial(inner_kernel, w, span), (gal, wide, far_s, far_x), "vvvv",
        [((w, 5 * w), F32)], flops=4 * w * span * 3 * w, limit=16 << 20,
    )
    (out,) = call(
        functools.partial(final_kernel, w), (par, mine, from_s, from_x), "svvv",
        [((w, 7 * w), BF16)], flops=w * 7 * w, limit=16 << 20,
    )
    return out.reshape(CA, b, 7 * w)


def solution(mesh):
    return jax.shard_map(
        shards,
        mesh=mesh,
        in_specs=(
            P(AXES, None, None, None),
            P(AXES, None),
            P(AXES, None, None),
            P(AXES, None, None),
            P(AXES),
            P(AXES, None, None),
            P(),
        ),
        out_specs=P(AXES, None, None),
        check_vma=False,
    )
```

time: 127 us -> 56.3 us (0.44)
  matrix products: 34.8 us -> 0 us
  local copies, waits for them, and re-layouts: 28.8 us -> 0.01 us
  Pallas kernels: 0 us -> 21.5 us
  starting transfers between devices: 38.3 us -> 24.5 us
  other arithmetic: 8.63 us -> 0 us
  waiting for transfers between devices: 14.5 us -> 9.31 us
    dot_general x9 -> x0, matrix products: 34.8 us -> none  [the longest x2 11.7 us: assemble(): jnp.einsum('rlab,lbc->rac', dense[:, :own_count], lookup[:own_count], pre...]
    pallas_call x0 -> x7, Pallas kernels: none -> 21.5 us  [call(): pl.pallas_call(kernel, out_shape=[jax.ShapeDtypeStruct(*o) for o in outs]...]
    ppermute x8 -> x6, starting transfers between devices: 38.3 us -> 24.5 us  [swap(): return lax.ppermute(x, AXES, route)]
    gather x4 -> x0, local copies, waits for them, and re-layouts: 11 us -> none  [the longest x1 3.14 us: shards(): right_smoothed = rim_smoothed(jnp.take(prolong, wanted_left, axis=0), -1)]
    slice x4 -> x0, local copies, waits for them, and re-layouts: 7.38 us -> none  [the longest x1 3.76 us: assemble(): dense[:, :own_count]]
    select_n x7 -> x0, other arithmetic: 6.65 us -> none  [the longest x1 2.24 us: place_own(): jnp.where(aggregate_mask[:, None, :, None], tentative[:, :, None, :], jnp...]
    ppermute x8 -> x6, waiting for transfers between devices: 14.5 us -> 9.31 us  [swap(): return lax.ppermute(x, AXES, route)]
    pad x2 -> x0, local copies, waits for them, and re-layouts: 3.46 us -> none  [assemble(): total = jnp.pad(middle, ((0, 0), (0, 0), (block_span, block_span)))]
  transfers between devices with their start and end apart: 8 -> 6, of which waited for: 3 -> 2; matrix products, arithmetic and copies ran while one was open for 32% -> 0% of each run, Pallas kernels for 0% -> 25%
where the time goes in v1:
time: 56.3 us; the launch traced here: 56.1 us
  starting transfers between devices  24.5 us (44%)
  Pallas kernels  21.5 us (38%)
  waiting for transfers between devices  9.31 us (17%)
  between operations  0.78 us (1%)
    ppermute x6, starting transfers between devices, swap(): return lax.ppermute(x, AXES, route)  24.5 us
    pallas_call x7, Pallas kernels, call(): pl.pallas_call(kernel, out_shape=[jax.ShapeDtypeStruct(*o) for o in outs]...  21.5 us
    ppermute x6, waiting for transfers between devices, swap(): return lax.ppermute(x, AXES, route)  9.31 us
  transfers between devices with their start and end apart: 6, of which 2 were waited for; matrix products, arithmetic and copies ran while one was open for 0% of the time, Pallas kernels for 25%

profile of v1, /device:TPU:6, one launch (start us, length us, event | category | flops | bytes accessed | tf_op | source)
XLA Modules:
  0.0 56.1 jit_solution(12411561650844974211)
XLA Ops:
  0.0 1.0 %shard_map.73.pay = bf16[1568,128]{1,0:T(8,128)(2,1)S(1)} custom-call(s32[12]{0:T(128)} %agg_hbm.3, s32[1,2,3]{2,1,0:T(2,128)} %ghost.1, bf16[1536,128]{1,0:T(8,128)(2,1)} %bitcast.4), custom_call_target="tpu_custom_call" | custom-call | flops 1 | bytes 393288 | tf_op jit(solution)/shard_map/pallas_call | solution.py:25
  1.0 0.0 copy-start
  1.0 9.9 %collective-permute-start.1 = (bf16[1568,128]{1,0:T(8,128)(2,1)S(1)}, bf16[1568,128]{1,0:T(8,128)(2,1)S(1)}, u32[]{:S(2)}, u32[]{:S(2)}) collective-permute-start(bf16[1568,128]{1,0:T(8,128)(2,1)S(1)} %shard_map.73.pay), channel_id=1, source_target_pairs={{1,2},{2,1},{3,4},{4,3},{5,6},{6,5},{7,8},{8,7},{9,10},{10,9},{11,... | collective-permute-start | bytes 1204232 | tf_op jit(solution)/shard_map/ppermute | solution.py:229
  11.0 0.1 collective-permute-start
  11.7 4.6 %shard_map.74 = (bf16[1536,2304]{1,0:T(8,128)(2,1)S(1)}, bf16[1536,128]{1,0:T(8,128)(2,1)S(1)}, bf16[1536,256]{1,0:T(8,128)(2,1)S(1)}) custom-call(s32[12,9]{1,0:T(8,128)} %cols_hbm.1, s32[12]{0:T(128)} %agg_hbm.3, s32[1]{0:T(128)} %bitcast.par, f32[1]{0:T(128)S(6)} %copy.8.damp, bf16[12,9,128,128]{3,2,1,0:T(8,128)(2,1)} %vals_hbm.1, ...), custom_call_target="tpu_custom_call" | custom-call | flops 1207959552 | bytes 4334056 | tf_op jit(solution)/shard_map/pallas_call | solution.py:25
  16.3 0.2 collective-permute-done.1.pay_x
  16.5 0.0 collective-permute-done.pay_s
  16.5 0.0 copy-done
  16.5 4.3 %shard_map.75 = (bf16[1536,256]{1,0:T(8,128)(2,1)S(1)}, bf16[1536,256]{1,0:T(8,128)(2,1)S(1)}, bf16[384,768]{1,0:T(8,128)(2,1)S(1)}, bf16[384,768]{1,0:T(8,128)(2,1)S(1)}) custom-call(s32[1,2,3]{2,1,0:T(2,128)S(1)} %copy-done, s32[1]{0:T(128)} %bitcast.par, f32[1]{0:T(128)S(6)} %copy.8.damp, bf16[1536,2304]{1,0:T(8,128)(2,1)S(1)} %get-tuple-element.16.dense, ...), custom_call_target="tpu_custom_call" | custom-call | flops 603979776 | bytes 9060384 | tf_op jit(solution)/shard_map/pallas_call | solution.py:25
  20.8 0.4 collective-permute-start.2
  21.3 7.5 %collective-permute-start.3 = (bf16[384,768]{1,0:T(8,128)(2,1)S(1)}, bf16[384,768]{1,0:T(8,128)(2,1)S(1)}, u32[]{:S(2)}, u32[]{:S(2)}) collective-permute-start(bf16[384,768]{1,0:T(8,128)(2,1)S(1)} %get-tuple-element.24), channel_id=1, source_target_pairs={{1,2},{2,1},{3,4},{4,3},{5,6},{6,5},{7,8},{8,7},{9,10},{10,9},{11,... | collective-permute-start | bytes 1769480 | tf_op jit(solution)/shard_map/ppermute | solution.py:229
  28.8 9.0 %shard_map.76 = (f32[768,768]{1,0:T(8,128)S(1)}, bf16[768,768]{1,0:T(8,128)(2,1)S(1)}) custom-call(bf16[1536,2304]{1,0:T(8,128)(2,1)S(1)} %get-tuple-element.16.dense, bf16[1536,256]{1,0:T(8,128)(2,1)S(1)} %get-tuple-element.19.p_s, bf16[1536,256]{1,0:T(8,128)(2,1)S(1)} %get-tuple-element.18.p_own, bf16[1536,256]{1,0:T(8,128)(2,1)S(1)} %get-tuple-element.20.p_x), custom_call_target="tpu_custom_call" | custom-call | flops 3623878656 | bytes 9437184 | tf_op jit(solution)/shard_map/pallas_call | solution.py:25
  37.8 0.0 collective-permute-done.2.far_s
  37.8 0.0 collective-permute-done.3.far_x
  37.8 1.0 %shard_map.78 = (bf16[256,1280]{1,0:T(8,128)(2,1)S(1)}, bf16[256,1280]{1,0:T(8,128)(2,1)S(1)}) custom-call(f32[768,768]{1,0:T(8,128)S(1)} %get-tuple-element.21.gal, bf16[768,768]{1,0:T(8,128)(2,1)S(1)} %get-tuple-element.22.wide, bf16[384,768]{1,0:T(8,128)(2,1)S(1)} %collective-permute-done.2.far_s, bf16[384,768]{1,0:T(8,128)(2,1)S(1)} %collective-permute-done.3.far_x), custom_call_target="tpu_custom_call" | custom-call | flops 603979776 | bytes 4718592 | tf_op jit(solution)/shard_map/pallas_call | solution.py:25
  38.8 0.1 collective-permute-start.4
  38.9 6.4 %collective-permute-start.5 = (bf16[256,1280]{1,0:T(8,128)(2,1)S(1)}, bf16[256,1280]{1,0:T(8,128)(2,1)S(1)}, u32[]{:S(2)}, u32[]{:S(2)}) collective-permute-start(bf16[256,1280]{1,0:T(8,128)(2,1)S(1)} %get-tuple-element.26), channel_id=1, source_target_pairs={{1,2},{2,1},{3,4},{4,3},{5,6},{6,5},{7,8},{8,7},{9,10},{10,9},{11,... | collective-permute-start | bytes 1966088 | tf_op jit(solution)/shard_map/ppermute | solution.py:229
  45.3 0.6 %shard_map.77.mine = f32[256,1280]{1,0:T(8,128)S(1)} custom-call(f32[768,768]{1,0:T(8,128)S(1)} %get-tuple-element.21.gal, bf16[768,768]{1,0:T(8,128)(2,1)S(1)} %get-tuple-element.22.wide, bf16[384,768]{1,0:T(8,128)(2,1)S(1)} %collective-permute-done.2.far_s, bf16[384,768]{1,0:T(8,128)(2,1)S(1)} %collective-permute-done.3.far_x), custom_call_target="tpu_custom_call" | custom-call | flops 301989888 | bytes 4718592 | tf_op jit(solution)/shard_map/pallas_call | solution.py:25
  45.9 0.0 collective-permute-done.4.from_s
  45.9 9.1 %collective-permute-done.5.from_x = bf16[256,1280]{1,0:T(8,128)(2,1)S(1)} collective-permute-done((bf16[256,1280]{1,0:T(8,128)(2,1)S(1)}, bf16[256,1280]{1,0:T(8,128)(2,1)S(1)}, u32[]{:S(2)}, u32[]{:S(2)}) %collective-permute-start.5) | collective-permute-done | bytes 655392 | tf_op jit(solution)/shard_map/ppermute | solution.py:229
  55.0 1.1 %shard_map.79 = bf16[256,1792]{1,0:T(8,128)(2,1)} custom-call(s32[1]{0:T(128)} %bitcast.par, f32[256,1280]{1,0:T(8,128)S(1)} %shard_map.77.mine, bf16[256,1280]{1,0:T(8,128)(2,1)S(1)} %collective-permute-done.4.from_s, bf16[256,1280]{1,0:T(8,128)(2,1)S(1)} %collective-permute-done.5.from_x), custom_call_target="tpu_custom_call" | custom-call | flops 458752 | bytes 2621444 | tf_op jit(solution)/shard_map/pallas_call | solution.py:25
Async XLA Ops:
  1.0 15.5 %copy-start = (s32[1,2,3]{2,1,0:T(2,128)S(1)}, s32[1,2,3]{2,1,0:T(2,128)}, u32[]{:S(2)}) copy-start(s32[1,2,3]{2,1,0:T(2,128)} %ghost.1) | copy-start | bytes 76
  1.0 15.5 %collective-permute-start.1 = (bf16[1568,128]{1,0:T(8,128)(2,1)S(1)}, bf16[1568,128]{1,0:T(8,128)(2,1)S(1)}, u32[]{:S(2)}, u32[]{:S(2)}) collective-permute-start(bf16[1568,128]{1,0:T(8,128)(2,1)S(1)} %shard_map.73.pay), channel_id=1, source_target_pairs={{1,2},{2,1},{3,4},{4,3},{5,6},{6,5},{7,8},{8,7},{9,10},{10,9},{11,... | collective-permute-start | bytes 1204232 | tf_op jit(solution)/shard_map/ppermute | solution.py:229
  11.0 5.5 %collective-permute-start = (bf16[1568,128]{1,0:T(8,128)(2,1)S(1)}, bf16[1568,128]{1,0:T(8,128)(2,1)S(1)}, u32[]{:S(2)}, u32[]{:S(2)}) collective-permute-start(bf16[1568,128]{1,0:T(8,128)(2,1)S(1)} %shard_map.73.pay), channel_id=1, source_target_pairs={{0,1},{1,0},{2,3},{3,2},{4,5},{5,4},{6,7},{7,6},{8,9},{9,8},{10,11... | collective-permute-start | bytes 1204232 | tf_op jit(solution)/shard_map/ppermute | solution.py:229
  20.8 17.0 %collective-permute-start.2 = (bf16[384,768]{1,0:T(8,128)(2,1)S(1)}, bf16[384,768]{1,0:T(8,128)(2,1)S(1)}, u32[]{:S(2)}, u32[]{:S(2)}) collective-permute-start(bf16[384,768]{1,0:T(8,128)(2,1)S(1)} %get-tuple-element.23), channel_id=1, source_target_pairs={{0,1},{1,0},{2,3},{3,2},{4,5},{5,4},{6,7},{7,6},{8,9},{9,8},{10,11... | collective-permute-start | bytes 1769480 | tf_op jit(solution)/shard_map/ppermute | solution.py:229
  21.3 16.5 %collective-permute-start.3 = (bf16[384,768]{1,0:T(8,128)(2,1)S(1)}, bf16[384,768]{1,0:T(8,128)(2,1)S(1)}, u32[]{:S(2)}, u32[]{:S(2)}) collective-permute-start(bf16[384,768]{1,0:T(8,128)(2,1)S(1)} %get-tuple-element.24), channel_id=1, source_target_pairs={{1,2},{2,1},{3,4},{4,3},{5,6},{6,5},{7,8},{8,7},{9,10},{10,9},{11,... | collective-permute-start | bytes 1769480 | tf_op jit(solution)/shard_map/ppermute | solution.py:229
  38.8 7.1 %collective-permute-start.4 = (bf16[256,1280]{1,0:T(8,128)(2,1)S(1)}, bf16[256,1280]{1,0:T(8,128)(2,1)S(1)}, u32[]{:S(2)}, u32[]{:S(2)}) collective-permute-start(bf16[256,1280]{1,0:T(8,128)(2,1)S(1)} %get-tuple-element.25), channel_id=1, source_target_pairs={{0,1},{1,0},{2,3},{3,2},{4,5},{5,4},{6,7},{7,6},{8,9},{9,8},{10,11... | collective-permute-start | bytes 1966088 | tf_op jit(solution)/shard_map/ppermute | solution.py:229
  38.9 16.1 %collective-permute-start.5 = (bf16[256,1280]{1,0:T(8,128)(2,1)S(1)}, bf16[256,1280]{1,0:T(8,128)(2,1)S(1)}, u32[]{:S(2)}, u32[]{:S(2)}) collective-permute-start(bf16[256,1280]{1,0:T(8,128)(2,1)S(1)} %get-tuple-element.26), channel_id=1, source_target_pairs={{1,2},{2,1},{3,4},{4,3},{5,6},{6,5},{7,8},{8,7},{9,10},{10,9},{11,... | collective-permute-start | bytes 1966088 | tf_op jit(solution)/shard_map/ppermute | solution.py:229

commit v2 on v1

v2 whole, which is shorter than its diff:
```python
import functools

import jax
import jax.numpy as jnp
from jax import lax
from jax.experimental import pallas as pl
from jax.experimental.pallas import tpu as pltpu
from jax.sharding import PartitionSpec as P

CA = 2
META = 32
AXES = ("grp", "dev")
VMEM = pltpu.VMEM
SMEM = pltpu.SMEM
F32 = jnp.float32
BF16 = jnp.bfloat16


SPACES = {"v": VMEM, "s": SMEM, "h": pltpu.HBM}


def call(kernel, args, spaces, outs, scratch=(), flops=1, limit=None):
    nbytes = sum(a.size * a.dtype.itemsize for a in args)
    in_specs = [pl.BlockSpec(memory_space=SPACES[c]) for c in spaces]
    return pl.pallas_call(
        kernel,
        out_shape=[jax.ShapeDtypeStruct(*o) for o in outs],
        in_specs=in_specs,
        out_specs=[pl.BlockSpec(memory_space=VMEM) for _ in outs],
        scratch_shapes=list(scratch),
        cost_estimate=pl.CostEstimate(flops=flops, bytes_accessed=nbytes, transcendentals=0),
        compiler_params=pltpu.CompilerParams(vmem_limit_bytes=limit),
    )(*[pltpu.with_memory_space_constraint(a, pltpu.HBM) if c == "h" else a for a, c in zip(args, spaces)])


def rows(index, size):
    return pl.ds(pl.multiple_of(index * size, size), size)


def dot(a, b):
    return jnp.dot(a, b, preferred_element_type=F32)


def pack_kernel(r, b, s, agg_hbm, ghost_hbm, tent_hbm, out, agg, ghost, sems):
    copies = [
        pltpu.make_async_copy(agg_hbm, agg, sems.at[0]),
        pltpu.make_async_copy(ghost_hbm, ghost, sems.at[1]),
        pltpu.make_async_copy(tent_hbm, out.at[: r * b, :], sems.at[2]),
    ]
    for copy in copies:
        copy.start()
    copies[0].wait()
    copies[1].wait()
    sub = lax.broadcasted_iota(jnp.int32, (META, b), 0)
    meta = jnp.zeros((META, b), F32)
    for j in range(r):
        meta = jnp.where(sub == j, agg[j].astype(F32), meta)
    for side in range(2):
        for j in range(s):
            meta = jnp.where(sub == 16 + 8 * side + j, ghost[0, side, j].astype(F32), meta)
    out[r * b :, :] = meta.astype(BF16)
    copies[2].wait()


def smooth(r, b, dense, cols, placed, inv, damp, target, base=None):
    step = 4
    for t in range(r // step):
        half = dot(dense[t * step * b : (t + 1) * step * b, cols], placed).astype(BF16)
        for q in range(step):
            at = slice((t * step + q) * b, (t * step + q + 1) * b)
            value = -damp[0] * dot(inv[at, :], half[q * b : (q + 1) * b, :])
            if base is not None:
                value = base[at, :].astype(F32) + value
            target[at, :] = value.astype(BF16)


def place_ghosts(r, b, s, ghost, mine, pay, meta, placed):
    meta[...] = pay[r * b :, :].astype(F32)
    for j in range(s):
        row = jnp.clip(ghost[0, mine, j], 0, r - 1)
        block = pay[rows(row, b), :]
        here = jnp.broadcast_to(meta[pl.ds(row, 1), :], (b, b))
        for c in range(CA):
            placed[j * b : (j + 1) * b, c * b : (c + 1) * b] = jnp.where(here == c, block.astype(F32), 0.0).astype(BF16)


def wanted_rows(r, s, theirs, meta):
    found = []
    for j in range(s):
        value = jnp.max(meta[pl.ds(16 + 8 * theirs + j, 1), :])
        found.append(jnp.clip(value.astype(jnp.int32), 0, r - 1))
    return found


def own_kernel(
    r, k, b, s, cols_hbm, agg_hbm, par, damp, vals_hbm, inv_hbm, pay, dense, inv, p_own, cols, agg, vals, placed, sems
):
    def fetch(j):
        return pltpu.make_async_copy(vals_hbm.at[j], vals.at[j], sems.at[j])

    others = [
        pltpu.make_async_copy(cols_hbm, cols, sems.at[r]),
        pltpu.make_async_copy(agg_hbm, agg, sems.at[r + 1]),
        pltpu.make_async_copy(inv_hbm, inv, sems.at[r + 2]),
    ]
    others[0].start()
    others[1].start()
    for j in range(r):
        fetch(j).start()
    others[2].start()

    def clear(j, carry):
        dense[rows(j, b), :] = jnp.zeros((b, (r + 2 * s) * b), BF16)
        return carry

    lax.fori_loop(0, r, clear, 0)
    others[0].wait()
    others[1].wait()
    zero = jnp.zeros((b, b), BF16)
    for j in range(r):
        own = slice(j * b, (j + 1) * b)
        block = pay[own, :]
        here = agg[j]
        for c in range(CA):
            placed[own, c * b : (c + 1) * b] = jnp.where(here == c, block, zero)
    odd = par[0]
    left = s * (1 - odd)

    def row(j, carry):
        fetch(j).wait()
        at = rows(j, b)
        for e in range(k):
            c = cols[j, e]
            c = jnp.where(c < r, c, jnp.where(c < r + s, c + left, c - left))
            dense[at, rows(c, b)] = vals[j, e]
        return carry

    lax.fori_loop(0, r, row, 0)
    others[2].wait()
    smooth(r, b, dense, slice(0, r * b), placed[...], inv, damp, p_own, placed)


def near_kernel(r, b, s, ghost, par, damp, dense, inv, p_own, pay, p_s, applied, meta, placed):
    place_ghosts(r, b, s, ghost, 1 - par[0], pay, meta, placed)
    smooth(r, b, dense, slice(r * b, (r + s) * b), placed[...], inv, damp, p_s)
    w = CA * b
    step = 4
    for t in range(r // step):
        at = slice(t * step * b, (t + 1) * step * b)
        block = dense[at, : r * b]
        applied[at, :w] = dot(block, p_s[...]).astype(BF16)
        applied[at, w:] = dot(block, p_own[...]).astype(BF16)


def far_kernel(r, b, s, ghost, par, damp, dense, inv, p_s, p_own, pay_s, pay_x, p_x, out_x, out_s, meta, near, placed):
    odd = par[0]
    place_ghosts(r, b, s, ghost, odd, pay_x, meta, placed)
    near[...] = pay_s[r * b :, :].astype(F32)
    wanted = (wanted_rows(r, s, 1 - odd, meta), wanted_rows(r, s, odd, near))
    smooth(r, b, dense, slice((r + s) * b, (r + 2 * s) * b), placed[...], inv, damp, p_x)
    w = CA * b
    for found, out in zip(wanted, (out_x, out_s)):
        for j in range(s):
            at = rows(found[j], b)
            to = slice(j * b, (j + 1) * b)
            out[to, :w] = p_s[at, :]
            out[to, w : 2 * w] = p_own[at, :]
            out[to, 2 * w :] = p_x[at, :]


def flip(r, b, p, flipped, d, w):
    for j in range(r):
        at = slice(j * b, (j + 1) * b)
        flipped[d * w : (d + 1) * w, at] = p[at, :].T


def cross_kernel(r, b, w, dense, p_x, applied, gal, wide, applied_x, flipped):
    flip(r, b, p_x, flipped, 0, w)
    step = 4
    for t in range(r // step):
        at = slice(t * step * b, (t + 1) * step * b)
        applied_x[at, :] = dot(dense[at, : r * b], p_x[...]).astype(BF16)
    left = flipped[...]
    wide[...] = dot(left, dense[:, r * b :]).astype(BF16)
    gal[:, : 2 * w] = dot(left, applied[...])
    gal[:, 2 * w :] = dot(left, applied_x[...])


def outer_kernel(w, span, gal, wide, far_s, out):
    by_s = dot(wide[:, :span], far_s[...])
    out[:, :w] = by_s[:, 2 * w :].astype(BF16)
    out[:, w : 2 * w] = (gal[:, :w] + by_s[:, w : 2 * w]).astype(BF16)
    out[:, 2 * w : 3 * w] = (gal[:, w : 2 * w] + by_s[:, :w]).astype(BF16)
    out[:, 3 * w : 4 * w] = gal[:, 2 * w :].astype(BF16)
    out[:, 4 * w :] = wide[:, span:]


def rest_kernel(r, b, w, dense, p_s, p_own, applied, applied_x, gal, wide, flipped):
    for d, p in enumerate((p_s, p_own)):
        flip(r, b, p, flipped, d, w)
    for d in range(2):
        at = slice(d * w, (d + 1) * w)
        left = flipped[at, :]
        wide[at, :] = dot(left, dense[:, r * b :]).astype(BF16)
        gal[at, : 2 * w] = dot(left, applied[...])
        gal[at, 2 * w :] = dot(left, applied_x[...])


def galerkin_rows(index, w, span, gal, wide, far_s, far_x):
    at = slice(index * w, (index + 1) * w)
    by_s = dot(wide[at, :span], far_s[...])
    by_x = dot(wide[at, span:], far_x[...])
    return (
        by_s[:, 2 * w :],
        gal[at, :w] + by_s[:, w : 2 * w],
        gal[at, w : 2 * w] + by_s[:, :w] + by_x[:, 2 * w :],
        gal[at, 2 * w :] + by_x[:, w : 2 * w],
        by_x[:, :w],
    )


def chip_kernel(w, span, gal, wide, far_s, far_x, out):
    for c, value in enumerate(galerkin_rows(0, w, span, gal, wide, far_s, far_x)):
        out[:, c * w : (c + 1) * w] = value.astype(BF16)


def inner_kernel(w, span, gal, wide, far_s, far_x, from_s, out):
    mine = galerkin_rows(1, w, span, gal, wide, far_s, far_x)
    for u in range(-3, 4):
        total = mine[2 - u] if abs(u) < 3 else jnp.zeros((w, w), F32)
        if 0 <= 1 + u < 5:
            total = total + from_s[:, (1 + u) * w : (2 + u) * w].astype(F32)
        out[:, (3 - u) * w : (4 - u) * w] = total


def final_kernel(w, par, mine, sent_x, from_x, out):
    sign = 1 - 2 * par[0]
    back = dot(from_x[:, 4 * w :], sent_x[...])
    for u in range(-3, 4):
        total = mine[:, (3 - u) * w : (4 - u) * w]
        if 0 <= 3 + u < 4:
            total = total + from_x[:, (3 + u) * w : (4 + u) * w].astype(F32)
        if abs(u) < 2:
            total = total + back[:, (1 - u) * w : (2 - u) * w]
        out[:, rows(3 + sign * u, w)] = total.astype(BF16)


def swap(x, route):
    return lax.ppermute(x, AXES, route)


def shards(block_values, block_columns, tentative, inverse_diagonal, aggregate, ghost_rows, damping):
    r, k = block_columns.shape
    b = tentative.shape[1]
    s = ghost_rows.shape[2]
    w = CA * b
    span = s * b
    devices = lax.axis_size(AXES)
    chip = [(i, i ^ 1) for i in range(devices) if i ^ 1 < devices]
    cross = []
    for i in range(1, devices - 1, 2):
        cross += [(i, i + 1), (i + 1, i)]
    par = (lax.axis_index(AXES) % 2).astype(jnp.int32).reshape(1)
    tent = tentative.reshape(r * b, b)
    inv = inverse_diagonal.reshape(r * b, b)
    dma = pltpu.SemaphoreType.DMA

    (pay,) = call(
        functools.partial(pack_kernel, r, b, s), (aggregate, ghost_rows, tent), "hhh",
        [((r * b + META, b), BF16)],
        scratch=[SMEM((r,), jnp.int32), SMEM((1, 2, s), jnp.int32), dma((3,))], limit=2 << 20,
    )
    pay_x = swap(pay, cross)
    pay_s = swap(pay, chip)
    dense, inv, p_own = call(
        functools.partial(own_kernel, r, k, b, s),
        (block_columns, aggregate, par, damping, block_values, inv, pay), "hhsshhv",
        [((r * b, (r + 2 * s) * b), BF16), ((r * b, b), BF16), ((r * b, w), BF16)],
        scratch=[
            SMEM((r, k), jnp.int32), SMEM((r,), jnp.int32), VMEM((r, k, b, b), BF16), VMEM((r * b, w), BF16),
            dma((r + 3,)),
        ],
        flops=2 * r * b * r * b * w, limit=24 << 20,
    )
    p_s, applied = call(
        functools.partial(near_kernel, r, b, s), (ghost_rows, par, damping, dense, inv, p_own, pay_s), "sssvvvv",
        [((r * b, w), BF16), ((r * b, 2 * w), BF16)],
        scratch=[VMEM((META, b), F32), VMEM((span, w), BF16)],
        flops=4 * r * b * r * b * w, limit=24 << 20,
    )
    p_x, out_x, out_s = call(
        functools.partial(far_kernel, r, b, s),
        (ghost_rows, par, damping, dense, inv, p_s, p_own, pay_s, pay_x), "sssvvvvvv",
        [((r * b, w), BF16), ((span, 3 * w), BF16), ((span, 3 * w), BF16)],
        scratch=[VMEM((META, b), F32), VMEM((META, b), F32), VMEM((span, w), BF16)],
        flops=2 * r * b * span * w, limit=24 << 20,
    )
    far_x = swap(out_x, cross)
    far_s = swap(out_s, chip)
    gal_x, wide_x, applied_x = call(
        functools.partial(cross_kernel, r, b, w), (dense, p_x, applied), "vvv",
        [((w, 3 * w), F32), ((w, 2 * span), BF16), ((r * b, w), BF16)],
        scratch=[VMEM((w, r * b), BF16)],
        flops=2 * r * b * r * b * 2 * w, limit=24 << 20,
    )
    (sum_x,) = call(
        functools.partial(outer_kernel, w, span), (gal_x, wide_x, far_s), "vvv",
        [((w, 4 * w + span), BF16)], flops=2 * w * span * 3 * w, limit=16 << 20,
    )
    from_x = swap(sum_x, cross)
    gal, wide = call(
        functools.partial(rest_kernel, r, b, w), (dense, p_s, p_own, applied, applied_x), "vvvvv",
        [((2 * w, 3 * w), F32), ((2 * w, 2 * span), BF16)],
        scratch=[VMEM((2 * w, r * b), BF16)],
        flops=2 * r * b * r * b * 2 * w, limit=24 << 20,
    )
    (sum_s,) = call(
        functools.partial(chip_kernel, w, span), (gal, wide, far_s, far_x), "vvvv",
        [((w, 5 * w), BF16)], flops=4 * w * span * 3 * w, limit=16 << 20,
    )
    from_s = swap(sum_s, chip)
    (mine,) = call(
        functools.partial(inner_kernel, w, span), (gal, wide, far_s, far_x, from_s), "vvvvv",
        [((w, 7 * w), F32)], flops=4 * w * span * 3 * w, limit=16 << 20,
    )
    (out,) = call(
        functools.partial(final_kernel, w), (par, mine, out_x, from_x), "svvv",
        [((w, 7 * w), BF16)], flops=2 * w * span * 3 * w, limit=16 << 20,
    )
    return out.reshape(CA, b, 7 * w)


def solution(mesh):
    return jax.shard_map(
        shards,
        mesh=mesh,
        in_specs=(
            P(AXES, None, None, None),
            P(AXES, None),
            P(AXES, None, None),
            P(AXES, None, None),
            P(AXES),
            P(AXES, None, None),
            P(),
        ),
        out_specs=P(AXES, None, None),
        check_vma=False,
    )
```

time: 56.3 us -> 48.4 us (0.86)
  starting transfers between devices: 24.5 us -> 20.6 us
  waiting for transfers between devices: 9.31 us -> 6.81 us
  Pallas kernels: 21.5 us -> 20 us
    ppermute x6, starting transfers between devices: 24.5 us -> 20.6 us  [swap(): return lax.ppermute(x, AXES, route)]
    ppermute x6, waiting for transfers between devices: 9.31 us -> 6.81 us  [swap(): return lax.ppermute(x, AXES, route)]
    pallas_call x7 -> x10, Pallas kernels: 21.5 us -> 20 us  [call(): pl.pallas_call(kernel, out_shape=[jax.ShapeDtypeStruct(*o) for o in outs]...]
  transfers between devices with their start and end apart: 6 -> 6, of which waited for: 2 -> 2; matrix products, arithmetic and copies ran while one was open for 0% -> 0% of each run, Pallas kernels for 25% -> 33%
where the time goes in v2:
time: 48.4 us; the launch traced here: 48.2 us
  starting transfers between devices  20.6 us (43%)
  Pallas kernels  20 us (41%)
  waiting for transfers between devices  6.81 us (14%)
  between operations  0.82 us (2%)
    ppermute x6, starting transfers between devices, swap(): return lax.ppermute(x, AXES, route)  20.6 us
    pallas_call x10, Pallas kernels, call(): pl.pallas_call(kernel, out_shape=[jax.ShapeDtypeStruct(*o) for o in outs]...  20 us
    ppermute x6, waiting for transfers between devices, swap(): return lax.ppermute(x, AXES, route)  6.81 us
  transfers between devices with their start and end apart: 6, of which 2 were waited for; matrix products, arithmetic and copies ran while one was open for 0% of the time, Pallas kernels for 33%

profile of v2, /device:TPU:6, one launch (start us, length us, event | category | flops | bytes accessed | tf_op | source)
XLA Modules:
  0.0 48.2 jit_solution(2129961427654393630)
XLA Ops:
  0.0 1.0 %shard_map.73.pay = bf16[1568,128]{1,0:T(8,128)(2,1)S(1)} custom-call(s32[12]{0:T(128)} %agg_hbm.3, s32[1,2,3]{2,1,0:T(2,128)} %ghost.3, bf16[1536,128]{1,0:T(8,128)(2,1)} %bitcast.4), custom_call_target="tpu_custom_call" | custom-call | flops 1 | bytes 393288 | tf_op jit(solution)/shard_map/pallas_call | solution.py:25
  1.0 0.1 collective-permute-start
  1.1 10.6 %collective-permute-start.1 = (bf16[1568,128]{1,0:T(8,128)(2,1)S(1)}, bf16[1568,128]{1,0:T(8,128)(2,1)S(1)}, u32[]{:S(2)}, u32[]{:S(2)}) collective-permute-start(bf16[1568,128]{1,0:T(8,128)(2,1)S(1)} %shard_map.73.pay), channel_id=1, source_target_pairs={{1,2},{2,1},{3,4},{4,3},{5,6},{6,5},{7,8},{8,7},{9,10},{10,9},{11,... | collective-permute-start | bytes 1204232 | tf_op jit(solution)/shard_map/ppermute | solution.py:249
  12.4 0.0 copy-start
  12.4 4.8 %shard_map.74 = (bf16[1536,2304]{1,0:T(8,128)(2,1)S(1)}, bf16[1536,128]{1,0:T(8,128)(2,1)S(1)}, bf16[1536,256]{1,0:T(8,128)(2,1)S(1)}) custom-call(s32[12,9]{1,0:T(8,128)} %cols_hbm.1, s32[12]{0:T(128)} %agg_hbm.3, s32[1]{0:T(128)} %bitcast.par, f32[1]{0:T(128)S(6)} %copy.8.damp, bf16[12,9,128,128]{3,2,1,0:T(8,128)(2,1)} %vals_hbm.1, ...), custom_call_target="tpu_custom_call" | custom-call | flops 1207959552 | bytes 4334056 | tf_op jit(solution)/shard_map/pallas_call | solution.py:25
  17.2 0.0 collective-permute-done.pay.pay_s
  17.2 0.0 copy-done
  17.2 4.2 %shard_map.75 = (bf16[1536,256]{1,0:T(8,128)(2,1)S(1)}, bf16[1536,512]{1,0:T(8,128)(2,1)S(1)}) custom-call(s32[1,2,3]{2,1,0:T(2,128)S(1)} %copy-done, s32[1]{0:T(128)} %bitcast.par, f32[1]{0:T(128)S(6)} %copy.8.damp, bf16[1536,2304]{1,0:T(8,128)(2,1)S(1)} %get-tuple-element.18.dense, bf16[1536,128]{1,0:T(8,128)(2,1)S(1)} %get-tuple-element.19.inv, ...), custom_call_target="tpu_custom_call" | custom-call | flops 2415919104 | bytes 8658976 | tf_op jit(solution)/shard_map/pallas_call | solution.py:25
  21.4 0.0 collective-permute-done.1.pay_x
  21.4 1.8 %shard_map.76 = (bf16[1536,256]{1,0:T(8,128)(2,1)S(1)}, bf16[384,768]{1,0:T(8,128)(2,1)S(1)}, bf16[384,768]{1,0:T(8,128)(2,1)S(1)}) custom-call(s32[1,2,3]{2,1,0:T(2,128)S(1)} %copy-done, s32[1]{0:T(128)} %bitcast.par, f32[1]{0:T(128)S(6)} %copy.8.damp, bf16[1536,2304]{1,0:T(8,128)(2,1)S(1)} %get-tuple-element.18.dense, ...), custom_call_target="tpu_custom_call" | custom-call | flops 301989888 | bytes 9846816 | tf_op jit(solution)/shard_map/pallas_call | solution.py:25
  23.2 0.1 collective-permute-start.2
  23.3 3.7 %collective-permute-start.3 = (bf16[384,768]{1,0:T(8,128)(2,1)S(1)}, bf16[384,768]{1,0:T(8,128)(2,1)S(1)}, u32[]{:S(2)}, u32[]{:S(2)}) collective-permute-start(bf16[384,768]{1,0:T(8,128)(2,1)S(1)} %get-tuple-element.28.sent_x), channel_id=1, source_target_pairs={{1,2},{2,1},{3,4},{4,3},{5,6},{6,5},{7,8},{8,7},{9,10},{10,9},{11,... | collective-permute-start | bytes 1769480 | tf_op jit(solution)/shard_map/ppermute | solution.py:249
  27.0 2.6 %shard_map.77 = (f32[256,768]{1,0:T(8,128)S(1)}, bf16[256,768]{1,0:T(8,128)(2,1)S(1)}, bf16[1536,256]{1,0:T(8,128)(2,1)S(1)}) custom-call(bf16[1536,2304]{1,0:T(8,128)(2,1)S(1)} %get-tuple-element.18.dense, bf16[1536,256]{1,0:T(8,128)(2,1)S(1)} %get-tuple-element.23.p_x, bf16[1536,512]{1,0:T(8,128)(2,1)S(1)} %get-tuple-element.22.applied), custom_call_target="tpu_custom_call" | custom-call | flops 2415919104 | bytes 9437184 | tf_op jit(solution)/shard_map/pallas_call | solution.py:25
  29.6 0.0 collective-permute-done.2.far_s
  29.7 0.4 shard_map.81
  30.0 6.1 %collective-permute-start.5 = (bf16[256,1408]{1,0:T(8,128)(2,1)S(1)}, bf16[256,1408]{1,0:T(8,128)(2,1)S(1)}, u32[]{:S(2)}, u32[]{:S(2)}) collective-permute-start(bf16[256,1408]{1,0:T(8,128)(2,1)S(1)} %shard_map.81), channel_id=1, source_target_pairs={{1,2},{2,1},{3,4},{4,3},{5,6},{6,5},{7,8},{8,7},{9,10},{10,9},{11,... | collective-permute-start | bytes 2162696 | tf_op jit(solution)/shard_map/ppermute | solution.py:249
  36.2 2.6 %shard_map.78 = (f32[512,768]{1,0:T(8,128)S(1)}, bf16[512,768]{1,0:T(8,128)(2,1)S(1)}) custom-call(bf16[1536,2304]{1,0:T(8,128)(2,1)S(1)} %get-tuple-element.18.dense, bf16[1536,256]{1,0:T(8,128)(2,1)S(1)} %get-tuple-element.21.p_s, bf16[1536,256]{1,0:T(8,128)(2,1)S(1)} %get-tuple-element.20.p_own, bf16[1536,512]{1,0:T(8,128)(2,1)S(1)} %get-tuple-element.22.applied, ...), custom_call_target="tpu_custom_call" | custom-call | flops 2415919104 | bytes 11010048 | tf_op jit(solution)/shard_map/pallas_call | solution.py:25
  38.8 0.0 collective-permute-done.3.far_x
  38.8 0.6 %shard_map.79 = bf16[256,1280]{1,0:T(8,128)(2,1)S(1)} custom-call(f32[512,768]{1,0:T(8,128)S(1)} %get-tuple-element.25.gal, bf16[512,768]{1,0:T(8,128)(2,1)S(1)} %get-tuple-element.26.wide, bf16[384,768]{1,0:T(8,128)(2,1)S(1)} %collective-permute-done.2.far_s, bf16[384,768]{1,0:T(8,128)(2,1)S(1)} %collective-permute-done.3.far_x), custom_call_target="tpu_custom_call" | custom-call | flops 301989888 | bytes 3538944 | tf_op jit(solution)/shard_map/pallas_call | solution.py:25
  39.4 0.1 collective-permute-start.4
  39.5 2.1 %collective-permute-done.4.from_s = bf16[256,1280]{1,0:T(8,128)(2,1)S(1)} collective-permute-done((bf16[256,1280]{1,0:T(8,128)(2,1)S(1)}, bf16[256,1280]{1,0:T(8,128)(2,1)S(1)}, u32[]{:S(2)}, u32[]{:S(2)}) %collective-permute-start.4) | collective-permute-done | bytes 655392 | tf_op jit(solution)/shard_map/ppermute | solution.py:249
  41.6 0.6 %shard_map.80.mine = f32[256,1792]{1,0:T(8,128)S(1)} custom-call(f32[512,768]{1,0:T(8,128)S(1)} %get-tuple-element.25.gal, bf16[512,768]{1,0:T(8,128)(2,1)S(1)} %get-tuple-element.26.wide, bf16[384,768]{1,0:T(8,128)(2,1)S(1)} %collective-permute-done.2.far_s, bf16[384,768]{1,0:T(8,128)(2,1)S(1)} %collective-permute-done.3.far_x, ...), custom_call_target="tpu_custom_call" | custom-call | flops 301989888 | bytes 4194304 | tf_op jit(solution)/shard_map/pallas_call | solution.py:25
  42.1 4.7 %collective-permute-done.5.from_x = bf16[256,1408]{1,0:T(8,128)(2,1)S(1)} collective-permute-done((bf16[256,1408]{1,0:T(8,128)(2,1)S(1)}, bf16[256,1408]{1,0:T(8,128)(2,1)S(1)}, u32[]{:S(2)}, u32[]{:S(2)}) %collective-permute-start.5) | collective-permute-done | bytes 720928 | tf_op jit(solution)/shard_map/ppermute | solution.py:249
  46.9 1.4 %shard_map.82 = bf16[256,1792]{1,0:T(8,128)(2,1)} custom-call(s32[1]{0:T(128)} %bitcast.par, f32[256,1792]{1,0:T(8,128)S(1)} %shard_map.80.mine, bf16[384,768]{1,0:T(8,128)(2,1)S(1)} %get-tuple-element.28.sent_x, bf16[256,1408]{1,0:T(8,128)(2,1)S(1)} %collective-permute-done.5.from_x), custom_call_target="tpu_custom_call" | custom-call | flops 150994944 | bytes 3145732 | tf_op jit(solution)/shard_map/pallas_call | solution.py:25
Async XLA Ops:
  1.0 16.1 %collective-permute-start = (bf16[1568,128]{1,0:T(8,128)(2,1)S(1)}, bf16[1568,128]{1,0:T(8,128)(2,1)S(1)}, u32[]{:S(2)}, u32[]{:S(2)}) collective-permute-start(bf16[1568,128]{1,0:T(8,128)(2,1)S(1)} %shard_map.73.pay), channel_id=1, source_target_pairs={{0,1},{1,0},{2,3},{3,2},{4,5},{5,4},{6,7},{7,6},{8,9},{9,8},{10,11... | collective-permute-start | bytes 1204232 | tf_op jit(solution)/shard_map/ppermute | solution.py:249
  1.1 20.3 %collective-permute-start.1 = (bf16[1568,128]{1,0:T(8,128)(2,1)S(1)}, bf16[1568,128]{1,0:T(8,128)(2,1)S(1)}, u32[]{:S(2)}, u32[]{:S(2)}) collective-permute-start(bf16[1568,128]{1,0:T(8,128)(2,1)S(1)} %shard_map.73.pay), channel_id=1, source_target_pairs={{1,2},{2,1},{3,4},{4,3},{5,6},{6,5},{7,8},{8,7},{9,10},{10,9},{11,... | collective-permute-start | bytes 1204232 | tf_op jit(solution)/shard_map/ppermute | solution.py:249
  12.4 4.8 %copy-start = (s32[1,2,3]{2,1,0:T(2,128)S(1)}, s32[1,2,3]{2,1,0:T(2,128)}, u32[]{:S(2)}) copy-start(s32[1,2,3]{2,1,0:T(2,128)} %ghost.3) | copy-start | bytes 76
  23.2 6.4 %collective-permute-start.2 = (bf16[384,768]{1,0:T(8,128)(2,1)S(1)}, bf16[384,768]{1,0:T(8,128)(2,1)S(1)}, u32[]{:S(2)}, u32[]{:S(2)}) collective-permute-start(bf16[384,768]{1,0:T(8,128)(2,1)S(1)} %get-tuple-element.27), channel_id=1, source_target_pairs={{0,1},{1,0},{2,3},{3,2},{4,5},{5,4},{6,7},{7,6},{8,9},{9,8},{10,11... | collective-permute-start | bytes 1769480 | tf_op jit(solution)/shard_map/ppermute | solution.py:249
  23.3 15.5 %collective-permute-start.3 = (bf16[384,768]{1,0:T(8,128)(2,1)S(1)}, bf16[384,768]{1,0:T(8,128)(2,1)S(1)}, u32[]{:S(2)}, u32[]{:S(2)}) collective-permute-start(bf16[384,768]{1,0:T(8,128)(2,1)S(1)} %get-tuple-element.28.sent_x), channel_id=1, source_target_pairs={{1,2},{2,1},{3,4},{4,3},{5,6},{6,5},{7,8},{8,7},{9,10},{10,9},{11,... | collective-permute-start | bytes 1769480 | tf_op jit(solution)/shard_map/ppermute | solution.py:249
  30.0 16.8 %collective-permute-start.5 = (bf16[256,1408]{1,0:T(8,128)(2,1)S(1)}, bf16[256,1408]{1,0:T(8,128)(2,1)S(1)}, u32[]{:S(2)}, u32[]{:S(2)}) collective-permute-start(bf16[256,1408]{1,0:T(8,128)(2,1)S(1)} %shard_map.81), channel_id=1, source_target_pairs={{1,2},{2,1},{3,4},{4,3},{5,6},{6,5},{7,8},{8,7},{9,10},{10,9},{11,... | collective-permute-start | bytes 2162696 | tf_op jit(solution)/shard_map/ppermute | solution.py:249
  39.4 2.2 %collective-permute-start.4 = (bf16[256,1280]{1,0:T(8,128)(2,1)S(1)}, bf16[256,1280]{1,0:T(8,128)(2,1)S(1)}, u32[]{:S(2)}, u32[]{:S(2)}) collective-permute-start(bf16[256,1280]{1,0:T(8,128)(2,1)S(1)} %shard_map.79), channel_id=1, source_target_pairs={{0,1},{1,0},{2,3},{3,2},{4,5},{5,4},{6,7},{7,6},{8,9},{9,8},{10,11... | collective-permute-start | bytes 1966088 | tf_op jit(solution)/shard_map/ppermute | solution.py:249

commit v3 on v2

v3 whole, which is shorter than its diff:
```python
import functools

import jax
import jax.numpy as jnp
from jax import lax
from jax.experimental import pallas as pl
from jax.experimental.pallas import tpu as pltpu
from jax.sharding import PartitionSpec as P

CA = 2
META = 32
AXES = ("grp", "dev")
VMEM = pltpu.VMEM
SMEM = pltpu.SMEM
F32 = jnp.float32
BF16 = jnp.bfloat16


SPACES = {"v": VMEM, "s": SMEM, "h": pltpu.HBM}


def call(kernel, args, spaces, outs, scratch=(), flops=1, limit=None, aliases=None, out_space=VMEM):
    nbytes = sum(a.size * a.dtype.itemsize for a in args)
    in_specs = [pl.BlockSpec(memory_space=SPACES[c]) for c in spaces]
    return pl.pallas_call(
        kernel,
        out_shape=[jax.ShapeDtypeStruct(*o) for o in outs],
        in_specs=in_specs,
        out_specs=[pl.BlockSpec(memory_space=out_space) for _ in outs],
        scratch_shapes=list(scratch),
        input_output_aliases=aliases or {},
        cost_estimate=pl.CostEstimate(flops=flops, bytes_accessed=nbytes, transcendentals=0),
        compiler_params=pltpu.CompilerParams(vmem_limit_bytes=limit),
    )(*[pltpu.with_memory_space_constraint(a, pltpu.HBM) if c == "h" else a for a, c in zip(args, spaces)])


def rows(index, size):
    return pl.ds(pl.multiple_of(index * size, size), size)


def dot(a, b):
    return jnp.dot(a, b, preferred_element_type=F32)


def pack_kernel(
    r, k, b, s, par, early, damp, agg_hbm, ghost_hbm, tent_hbm, cols_hbm, vals_hbm, inv_hbm,
    out, dense, inv, p_own, agg, ghost, cols, vals, placed, sems, own_sems,
):
    copies = [
        pltpu.make_async_copy(agg_hbm, agg, sems.at[0]),
        pltpu.make_async_copy(ghost_hbm, ghost, sems.at[1]),
        pltpu.make_async_copy(tent_hbm, out.at[: r * b, :], sems.at[2]),
    ]
    for copy in copies:
        copy.start()
    copies[0].wait()
    copies[1].wait()
    sub = lax.broadcasted_iota(jnp.int32, (META, b), 0)
    meta = jnp.zeros((META, b), F32)
    for j in range(r):
        meta = jnp.where(sub == j, agg[j].astype(F32), meta)
    for side in range(2):
        for j in range(s):
            meta = jnp.where(sub == 16 + 8 * side + j, ghost[0, side, j].astype(F32), meta)
    out[r * b :, :] = meta.astype(BF16)
    copies[2].wait()

    @pl.when(early[0] == 1)
    def _():
        own_rows(
            r, k, b, s, par, damp, agg_hbm, cols_hbm, vals_hbm, inv_hbm, out, dense, inv, p_own, agg, cols, vals,
            placed, own_sems,
        )


def own_kernel(
    r, k, b, s, par, early, damp, agg_hbm, cols_hbm, vals_hbm, inv_hbm, pay, dense_in, inv_in, p_own_in,
    dense, inv, p_own, agg, cols, vals, placed, sems,
):
    @pl.when(early[0] == 0)
    def _():
        own_rows(
            r, k, b, s, par, damp, agg_hbm, cols_hbm, vals_hbm, inv_hbm, pay, dense, inv, p_own, agg, cols, vals,
            placed, sems,
        )


def smooth(r, b, dense, cols, placed, inv, damp, target, base=None):
    step = 4
    for t in range(r // step):
        half = dot(dense[t * step * b : (t + 1) * step * b, cols], placed).astype(BF16)
        for q in range(step):
            at = slice((t * step + q) * b, (t * step + q + 1) * b)
            value = -damp[0] * dot(inv[at, :], half[q * b : (q + 1) * b, :])
            if base is not None:
                value = base[at, :].astype(F32) + value
            target[at, :] = value.astype(BF16)


def place_ghosts(r, b, s, ghost, mine, pay, meta, placed):
    meta[...] = pay[r * b :, :].astype(F32)
    for j in range(s):
        row = jnp.clip(ghost[0, mine, j], 0, r - 1)
        block = pay[rows(row, b), :]
        here = jnp.broadcast_to(meta[pl.ds(row, 1), :], (b, b))
        for c in range(CA):
            placed[j * b : (j + 1) * b, c * b : (c + 1) * b] = jnp.where(here == c, block.astype(F32), 0.0).astype(BF16)


def wanted_rows(r, s, theirs, meta):
    found = []
    for j in range(s):
        value = jnp.max(meta[pl.ds(16 + 8 * theirs + j, 1), :])
        found.append(jnp.clip(value.astype(jnp.int32), 0, r - 1))
    return found


def own_rows(
    r, k, b, s, par, damp, agg_hbm, cols_hbm, vals_hbm, inv_hbm, pay, dense, inv, p_own, agg, cols, vals, placed, sems
):
    def fetch(j):
        return pltpu.make_async_copy(vals_hbm.at[j], vals.at[j], sems.at[j])

    others = [
        pltpu.make_async_copy(cols_hbm, cols, sems.at[r]),
        pltpu.make_async_copy(agg_hbm, agg, sems.at[r + 1]),
        pltpu.make_async_copy(inv_hbm, inv, sems.at[r + 2]),
    ]
    others[0].start()
    others[1].start()
    for j in range(r):
        fetch(j).start()
    others[2].start()

    def clear(j, carry):
        dense[rows(j, b), :] = jnp.zeros((b, (r + 2 * s) * b), BF16)
        return carry

    lax.fori_loop(0, r, clear, 0)
    others[0].wait()
    others[1].wait()
    zero = jnp.zeros((b, b), BF16)
    for j in range(r):
        own = slice(j * b, (j + 1) * b)
        block = pay[own, :]
        here = agg[j]
        for c in range(CA):
            placed[own, c * b : (c + 1) * b] = jnp.where(here == c, block, zero)
    odd = par[0]
    left = s * (1 - odd)

    def row(j, carry):
        fetch(j).wait()
        at = rows(j, b)
        for e in range(k):
            c = cols[j, e]
            c = jnp.where(c < r, c, jnp.where(c < r + s, c + left, c - left))
            dense[at, rows(c, b)] = vals[j, e]
        return carry

    lax.fori_loop(0, r, row, 0)
    others[2].wait()
    smooth(r, b, dense, slice(0, r * b), placed[...], inv, damp, p_own, placed)


def near_kernel(r, b, s, ghost, par, damp, dense, inv, p_own, pay, p_s, y_own, meta, placed, flipped):
    flip(r, b, p_own, flipped)
    place_ghosts(r, b, s, ghost, 1 - par[0], pay, meta, placed)
    smooth(r, b, dense, slice(r * b, (r + s) * b), placed[...], inv, damp, p_s)
    y_own[...] = dot(flipped[...], dense[...]).astype(BF16)


def far_kernel(
    r, b, s, w, ghost, par, early, damp, dense, inv, p_s, p_own, pay_s, pay_x,
    p_x, out_x, out_s, y_x, gal_x, meta, near, placed, flipped,
):
    odd = par[0]
    place_ghosts(r, b, s, ghost, odd, pay_x, meta, placed)
    near[...] = pay_s[r * b :, :].astype(F32)
    wanted = (wanted_rows(r, s, 1 - odd, meta), wanted_rows(r, s, odd, near))
    smooth(r, b, dense, slice((r + s) * b, (r + 2 * s) * b), placed[...], inv, damp, p_x)
    for found, out in zip(wanted, (out_x, out_s)):
        for j in range(s):
            at = rows(found[j], b)
            to = slice(j * b, (j + 1) * b)
            out[to, :w] = p_s[at, :]
            out[to, w : 2 * w] = p_own[at, :]
            out[to, 2 * w :] = p_x[at, :]

    @pl.when(early[0] == 1)
    def _():
        part_rows(r, b, w, dense, p_x, (p_s, p_own, p_x), y_x, gal_x, flipped)


def cross_kernel(r, b, w, early, dense, p_s, p_own, p_x, y_in, gal_in, y_x, gal_x, flipped):
    @pl.when(early[0] == 0)
    def _():
        part_rows(r, b, w, dense, p_x, (p_s, p_own, p_x), y_x, gal_x, flipped)


def flip(r, b, p, flipped):
    for j in range(r):
        at = slice(j * b, (j + 1) * b)
        flipped[:, at] = p[at, :].T


def part_rows(r, b, w, dense, p, parts, y, gal, flipped):
    flip(r, b, p, flipped)
    y[...] = dot(flipped[...], dense[...]).astype(BF16)
    for d, other in enumerate(parts):
        gal[:, d * w : (d + 1) * w] = dot(y[:, : r * b], other[...])


def outer_kernel(w, span, gal, y, far_s, out):
    own = y.shape[1] - 2 * span
    by_s = dot(y[:, own : own + span], far_s[...])
    out[:, :w] = by_s[:, 2 * w :].astype(BF16)
    out[:, w : 2 * w] = (gal[:, :w] + by_s[:, w : 2 * w]).astype(BF16)
    out[:, 2 * w : 3 * w] = (gal[:, w : 2 * w] + by_s[:, :w]).astype(BF16)
    out[:, 3 * w : 4 * w] = gal[:, 2 * w :].astype(BF16)
    out[:, 4 * w :] = y[:, own + span :]


def rest_kernel(r, b, w, dense, p_s, p_own, p_x, y_own, y_s, gal_s, gal_own, flipped):
    parts = (p_s, p_own, p_x)
    for d, other in enumerate(parts):
        gal_own[:, d * w : (d + 1) * w] = dot(y_own[:, : r * b], other[...])
    part_rows(r, b, w, dense, p_s, parts, y_s, gal_s, flipped)


def galerkin_rows(w, span, gal, y, far_s, far_x):
    own = y.shape[1] - 2 * span
    by_s = dot(y[:, own : own + span], far_s[...])
    by_x = dot(y[:, own + span :], far_x[...])
    return (
        by_s[:, 2 * w :],
        gal[:, :w] + by_s[:, w : 2 * w],
        gal[:, w : 2 * w] + by_s[:, :w] + by_x[:, 2 * w :],
        gal[:, 2 * w :] + by_x[:, w : 2 * w],
        by_x[:, :w],
    )


def chip_kernel(w, span, gal, y, far_s, far_x, out):
    for c, value in enumerate(galerkin_rows(w, span, gal, y, far_s, far_x)):
        out[:, c * w : (c + 1) * w] = value.astype(BF16)


def inner_kernel(w, span, gal, y, far_s, far_x, from_s, out):
    mine = galerkin_rows(w, span, gal, y, far_s, far_x)
    for u in range(-3, 4):
        total = mine[2 - u] if abs(u) < 3 else jnp.zeros((w, w), F32)
        if 0 <= 1 + u < 5:
            total = total + from_s[:, (1 + u) * w : (2 + u) * w].astype(F32)
        out[:, (3 - u) * w : (4 - u) * w] = total


def final_kernel(w, par, mine, sent_x, from_x, out_hbm, out, sems):
    sign = 1 - 2 * par[0]
    back = dot(from_x[:, 4 * w :], sent_x[...])
    copies = []
    for u in (3, 2, -3, -2, -1, 0, 1):
        total = mine[:, (3 - u) * w : (4 - u) * w]
        if 0 <= 3 + u < 4:
            total = total + from_x[:, (3 + u) * w : (4 + u) * w].astype(F32)
        if abs(u) < 2:
            total = total + back[:, (1 - u) * w : (2 - u) * w]
        out[u + 3, :, :] = total.astype(BF16)
        copies.append(pltpu.make_async_copy(out.at[u + 3], out_hbm.at[:, rows(3 + sign * u, w)], sems.at[u + 3]))
        copies[-1].start()
    for copy in copies:
        copy.wait()


def swap(x, route):
    return lax.ppermute(x, AXES, route)


def shards(block_values, block_columns, tentative, inverse_diagonal, aggregate, ghost_rows, damping):
    r, k = block_columns.shape
    b = tentative.shape[1]
    s = ghost_rows.shape[2]
    w = CA * b
    span = s * b
    devices = lax.axis_size(AXES)
    chip = [(i, i ^ 1) for i in range(devices) if i ^ 1 < devices]
    cross = []
    for i in range(1, devices - 1, 2):
        cross += [(i, i + 1), (i + 1, i)]
    grp, dev = (lax.axis_index(a) for a in AXES)
    par = (dev & 1).astype(jnp.int32).reshape(1)
    early = ((dev == 0) & (grp > 0)).astype(jnp.int32).reshape(1)
    tent = tentative.reshape(r * b, b)
    inv_hbm = inverse_diagonal.reshape(r * b, b)
    dma = pltpu.SemaphoreType.DMA
    total = (r + 2 * s) * b
    own_outs = [((r * b, total), BF16), ((r * b, b), BF16), ((r * b, w), BF16)]
    own_scratch = [SMEM((r, k), jnp.int32), VMEM((r, k, b, b), BF16), VMEM((r * b, w), BF16)]

    pay, dense, inv, p_own = call(
        functools.partial(pack_kernel, r, k, b, s),
        (par, early, damping, aggregate, ghost_rows, tent, block_columns, block_values, inv_hbm), "ssshhhhhh",
        [((r * b + META, b), BF16)] + own_outs,
        scratch=[SMEM((r,), jnp.int32), SMEM((1, 2, s), jnp.int32)] + own_scratch + [dma((3,)), dma((r + 3,))],
        limit=24 << 20,
    )
    pay_x = swap(pay, cross)
    pay_s = swap(pay, chip)
    dense, inv, p_own = call(
        functools.partial(own_kernel, r, k, b, s),
        (par, early, damping, aggregate, block_columns, block_values, inv_hbm, pay, dense, inv, p_own), "ssshhhhvvvv",
        own_outs, scratch=[SMEM((r,), jnp.int32)] + own_scratch + [dma((r + 3,))],
        flops=2 * r * b * r * b * w, limit=24 << 20, aliases={8: 0, 9: 1, 10: 2},
    )
    p_s, y_own = call(
        functools.partial(near_kernel, r, b, s), (ghost_rows, par, damping, dense, inv, p_own, pay_s), "sssvvvv",
        [((r * b, w), BF16), ((w, total), BF16)],
        scratch=[VMEM((META, b), F32), VMEM((span, w), BF16), VMEM((w, r * b), BF16)],
        flops=2 * r * b * total * w, limit=24 << 20,
    )
    p_x, out_x, out_s, y_x, gal_x = call(
        functools.partial(far_kernel, r, b, s, w),
        (ghost_rows, par, early, damping, dense, inv, p_s, p_own, pay_s, pay_x), "ssssvvvvvv",
        [((r * b, w), BF16), ((span, 3 * w), BF16), ((span, 3 * w), BF16), ((w, total), BF16), ((w, 3 * w), F32)],
        scratch=[VMEM((META, b), F32), VMEM((META, b), F32), VMEM((span, w), BF16), VMEM((w, r * b), BF16)],
        flops=2 * r * b * span * w, limit=24 << 20,
    )
    far_x = swap(out_x, cross)
    far_s = swap(out_s, chip)
    y_x, gal_x = call(
        functools.partial(cross_kernel, r, b, w), (early, dense, p_s, p_own, p_x, y_x, gal_x), "svvvvvv",
        [((w, total), BF16), ((w, 3 * w), F32)], scratch=[VMEM((w, r * b), BF16)],
        flops=2 * r * b * r * b * 2 * w, limit=24 << 20, aliases={5: 0, 6: 1},
    )
    (sum_x,) = call(
        functools.partial(outer_kernel, w, span), (gal_x, y_x, far_s), "vvv",
        [((w, 4 * w + span), BF16)], flops=2 * w * span * 3 * w, limit=16 << 20,
    )
    from_x = swap(sum_x, cross)
    y_s, gal_s, gal_own = call(
        functools.partial(rest_kernel, r, b, w), (dense, p_s, p_own, p_x, y_own), "vvvvv",
        [((w, total), BF16), ((w, 3 * w), F32), ((w, 3 * w), F32)], scratch=[VMEM((w, r * b), BF16)],
        flops=2 * r * b * r * b * 2 * w, limit=24 << 20,
    )
    (sum_s,) = call(
        functools.partial(chip_kernel, w, span), (gal_s, y_s, far_s, far_x), "vvvv",
        [((w, 5 * w), BF16)], flops=4 * w * span * 3 * w, limit=16 << 20,
    )
    from_s = swap(sum_s, chip)
    (mine,) = call(
        functools.partial(inner_kernel, w, span), (gal_own, y_own, far_s, far_x, from_s), "vvvvv",
        [((w, 7 * w), F32)], flops=4 * w * span * 3 * w, limit=16 << 20,
    )
    (out,) = call(
        functools.partial(final_kernel, w), (par, mine, out_x, from_x), "svvv",
        [((w, 7 * w), BF16)], scratch=[VMEM((7, w, w), BF16), dma((7,))],
        flops=2 * w * span * 3 * w, limit=16 << 20, out_space=pltpu.HBM,
    )
    return out.reshape(CA, b, 7 * w)


def solution(mesh):
    return jax.shard_map(
        shards,
        mesh=mesh,
        in_specs=(
            P(AXES, None, None, None),
            P(AXES, None),
            P(AXES, None, None),
            P(AXES, None, None),
            P(AXES),
            P(AXES, None, None),
            P(),
        ),
        out_specs=P(AXES, None, None),
        check_vma=False,
    )
```

time: 48.4 us -> 49.2 us (1.017)
  starting transfers between devices: 20.6 us -> 18.6 us
  waiting for transfers between devices: 6.81 us -> 8.61 us
  local copies, waits for them, and re-layouts: 0.01 us -> 0.51 us
    ppermute x6, starting transfers between devices: 20.6 us -> 18.6 us  [swap(): return lax.ppermute(x, AXES, route)]
    ppermute x6, waiting for transfers between devices: 6.81 us -> 8.61 us  [swap(): return lax.ppermute(x, AXES, route)]
    unnamed x2, local copies, waits for them, and re-layouts: 0.01 us -> 0.51 us
  transfers between devices with their start and end apart: 6 -> 6, of which waited for: 2 -> 3; matrix products, arithmetic and copies ran while one was open for 0% -> 0% of each run, Pallas kernels for 33% -> 18%
where the time goes in v3:
time: 49.2 us; the launch traced here: 49 us
  Pallas kernels  20.3 us (41%)
  starting transfers between devices  18.6 us (38%)
  waiting for transfers between devices  8.61 us (18%)
  between operations  0.96 us (2%)
  local copies, waits for them, and re-layouts  0.51 us (1%)
    pallas_call x10, Pallas kernels, call(): pl.pallas_call(kernel, out_shape=[jax.ShapeDtypeStruct(*o) for o in outs]...  20.3 us
    ppermute x6, starting transfers between devices, swap(): return lax.ppermute(x, AXES, route)  18.6 us
    ppermute x6, waiting for transfers between devices, swap(): return lax.ppermute(x, AXES, route)  8.61 us
  transfers between devices with their start and end apart: 6, of which 3 were waited for; matrix products, arithmetic and copies ran while one was open for 0% of the time, Pallas kernels for 18%

profile of v3, /device:TPU:6, one launch (start us, length us, event | category | flops | bytes accessed | tf_op | source)
XLA Modules:
  0.0 49.0 jit_solution(9222144009846736964)
XLA Ops:
  0.7 5.8 %shard_map.73 = (bf16[1568,128]{1,0:T(8,128)(2,1)S(1)}, bf16[1536,2304]{1,0:T(8,128)(2,1)S(1)}, bf16[1536,128]{1,0:T(8,128)(2,1)S(1)}, bf16[1536,256]{1,0:T(8,128)(2,1)S(1)}) custom-call(s32[1]{0:T(128)} %bitcast.par, s32[1]{0:T(128)} %bitcast.1.early, f32[1]{0:T(128)S(6)} %copy.18.damp, s32[12]{0:T(128)} %agg_hbm.3, s32[1,2,3]{2,1,0:T(2,128)} %ghost.3, ...), custom_call_target="tpu_custom_call" | custom-call | flops 1 | bytes 4325892 | tf_op jit(solution)/shard_map/pallas_call | solution.py:25
  6.5 0.1 collective-permute-start
  6.6 5.9 %collective-permute-start.1 = (bf16[1568,128]{1,0:T(8,128)(2,1)S(1)}, bf16[1568,128]{1,0:T(8,128)(2,1)S(1)}, u32[]{:S(2)}, u32[]{:S(2)}) collective-permute-start(bf16[1568,128]{1,0:T(8,128)(2,1)S(1)} %get-tuple-element.24.pay), channel_id=1, source_target_pairs={{1,2},{2,1},{3,4},{4,3},{5,6},{6,5},{7,8},{8,7},{9,10},{10,9},{11,... | collective-permute-start | bytes 1204232 | tf_op jit(solution)/shard_map/ppermute | solution.py:276
  12.5 0.0 copy-start
  12.5 0.1 shard_map.74
  12.7 0.0 collective-permute-done.pay.pay_s
  12.7 0.5 %copy-done = s32[1,2,3]{2,1,0:T(2,128)S(1)} copy-done((s32[1,2,3]{2,1,0:T(2,128)S(1)}, s32[1,2,3]{2,1,0:T(2,128)}, u32[]{:S(2)}) %copy-start) | copy-done | bytes 48
  13.2 3.8 %shard_map.75 = (bf16[1536,256]{1,0:T(8,128)(2,1)S(1)}, bf16[256,2304]{1,0:T(8,128)(2,1)S(1)}) custom-call(s32[1,2,3]{2,1,0:T(2,128)S(1)} %copy-done, s32[1]{0:T(128)} %bitcast.par, f32[1]{0:T(128)S(6)} %copy.18.damp, bf16[1536,2304]{1,0:T(8,128)(2,1)S(1)} %get-tuple-element.28.dense, bf16[1536,128]{1,0:T(8,128)(2,1)S(1)} %get-tuple-element.29.inv, ...), custom_call_target="tpu_custom_call" | custom-call | flops 1811939328 | bytes 8658976 | tf_op jit(solution)/shard_map/pallas_call | solution.py:25
  16.9 3.0 %collective-permute-done.1.pay_x = bf16[1568,128]{1,0:T(8,128)(2,1)S(1)} collective-permute-done((bf16[1568,128]{1,0:T(8,128)(2,1)S(1)}, bf16[1568,128]{1,0:T(8,128)(2,1)S(1)}, u32[]{:S(2)}, u32[]{:S(2)}) %collective-permute-start.1) | collective-permute-done | bytes 401440 | tf_op jit(solution)/shard_map/ppermute | solution.py:276
  20.0 4.5 %shard_map.76 = (bf16[1536,256]{1,0:T(8,128)(2,1)S(1)}, bf16[384,768]{1,0:T(8,128)(2,1)S(1)}, bf16[384,768]{1,0:T(8,128)(2,1)S(1)}, bf16[256,2304]{1,0:T(8,128)(2,1)S(1)}, f32[256,768]{1,0:T(8,128)S(1)}) custom-call(s32[1,2,3]{2,1,0:T(2,128)S(1)} %copy-done, s32[1]{0:T(128)} %bitcast.par, s32[1]{0:T(128)} %bitcast.1.early, f32[1]{0:T(128)S(6)} %copy.18.damp, ...), custom_call_target="tpu_custom_call" | custom-call | flops 301989888 | bytes 9846820 | tf_op jit(solution)/shard_map/pallas_call | solution.py:25
  24.4 0.1 collective-permute-start.2
  24.5 3.3 %collective-permute-start.3 = (bf16[384,768]{1,0:T(8,128)(2,1)S(1)}, bf16[384,768]{1,0:T(8,128)(2,1)S(1)}, u32[]{:S(2)}, u32[]{:S(2)}) collective-permute-start(bf16[384,768]{1,0:T(8,128)(2,1)S(1)} %get-tuple-element.36.sent_x), channel_id=1, source_target_pairs={{1,2},{2,1},{3,4},{4,3},{5,6},{6,5},{7,8},{8,7},{9,10},{10,9},{11,... | collective-permute-start | bytes 1769480 | tf_op jit(solution)/shard_map/ppermute | solution.py:276
  27.8 0.2 shard_map.80
  28.0 0.0 collective-permute-done.2.far_s
  28.0 0.4 shard_map.81
  28.4 9.2 %collective-permute-start.5 = (bf16[256,1408]{1,0:T(8,128)(2,1)S(1)}, bf16[256,1408]{1,0:T(8,128)(2,1)S(1)}, u32[]{:S(2)}, u32[]{:S(2)}) collective-permute-start(bf16[256,1408]{1,0:T(8,128)(2,1)S(1)} %shard_map.81), channel_id=1, source_target_pairs={{1,2},{2,1},{3,4},{4,3},{5,6},{6,5},{7,8},{8,7},{9,10},{10,9},{11,... | collective-permute-start | bytes 2162696 | tf_op jit(solution)/shard_map/ppermute | solution.py:276
  37.6 3.2 %shard_map.77 = (bf16[256,2304]{1,0:T(8,128)(2,1)S(1)}, f32[256,768]{1,0:T(8,128)S(1)}, f32[256,768]{1,0:T(8,128)S(1)}) custom-call(bf16[1536,2304]{1,0:T(8,128)(2,1)S(1)} %get-tuple-element.28.dense, bf16[1536,256]{1,0:T(8,128)(2,1)S(1)} %get-tuple-element.31.p_s, bf16[1536,256]{1,0:T(8,128)(2,1)S(1)} %get-tuple-element.30.p_own, ...), custom_call_target="tpu_custom_call" | custom-call | flops 2415919104 | bytes 10616832 | tf_op jit(solution)/shard_map/pallas_call | solution.py:25
  40.8 0.0 collective-permute-done.3.far_x
  40.8 0.6 %shard_map.78 = bf16[256,1280]{1,0:T(8,128)(2,1)S(1)} custom-call(f32[256,768]{1,0:T(8,128)S(1)} %get-tuple-element.37.gal, bf16[256,2304]{1,0:T(8,128)(2,1)S(1)} %get-tuple-element.38.y, bf16[384,768]{1,0:T(8,128)(2,1)S(1)} %collective-permute-done.2.far_s, bf16[384,768]{1,0:T(8,128)(2,1)S(1)} %collective-permute-done.3.far_x), custom_call_target="tpu_custom_call" | custom-call | flops 301989888 | bytes 3145728 | tf_op jit(solution)/shard_map/pallas_call | solution.py:25
  41.4 0.1 collective-permute-start.4
  41.5 2.1 %collective-permute-done.4.from_s = bf16[256,1280]{1,0:T(8,128)(2,1)S(1)} collective-permute-done((bf16[256,1280]{1,0:T(8,128)(2,1)S(1)}, bf16[256,1280]{1,0:T(8,128)(2,1)S(1)}, u32[]{:S(2)}, u32[]{:S(2)}) %collective-permute-start.4) | collective-permute-done | bytes 655392 | tf_op jit(solution)/shard_map/ppermute | solution.py:276
  43.6 0.6 %shard_map.79.mine = f32[256,1792]{1,0:T(8,128)S(1)} custom-call(f32[256,768]{1,0:T(8,128)S(1)} %get-tuple-element.34.gal, bf16[256,2304]{1,0:T(8,128)(2,1)S(1)} %get-tuple-element.33.y_own.y, bf16[384,768]{1,0:T(8,128)(2,1)S(1)} %collective-permute-done.2.far_s, bf16[384,768]{1,0:T(8,128)(2,1)S(1)} %collective-permute-done.3.far_x, ...), custom_call_target="tpu_custom_call" | custom-call | flops 301989888 | bytes 3801088 | tf_op jit(solution)/shard_map/pallas_call | solution.py:25
  44.2 3.5 %collective-permute-done.5.from_x = bf16[256,1408]{1,0:T(8,128)(2,1)S(1)} collective-permute-done((bf16[256,1408]{1,0:T(8,128)(2,1)S(1)}, bf16[256,1408]{1,0:T(8,128)(2,1)S(1)}, u32[]{:S(2)}, u32[]{:S(2)}) %collective-permute-start.5) | collective-permute-done | bytes 720928 | tf_op jit(solution)/shard_map/ppermute | solution.py:276
  47.7 1.2 %shard_map.82 = bf16[256,1792]{1,0:T(8,128)(2,1)} custom-call(s32[1]{0:T(128)} %bitcast.par, f32[256,1792]{1,0:T(8,128)S(1)} %shard_map.79.mine, bf16[384,768]{1,0:T(8,128)(2,1)S(1)} %get-tuple-element.36.sent_x, bf16[256,1408]{1,0:T(8,128)(2,1)S(1)} %collective-permute-done.5.from_x), custom_call_target="tpu_custom_call" | custom-call | flops 150994944 | bytes 3145732 | tf_op jit(solution)/shard_map/pallas_call | solution.py:25
Async XLA Ops:
  6.5 6.2 %collective-permute-start = (bf16[1568,128]{1,0:T(8,128)(2,1)S(1)}, bf16[1568,128]{1,0:T(8,128)(2,1)S(1)}, u32[]{:S(2)}, u32[]{:S(2)}) collective-permute-start(bf16[1568,128]{1,0:T(8,128)(2,1)S(1)} %get-tuple-element.24.pay), channel_id=1, source_target_pairs={{0,1},{1,0},{2,3},{3,2},{4,5},{5,4},{6,7},{7,6},{8,9},{9,8},{10,11... | collective-permute-start | bytes 1204232 | tf_op jit(solution)/shard_map/ppermute | solution.py:276
  6.6 13.4 %collective-permute-start.1 = (bf16[1568,128]{1,0:T(8,128)(2,1)S(1)}, bf16[1568,128]{1,0:T(8,128)(2,1)S(1)}, u32[]{:S(2)}, u32[]{:S(2)}) collective-permute-start(bf16[1568,128]{1,0:T(8,128)(2,1)S(1)} %get-tuple-element.24.pay), channel_id=1, source_target_pairs={{1,2},{2,1},{3,4},{4,3},{5,6},{6,5},{7,8},{8,7},{9,10},{10,9},{11,... | collective-permute-start | bytes 1204232 | tf_op jit(solution)/shard_map/ppermute | solution.py:276
  12.5 0.7 %copy-start = (s32[1,2,3]{2,1,0:T(2,128)S(1)}, s32[1,2,3]{2,1,0:T(2,128)}, u32[]{:S(2)}) copy-start(s32[1,2,3]{2,1,0:T(2,128)} %ghost.3) | copy-start | bytes 76
  24.4 3.6 %collective-permute-start.2 = (bf16[384,768]{1,0:T(8,128)(2,1)S(1)}, bf16[384,768]{1,0:T(8,128)(2,1)S(1)}, u32[]{:S(2)}, u32[]{:S(2)}) collective-permute-start(bf16[384,768]{1,0:T(8,128)(2,1)S(1)} %get-tuple-element.35), channel_id=1, source_target_pairs={{0,1},{1,0},{2,3},{3,2},{4,5},{5,4},{6,7},{7,6},{8,9},{9,8},{10,11... | collective-permute-start | bytes 1769480 | tf_op jit(solution)/shard_map/ppermute | solution.py:276
  24.5 16.3 %collective-permute-start.3 = (bf16[384,768]{1,0:T(8,128)(2,1)S(1)}, bf16[384,768]{1,0:T(8,128)(2,1)S(1)}, u32[]{:S(2)}, u32[]{:S(2)}) collective-permute-start(bf16[384,768]{1,0:T(8,128)(2,1)S(1)} %get-tuple-element.36.sent_x), channel_id=1, source_target_pairs={{1,2},{2,1},{3,4},{4,3},{5,6},{6,5},{7,8},{8,7},{9,10},{10,9},{11,... | collective-permute-start | bytes 1769480 | tf_op jit(solution)/shard_map/ppermute | solution.py:276
  28.4 19.3 %collective-permute-start.5 = (bf16[256,1408]{1,0:T(8,128)(2,1)S(1)}, bf16[256,1408]{1,0:T(8,128)(2,1)S(1)}, u32[]{:S(2)}, u32[]{:S(2)}) collective-permute-start(bf16[256,1408]{1,0:T(8,128)(2,1)S(1)} %shard_map.81), channel_id=1, source_target_pairs={{1,2},{2,1},{3,4},{4,3},{5,6},{6,5},{7,8},{8,7},{9,10},{10,9},{11,... | collective-permute-start | bytes 2162696 | tf_op jit(solution)/shard_map/ppermute | solution.py:276
  41.4 2.2 %collective-permute-start.4 = (bf16[256,1280]{1,0:T(8,128)(2,1)S(1)}, bf16[256,1280]{1,0:T(8,128)(2,1)S(1)}, u32[]{:S(2)}, u32[]{:S(2)}) collective-permute-start(bf16[256,1280]{1,0:T(8,128)(2,1)S(1)} %shard_map.78), channel_id=1, source_target_pairs={{0,1},{1,0},{2,3},{3,2},{4,5},{5,4},{6,7},{7,6},{8,9},{9,8},{10,11... | collective-permute-start | bytes 1966088 | tf_op jit(solution)/shard_map/ppermute | solution.py:276

commit v4 on v3

--- a/solution.py
+++ b/solution.py
@@ -42,10 +42,7 @@
     return jnp.dot(a, b, preferred_element_type=F32)
 
 
-def pack_kernel(
-    r, k, b, s, par, early, damp, agg_hbm, ghost_hbm, tent_hbm, cols_hbm, vals_hbm, inv_hbm,
-    out, dense, inv, p_own, agg, ghost, cols, vals, placed, sems, own_sems,
-):
+def pack_kernel(r, b, s, agg_hbm, ghost_hbm, tent_hbm, out, agg, ghost, sems):
     copies = [
         pltpu.make_async_copy(agg_hbm, agg, sems.at[0]),
         pltpu.make_async_copy(ghost_hbm, ghost, sems.at[1]),
@@ -65,25 +62,6 @@
     out[r * b :, :] = meta.astype(BF16)
     copies[2].wait()
 
-    @pl.when(early[0] == 1)
-    def _():
-        own_rows(
-            r, k, b, s, par, damp, agg_hbm, cols_hbm, vals_hbm, inv_hbm, out, dense, inv, p_own, agg, cols, vals,
-            placed, own_sems,
-        )
-
-
-def own_kernel(
-    r, k, b, s, par, early, damp, agg_hbm, cols_hbm, vals_hbm, inv_hbm, pay, dense_in, inv_in, p_own_in,
-    dense, inv, p_own, agg, cols, vals, placed, sems,
-):
-    @pl.when(early[0] == 0)
-    def _():
-        own_rows(
-            r, k, b, s, par, damp, agg_hbm, cols_hbm, vals_hbm, inv_hbm, pay, dense, inv, p_own, agg, cols, vals,
-            placed, sems,
-        )
-
 
 def smooth(r, b, dense, cols, placed, inv, damp, target, base=None):
     step = 4
@@ -115,7 +93,7 @@
     return found
 
 
-def own_rows(
+def own_kernel(
     r, k, b, s, par, damp, agg_hbm, cols_hbm, vals_hbm, inv_hbm, pay, dense, inv, p_own, agg, cols, vals, placed, sems
 ):
     def fetch(j):
@@ -163,17 +141,12 @@
     smooth(r, b, dense, slice(0, r * b), placed[...], inv, damp, p_own, placed)
 
 
-def near_kernel(r, b, s, ghost, par, damp, dense, inv, p_own, pay, p_s, y_own, meta, placed, flipped):
-    flip(r, b, p_own, flipped)
+def near_kernel(r, b, s, ghost, par, damp, dense, inv, pay, p_s, meta, placed):
     place_ghosts(r, b, s, ghost, 1 - par[0], pay, meta, placed)
     smooth(r, b, dense, slice(r * b, (r + s) * b), placed[...], inv, damp, p_s)
-    y_own[...] = dot(flipped[...], dense[...]).astype(BF16)
-
-
-def far_kernel(
-    r, b, s, w, ghost, par, early, damp, dense, inv, p_s, p_own, pay_s, pay_x,
-    p_x, out_x, out_s, y_x, gal_x, meta, near, placed, flipped,
-):
+
+
+def far_kernel(r, b, s, w, ghost, par, damp, dense, inv, p_s, p_own, pay_s, pay_x, p_x, out_x, out_s, meta, near, placed):
     odd = par[0]
     place_ghosts(r, b, s, ghost, odd, pay_x, meta, placed)
     near[...] = pay_s[r * b :, :].astype(F32)
@@ -187,15 +160,25 @@
             out[to, w : 2 * w] = p_own[at, :]
             out[to, 2 * w :] = p_x[at, :]
 
-    @pl.when(early[0] == 1)
+
+def cross_kernel(parity, r, b, w, par, dense, p_s, p_own, p_x, far_s, *refs):
+    out, y_own, y, flipped = refs[-4:]
+
+    @pl.when(par[0] == parity)
     def _():
-        part_rows(r, b, w, dense, p_x, (p_s, p_own, p_x), y_x, gal_x, flipped)
-
-
-def cross_kernel(r, b, w, early, dense, p_s, p_own, p_x, y_in, gal_in, y_x, gal_x, flipped):
-    @pl.when(early[0] == 0)
-    def _():
-        part_rows(r, b, w, dense, p_x, (p_s, p_own, p_x), y_x, gal_x, flipped)
+        flip(r, b, p_x, flipped)
+        y[...] = dot(flipped[...], dense[...]).astype(BF16)
+        inside = y[:, : r * b]
+        own = r * b
+        span = far_s.shape[0]
+        by_s = dot(y[:, own : own + span], far_s[...])
+        out[:, :w] = by_s[:, 2 * w :].astype(BF16)
+        out[:, w : 2 * w] = (dot(inside, p_s[...]) + by_s[:, w : 2 * w]).astype(BF16)
+        out[:, 2 * w : 3 * w] = (dot(inside, p_own[...]) + by_s[:, :w]).astype(BF16)
+        out[:, 3 * w : 4 * w] = dot(inside, p_x[...]).astype(BF16)
+        out[:, 4 * w :] = y[:, own + span :]
+        flip(r, b, p_own, flipped)
+        y_own[...] = dot(flipped[...], dense[...]).astype(BF16)
 
 
 def flip(r, b, p, flipped):
@@ -209,16 +192,6 @@
     y[...] = dot(flipped[...], dense[...]).astype(BF16)
     for d, other in enumerate(parts):
         gal[:, d * w : (d + 1) * w] = dot(y[:, : r * b], other[...])
-
-
-def outer_kernel(w, span, gal, y, far_s, out):
-    own = y.shape[1] - 2 * span
-    by_s = dot(y[:, own : own + span], far_s[...])
-    out[:, :w] = by_s[:, 2 * w :].astype(BF16)
-    out[:, w : 2 * w] = (gal[:, :w] + by_s[:, w : 2 * w]).astype(BF16)
-    out[:, 2 * w : 3 * w] = (gal[:, w : 2 * w] + by_s[:, :w]).astype(BF16)
-    out[:, 3 * w : 4 * w] = gal[:, 2 * w :].astype(BF16)
-    out[:, 4 * w :] = y[:, own + span :]
 
 
 def rest_kernel(r, b, w, dense, p_s, p_own, p_x, y_own, y_s, gal_s, gal_own, flipped):
@@ -255,21 +228,30 @@
         out[:, (3 - u) * w : (4 - u) * w] = total
 
 
-def final_kernel(w, par, mine, sent_x, from_x, out_hbm, out, sems):
-    sign = 1 - 2 * par[0]
-    back = dot(from_x[:, 4 * w :], sent_x[...])
-    copies = []
-    for u in (3, 2, -3, -2, -1, 0, 1):
-        total = mine[:, (3 - u) * w : (4 - u) * w]
-        if 0 <= 3 + u < 4:
-            total = total + from_x[:, (3 + u) * w : (4 + u) * w].astype(F32)
-        if abs(u) < 2:
-            total = total + back[:, (1 - u) * w : (2 - u) * w]
-        out[u + 3, :, :] = total.astype(BF16)
-        copies.append(pltpu.make_async_copy(out.at[u + 3], out_hbm.at[:, rows(3 + sign * u, w)], sems.at[u + 3]))
-        copies[-1].start()
-    for copy in copies:
-        copy.wait()
+def final_kernel(w, par, mine, sent_x, from_odd, from_even, out_hbm, out, sems):
+    def finish(sign, from_x):
+        back = dot(from_x[:, 4 * w :], sent_x[...])
+        copies = []
+        for u in (3, 2, -3, -2, -1, 0, 1):
+            total = mine[:, (3 - u) * w : (4 - u) * w]
+            if 0 <= 3 + u < 4:
+                total = total + from_x[:, (3 + u) * w : (4 + u) * w].astype(F32)
+            if abs(u) < 2:
+                total = total + back[:, (1 - u) * w : (2 - u) * w]
+            out[u + 3, :, :] = total.astype(BF16)
+            place = out_hbm.at[:, (3 + sign * u) * w : (4 + sign * u) * w]
+            copies.append(pltpu.make_async_copy(out.at[u + 3], place, sems.at[u + 3]))
+            copies[-1].start()
+        for copy in copies:
+            copy.wait()
+
+    @pl.when(par[0] == 0)
+    def _():
+        finish(1, from_odd)
+
+    @pl.when(par[0] == 1)
+    def _():
+        finish(-1, from_even)
 
 
 def swap(x, route):
@@ -284,59 +266,60 @@
     span = s * b
     devices = lax.axis_size(AXES)
     chip = [(i, i ^ 1) for i in range(devices) if i ^ 1 < devices]
-    cross = []
-    for i in range(1, devices - 1, 2):
-        cross += [(i, i + 1), (i + 1, i)]
-    grp, dev = (lax.axis_index(a) for a in AXES)
+    up = [(i, i + 1) for i in range(1, devices - 1, 2)]
+    down = [(j, i) for i, j in up]
+    _, dev = (lax.axis_index(a) for a in AXES)
     par = (dev & 1).astype(jnp.int32).reshape(1)
-    early = ((dev == 0) & (grp > 0)).astype(jnp.int32).reshape(1)
     tent = tentative.reshape(r * b, b)
-    inv_hbm = inverse_diagonal.reshape(r * b, b)
+    inv = inverse_diagonal.reshape(r * b, b)
     dma = pltpu.SemaphoreType.DMA
     total = (r + 2 * s) * b
-    own_outs = [((r * b, total), BF16), ((r * b, b), BF16), ((r * b, w), BF16)]
-    own_scratch = [SMEM((r, k), jnp.int32), VMEM((r, k, b, b), BF16), VMEM((r * b, w), BF16)]
-
-    pay, dense, inv, p_own = call(
-        functools.partial(pack_kernel, r, k, b, s),
-        (par, early, damping, aggregate, ghost_rows, tent, block_columns, block_values, inv_hbm), "ssshhhhhh",
-        [((r * b + META, b), BF16)] + own_outs,
-        scratch=[SMEM((r,), jnp.int32), SMEM((1, 2, s), jnp.int32)] + own_scratch + [dma((3,)), dma((r + 3,))],
-        limit=24 << 20,
-    )
-    pay_x = swap(pay, cross)
+
+    (pay,) = call(
+        functools.partial(pack_kernel, r, b, s), (aggregate, ghost_rows, tent), "hhh",
+        [((r * b + META, b), BF16)],
+        scratch=[SMEM((r,), jnp.int32), SMEM((1, 2, s), jnp.int32), dma((3,))], limit=2 << 20,
+    )
+    pay_x = swap(pay, up + down)
     pay_s = swap(pay, chip)
     dense, inv, p_own = call(
         functools.partial(own_kernel, r, k, b, s),
-        (par, early, damping, aggregate, block_columns, block_values, inv_hbm, pay, dense, inv, p_own), "ssshhhhvvvv",
-        own_outs, scratch=[SMEM((r,), jnp.int32)] + own_scratch + [dma((r + 3,))],
-        flops=2 * r * b * r * b * w, limit=24 << 20, aliases={8: 0, 9: 1, 10: 2},
-    )
-    p_s, y_own = call(
-        functools.partial(near_kernel, r, b, s), (ghost_rows, par, damping, dense, inv, p_own, pay_s), "sssvvvv",
-        [((r * b, w), BF16), ((w, total), BF16)],
-        scratch=[VMEM((META, b), F32), VMEM((span, w), BF16), VMEM((w, r * b), BF16)],
-        flops=2 * r * b * total * w, limit=24 << 20,
-    )
-    p_x, out_x, out_s, y_x, gal_x = call(
+        (par, damping, aggregate, block_columns, block_values, inv, pay), "sshhhhv",
+        [((r * b, total), BF16), ((r * b, b), BF16), ((r * b, w), BF16)],
+        scratch=[
+            SMEM((r,), jnp.int32), SMEM((r, k), jnp.int32), VMEM((r, k, b, b), BF16), VMEM((r * b, w), BF16),
+            dma((r + 3,)),
+        ],
+        flops=2 * r * b * r * b * w, limit=24 << 20,
+    )
+    (p_s,) = call(
+        functools.partial(near_kernel, r, b, s), (ghost_rows, par, damping, dense, inv, pay_s), "sssvvv",
+        [((r * b, w), BF16)], scratch=[VMEM((META, b), F32), VMEM((span, w), BF16)],
+        flops=2 * r * b * span * w, limit=24 << 20,
+    )
+    p_x, out_x, out_s = call(
         functools.partial(far_kernel, r, b, s, w),
-        (ghost_rows, par, early, damping, dense, inv, p_s, p_own, pay_s, pay_x), "ssssvvvvvv",
-        [((r * b, w), BF16), ((span, 3 * w), BF16), ((span, 3 * w), BF16), ((w, total), BF16), ((w, 3 * w), F32)],
-        scratch=[VMEM((META, b), F32), VMEM((META, b), F32), VMEM((span, w), BF16), VMEM((w, r * b), BF16)],
+        (ghost_rows, par, damping, dense, inv, p_s, p_own, pay_s, pay_x), "sssvvvvvv",
+        [((r * b, w), BF16), ((span, 3 * w), BF16), ((span, 3 * w), BF16)],
+        scratch=[VMEM((META, b), F32), VMEM((META, b), F32), VMEM((span, w), BF16)],
         flops=2 * r * b * span * w, limit=24 << 20,
     )
-    far_x = swap(out_x, cross)
+    far_x = swap(out_x, up + down)
     far_s = swap(out_s, chip)
-    y_x, gal_x = call(
-        functools.partial(cross_kernel, r, b, w), (early, dense, p_s, p_own, p_x, y_x, gal_x), "svvvvvv",
-        [((w, total), BF16), ((w, 3 * w), F32)], scratch=[VMEM((w, r * b), BF16)],
-        flops=2 * r * b * r * b * 2 * w, limit=24 << 20, aliases={5: 0, 6: 1},
-    )
-    (sum_x,) = call(
-        functools.partial(outer_kernel, w, span), (gal_x, y_x, far_s), "vvv",
-        [((w, 4 * w + span), BF16)], flops=2 * w * span * 3 * w, limit=16 << 20,
-    )
-    from_x = swap(sum_x, cross)
+    shapes = [((w, 4 * w + span), BF16), ((w, total), BF16)]
+    scratch = [VMEM((w, total), BF16), VMEM((w, r * b), BF16)]
+    flops = 2 * r * b * r * b * 4 * w
+    ready = (par, dense, p_s, p_own, p_x, far_s)
+    sum_odd, y_own = call(
+        functools.partial(cross_kernel, 1, r, b, w), ready, "svvvvv",
+        shapes, scratch=scratch, flops=flops, limit=24 << 20,
+    )
+    from_odd = swap(sum_odd, up)
+    sum_even, y_own = call(
+        functools.partial(cross_kernel, 0, r, b, w), ready + (y_own,), "svvvvvv",
+        shapes, scratch=scratch, flops=flops, limit=24 << 20, aliases={6: 1},
+    )
+    from_even = swap(sum_even, down)
     y_s, gal_s, gal_own = call(
         functools.partial(rest_kernel, r, b, w), (dense, p_s, p_own, p_x, y_own), "vvvvv",
         [((w, total), BF16), ((w, 3 * w), F32), ((w, 3 * w), F32)], scratch=[VMEM((w, r * b), BF16)],
@@ -352,7 +335,7 @@
         [((w, 7 * w), F32)], flops=4 * w * span * 3 * w, limit=16 << 20,
     )
     (out,) = call(
-        functools.partial(final_kernel, w), (par, mine, out_x, from_x), "svvv",
+        functools.partial(final_kernel, w), (par, mine, out_x, from_odd, from_even), "svvvv",
         [((w, 7 * w), BF16)], scratch=[VMEM((7, w, w), BF16), dma((7,))],
         flops=2 * w * span * 3 * w, limit=16 << 20, out_space=pltpu.HBM,
     )

time: 49.2 us -> 54.1 us (1.100)
  starting transfers between devices: 18.6 us -> 22 us
  waiting for transfers between devices: 8.61 us -> 11 us
    ppermute x6 -> x7, starting transfers between devices: 18.6 us -> 22 us  [swap(): return lax.ppermute(x, AXES, route)]
    ppermute x6 -> x7, waiting for transfers between devices: 8.61 us -> 11 us  [swap(): return lax.ppermute(x, AXES, route)]
  transfers between devices with their start and end apart: 6 -> 7, of which waited for: 3 -> 3; matrix products, arithmetic and copies ran while one was open for 0% -> 0% of each run, Pallas kernels for 18% -> 29%
where the time goes in v4:
time: 54.1 us; the launch traced here: 53.9 us
  starting transfers between devices  22 us (41%)
  Pallas kernels  19.9 us (37%)
  waiting for transfers between devices  11 us (20%)
  between operations  0.98 us (2%)
    ppermute x7, starting transfers between devices, swap(): return lax.ppermute(x, AXES, route)  22 us
    pallas_call x10, Pallas kernels, call(): pl.pallas_call(kernel, out_shape=[jax.ShapeDtypeStruct(*o) for o in outs]...  19.9 us
    ppermute x7, waiting for transfers between devices, swap(): return lax.ppermute(x, AXES, route)  11 us
  transfers between devices with their start and end apart: 7, of which 3 were waited for; matrix products, arithmetic and copies ran while one was open for 0% of the time, Pallas kernels for 29%

profile of v4, /device:TPU:6, one launch (start us, length us, event | category | flops | bytes accessed | tf_op | source)
XLA Modules:
  0.0 53.9 jit_solution(12657702271571411314)
XLA Ops:
  0.0 1.0 %shard_map.73.pay = bf16[1568,128]{1,0:T(8,128)(2,1)S(1)} custom-call(s32[12]{0:T(128)} %agg_hbm.3, s32[1,2,3]{2,1,0:T(2,128)} %ghost.3, bf16[1536,128]{1,0:T(8,128)(2,1)} %bitcast.4), custom_call_target="tpu_custom_call" | custom-call | flops 1 | bytes 393288 | tf_op jit(solution)/shard_map/pallas_call | solution.py:25
  1.0 0.1 collective-permute-start
  1.1 10.6 %collective-permute-start.1 = (bf16[1568,128]{1,0:T(8,128)(2,1)S(1)}, bf16[1568,128]{1,0:T(8,128)(2,1)S(1)}, u32[]{:S(2)}, u32[]{:S(2)}) collective-permute-start(bf16[1568,128]{1,0:T(8,128)(2,1)S(1)} %shard_map.73.pay), channel_id=1, source_target_pairs={{1,2},{3,4},{5,6},{7,8},{9,10},{11,12},{13,14},{15,16},{17,18},{19... | collective-permute-start | bytes 1204232 | tf_op jit(solution)/shard_map/ppermute | solution.py:258
  12.4 0.0 copy-start
  12.4 4.8 %shard_map.74 = (bf16[1536,2304]{1,0:T(8,128)(2,1)S(1)}, bf16[1536,128]{1,0:T(8,128)(2,1)S(1)}, bf16[1536,256]{1,0:T(8,128)(2,1)S(1)}) custom-call(s32[1]{0:T(128)} %bitcast.par, f32[1]{0:T(128)S(6)} %copy.10.damp, s32[12]{0:T(128)} %agg_hbm.3, s32[12,9]{1,0:T(8,128)} %cols_hbm.1, bf16[12,9,128,128]{3,2,1,0:T(8,128)(2,1)} %vals_hbm.1, ...), custom_call_target="tpu_custom_call" | custom-call | flops 1207959552 | bytes 4334056 | tf_op jit(solution)/shard_map/pallas_call | solution.py:25
  17.1 0.0 collective-permute-done.pay.pay_s
  17.2 0.0 copy-done
  17.2 1.8 %shard_map.75.p_s = bf16[1536,256]{1,0:T(8,128)(2,1)S(1)} custom-call(s32[1,2,3]{2,1,0:T(2,128)S(1)} %copy-done, s32[1]{0:T(128)} %bitcast.par, f32[1]{0:T(128)S(6)} %copy.10.damp, bf16[1536,2304]{1,0:T(8,128)(2,1)S(1)} %get-tuple-element.18.dense, bf16[1536,128]{1,0:T(8,128)(2,1)S(1)} %get-tuple-element.19.inv, ...), custom_call_target="tpu_custom_call" | custom-call | flops 301989888 | bytes 7872544 | tf_op jit(solution)/shard_map/pallas_call | solution.py:25
  18.9 0.0 collective-permute-done.1.pay_x
  19.0 1.8 %shard_map.76 = (bf16[1536,256]{1,0:T(8,128)(2,1)S(1)}, bf16[384,768]{1,0:T(8,128)(2,1)S(1)}, bf16[384,768]{1,0:T(8,128)(2,1)S(1)}) custom-call(s32[1,2,3]{2,1,0:T(2,128)S(1)} %copy-done, s32[1]{0:T(128)} %bitcast.par, f32[1]{0:T(128)S(6)} %copy.10.damp, bf16[1536,2304]{1,0:T(8,128)(2,1)S(1)} %get-tuple-element.18.dense, ...), custom_call_target="tpu_custom_call" | custom-call | flops 301989888 | bytes 9846816 | tf_op jit(solution)/shard_map/pallas_call | solution.py:25
  20.8 0.1 collective-permute-start.2
  20.9 6.1 %collective-permute-start.3 = (bf16[384,768]{1,0:T(8,128)(2,1)S(1)}, bf16[384,768]{1,0:T(8,128)(2,1)S(1)}, u32[]{:S(2)}, u32[]{:S(2)}) collective-permute-start(bf16[384,768]{1,0:T(8,128)(2,1)S(1)} %get-tuple-element.26.sent_x), channel_id=1, source_target_pairs={{1,2},{3,4},{5,6},{7,8},{9,10},{11,12},{13,14},{15,16},{17,18},{19... | collective-permute-start | bytes 1769480 | tf_op jit(solution)/shard_map/ppermute | solution.py:258
  27.0 0.0 collective-permute-done.2.far_s
  27.1 5.0 %shard_map.78 = (bf16[256,1408]{1,0:T(8,128)(2,1)S(1)}, bf16[256,2304]{1,0:T(8,128)(2,1)S(1)}) custom-call(s32[1]{0:T(128)} %bitcast.par, bf16[1536,2304]{1,0:T(8,128)(2,1)S(1)} %get-tuple-element.18.dense, bf16[1536,256]{1,0:T(8,128)(2,1)S(1)} %shard_map.75.p_s, bf16[1536,256]{1,0:T(8,128)(2,1)S(1)} %get-tuple-element.20.p_own, ...), custom_call_target="tpu_custom_call", output_to_operand_aliasing={{1}: (6, {})} | custom-call | flops 4831838208 | bytes 11206660 | tf_op jit(solution)/shard_map/pallas_call | solution.py:25
  32.0 3.7 %collective-permute-start.6 = (bf16[256,1408]{1,0:T(8,128)(2,1)S(1)}, bf16[256,1408]{1,0:T(8,128)(2,1)S(1)}, u32[]{:S(2)}, u32[]{:S(2)}) collective-permute-start(bf16[256,1408]{1,0:T(8,128)(2,1)S(1)} %get-tuple-element.30), channel_id=1, source_target_pairs={{2,1},{4,3},{6,5},{8,7},{10,9},{12,11},{14,13},{16,15},{18,17},{20... | collective-permute-start | bytes 2162696 | tf_op jit(solution)/shard_map/ppermute | solution.py:258
  35.7 1.3 %collective-permute-start.5 = (bf16[256,1408]{1,0:T(8,128)(2,1)S(1)}, bf16[256,1408]{1,0:T(8,128)(2,1)S(1)}, u32[]{:S(2)}, u32[]{:S(2)}) collective-permute-start(bf16[256,1408]{1,0:T(8,128)(2,1)S(1)} %get-tuple-element.29), channel_id=1, source_target_pairs={{1,2},{3,4},{5,6},{7,8},{9,10},{11,12},{13,14},{15,16},{17,18},{19... | collective-permute-start | bytes 2162696 | tf_op jit(solution)/shard_map/ppermute | solution.py:258
  37.0 3.2 %shard_map.79 = (bf16[256,2304]{1,0:T(8,128)(2,1)S(1)}, f32[256,768]{1,0:T(8,128)S(1)}, f32[256,768]{1,0:T(8,128)S(1)}) custom-call(bf16[1536,2304]{1,0:T(8,128)(2,1)S(1)} %get-tuple-element.18.dense, bf16[1536,256]{1,0:T(8,128)(2,1)S(1)} %shard_map.75.p_s, bf16[1536,256]{1,0:T(8,128)(2,1)S(1)} %get-tuple-element.20.p_own, ...), custom_call_target="tpu_custom_call" | custom-call | flops 2415919104 | bytes 10616832 | tf_op jit(solution)/shard_map/pallas_call | solution.py:25
  40.2 0.0 collective-permute-done.3.far_x
  40.3 0.6 %shard_map.80 = bf16[256,1280]{1,0:T(8,128)(2,1)S(1)} custom-call(f32[256,768]{1,0:T(8,128)S(1)} %get-tuple-element.27.gal, bf16[256,2304]{1,0:T(8,128)(2,1)S(1)} %get-tuple-element.28.y, bf16[384,768]{1,0:T(8,128)(2,1)S(1)} %collective-permute-done.2.far_s, bf16[384,768]{1,0:T(8,128)(2,1)S(1)} %collective-permute-done.3.far_x), custom_call_target="tpu_custom_call" | custom-call | flops 301989888 | bytes 3145728 | tf_op jit(solution)/shard_map/pallas_call | solution.py:25
  40.8 0.1 collective-permute-start.4
  40.9 2.1 %collective-permute-done.4.from_s = bf16[256,1280]{1,0:T(8,128)(2,1)S(1)} collective-permute-done((bf16[256,1280]{1,0:T(8,128)(2,1)S(1)}, bf16[256,1280]{1,0:T(8,128)(2,1)S(1)}, u32[]{:S(2)}, u32[]{:S(2)}) %collective-permute-start.4) | collective-permute-done | bytes 655392 | tf_op jit(solution)/shard_map/ppermute | solution.py:258
  43.0 0.6 %shard_map.81.mine = f32[256,1792]{1,0:T(8,128)S(1)} custom-call(f32[256,768]{1,0:T(8,128)S(1)} %get-tuple-element.25.gal, bf16[256,2304]{1,0:T(8,128)(2,1)S(1)} %get-tuple-element.24.y_own.y, bf16[384,768]{1,0:T(8,128)(2,1)S(1)} %collective-permute-done.2.far_s, bf16[384,768]{1,0:T(8,128)(2,1)S(1)} %collective-permute-done.3.far_x, ...), custom_call_target="tpu_custom_call" | custom-call | flops 301989888 | bytes 3801088 | tf_op jit(solution)/shard_map/pallas_call | solution.py:25
  43.6 0.9 %collective-permute-done.6.from_even = bf16[256,1408]{1,0:T(8,128)(2,1)S(1)} collective-permute-done((bf16[256,1408]{1,0:T(8,128)(2,1)S(1)}, bf16[256,1408]{1,0:T(8,128)(2,1)S(1)}, u32[]{:S(2)}, u32[]{:S(2)}) %collective-permute-start.6) | collective-permute-done | bytes 720928 | tf_op jit(solution)/shard_map/ppermute | solution.py:258
  44.5 8.1 %collective-permute-done.5.from_odd = bf16[256,1408]{1,0:T(8,128)(2,1)S(1)} collective-permute-done((bf16[256,1408]{1,0:T(8,128)(2,1)S(1)}, bf16[256,1408]{1,0:T(8,128)(2,1)S(1)}, u32[]{:S(2)}, u32[]{:S(2)}) %collective-permute-start.5) | collective-permute-done | bytes 720928 | tf_op jit(solution)/shard_map/ppermute | solution.py:258
  52.5 1.2 %shard_map.82 = bf16[256,1792]{1,0:T(8,128)(2,1)} custom-call(s32[1]{0:T(128)} %bitcast.par, f32[256,1792]{1,0:T(8,128)S(1)} %shard_map.81.mine, bf16[384,768]{1,0:T(8,128)(2,1)S(1)} %get-tuple-element.26.sent_x, bf16[256,1408]{1,0:T(8,128)(2,1)S(1)} %collective-permute-done.5.from_odd, bf16[256,1408]{1,0:T(8,128)(2,1)S(1)} %collective-permute-done.6.from_even), custom_call_target="tpu_custom_call" | custom-call | flops 150994944 | bytes 3866628 | tf_op jit(solution)/shard_map/pallas_call | solution.py:25
  (1 shorter events, 0.0 us)
Async XLA Ops:
  1.0 16.1 %collective-permute-start = (bf16[1568,128]{1,0:T(8,128)(2,1)S(1)}, bf16[1568,128]{1,0:T(8,128)(2,1)S(1)}, u32[]{:S(2)}, u32[]{:S(2)}) collective-permute-start(bf16[1568,128]{1,0:T(8,128)(2,1)S(1)} %shard_map.73.pay), channel_id=1, source_target_pairs={{0,1},{1,0},{2,3},{3,2},{4,5},{5,4},{6,7},{7,6},{8,9},{9,8},{10,11... | collective-permute-start | bytes 1204232 | tf_op jit(solution)/shard_map/ppermute | solution.py:258
  1.1 17.8 %collective-permute-start.1 = (bf16[1568,128]{1,0:T(8,128)(2,1)S(1)}, bf16[1568,128]{1,0:T(8,128)(2,1)S(1)}, u32[]{:S(2)}, u32[]{:S(2)}) collective-permute-start(bf16[1568,128]{1,0:T(8,128)(2,1)S(1)} %shard_map.73.pay), channel_id=1, source_target_pairs={{1,2},{3,4},{5,6},{7,8},{9,10},{11,12},{13,14},{15,16},{17,18},{19... | collective-permute-start | bytes 1204232 | tf_op jit(solution)/shard_map/ppermute | solution.py:258
  12.4 4.8 %copy-start = (s32[1,2,3]{2,1,0:T(2,128)S(1)}, s32[1,2,3]{2,1,0:T(2,128)}, u32[]{:S(2)}) copy-start(s32[1,2,3]{2,1,0:T(2,128)} %ghost.3) | copy-start | bytes 76
  20.8 6.3 %collective-permute-start.2 = (bf16[384,768]{1,0:T(8,128)(2,1)S(1)}, bf16[384,768]{1,0:T(8,128)(2,1)S(1)}, u32[]{:S(2)}, u32[]{:S(2)}) collective-permute-start(bf16[384,768]{1,0:T(8,128)(2,1)S(1)} %get-tuple-element.22), channel_id=1, source_target_pairs={{0,1},{1,0},{2,3},{3,2},{4,5},{5,4},{6,7},{7,6},{8,9},{9,8},{10,11... | collective-permute-start | bytes 1769480 | tf_op jit(solution)/shard_map/ppermute | solution.py:258
  20.9 19.4 %collective-permute-start.3 = (bf16[384,768]{1,0:T(8,128)(2,1)S(1)}, bf16[384,768]{1,0:T(8,128)(2,1)S(1)}, u32[]{:S(2)}, u32[]{:S(2)}) collective-permute-start(bf16[384,768]{1,0:T(8,128)(2,1)S(1)} %get-tuple-element.26.sent_x), channel_id=1, source_target_pairs={{1,2},{3,4},{5,6},{7,8},{9,10},{11,12},{13,14},{15,16},{17,18},{19... | collective-permute-start | bytes 1769480 | tf_op jit(solution)/shard_map/ppermute | solution.py:258
  32.0 12.4 %collective-permute-start.6 = (bf16[256,1408]{1,0:T(8,128)(2,1)S(1)}, bf16[256,1408]{1,0:T(8,128)(2,1)S(1)}, u32[]{:S(2)}, u32[]{:S(2)}) collective-permute-start(bf16[256,1408]{1,0:T(8,128)(2,1)S(1)} %get-tuple-element.30), channel_id=1, source_target_pairs={{2,1},{4,3},{6,5},{8,7},{10,9},{12,11},{14,13},{16,15},{18,17},{20... | collective-permute-start | bytes 2162696 | tf_op jit(solution)/shard_map/ppermute | solution.py:258
  35.7 16.8 %collective-permute-start.5 = (bf16[256,1408]{1,0:T(8,128)(2,1)S(1)}, bf16[256,1408]{1,0:T(8,128)(2,1)S(1)}, u32[]{:S(2)}, u32[]{:S(2)}) collective-permute-start(bf16[256,1408]{1,0:T(8,128)(2,1)S(1)} %get-tuple-element.29), channel_id=1, source_target_pairs={{1,2},{3,4},{5,6},{7,8},{9,10},{11,12},{13,14},{15,16},{17,18},{19... | collective-permute-start | bytes 2162696 | tf_op jit(solution)/shard_map/ppermute | solution.py:258
  40.8 2.2 %collective-permute-start.4 = (bf16[256,1280]{1,0:T(8,128)(2,1)S(1)}, bf16[256,1280]{1,0:T(8,128)(2,1)S(1)}, u32[]{:S(2)}, u32[]{:S(2)}) collective-permute-start(bf16[256,1280]{1,0:T(8,128)(2,1)S(1)} %shard_map.80), channel_id=1, source_target_pairs={{0,1},{1,0},{2,3},{3,2},{4,5},{5,4},{6,7},{7,6},{8,9},{9,8},{10,11... | collective-permute-start | bytes 1966088 | tf_op jit(solution)/shard_map/ppermute | solution.py:258

commit v5 on v4

--- a/solution.py
+++ b/solution.py
@@ -161,24 +161,24 @@
             out[to, 2 * w :] = p_x[at, :]
 
 
-def cross_kernel(parity, r, b, w, par, dense, p_s, p_own, p_x, far_s, *refs):
-    out, y_own, y, flipped = refs[-4:]
+def cross_kernel(parity, r, b, w, par, dense, p_s, p_own, p_x, *refs):
+    y, gal, flipped = refs[-3:]
 
     @pl.when(par[0] == parity)
     def _():
-        flip(r, b, p_x, flipped)
-        y[...] = dot(flipped[...], dense[...]).astype(BF16)
-        inside = y[:, : r * b]
-        own = r * b
-        span = far_s.shape[0]
+        part_rows(r, b, w, dense, p_x, (p_s, p_own, p_x), y, gal, flipped)
+
+
+def outer_kernel(parity, w, span, par, gal, y, far_s, out):
+    @pl.when(par[0] == parity)
+    def _():
+        own = y.shape[1] - 2 * span
         by_s = dot(y[:, own : own + span], far_s[...])
         out[:, :w] = by_s[:, 2 * w :].astype(BF16)
-        out[:, w : 2 * w] = (dot(inside, p_s[...]) + by_s[:, w : 2 * w]).astype(BF16)
-        out[:, 2 * w : 3 * w] = (dot(inside, p_own[...]) + by_s[:, :w]).astype(BF16)
-        out[:, 3 * w : 4 * w] = dot(inside, p_x[...]).astype(BF16)
+        out[:, w : 2 * w] = (gal[:, :w] + by_s[:, w : 2 * w]).astype(BF16)
+        out[:, 2 * w : 3 * w] = (gal[:, w : 2 * w] + by_s[:, :w]).astype(BF16)
+        out[:, 3 * w : 4 * w] = gal[:, 2 * w :].astype(BF16)
         out[:, 4 * w :] = y[:, own + span :]
-        flip(r, b, p_own, flipped)
-        y_own[...] = dot(flipped[...], dense[...]).astype(BF16)
 
 
 def flip(r, b, p, flipped):
@@ -194,11 +194,10 @@
         gal[:, d * w : (d + 1) * w] = dot(y[:, : r * b], other[...])
 
 
-def rest_kernel(r, b, w, dense, p_s, p_own, p_x, y_own, y_s, gal_s, gal_own, flipped):
+def rest_kernel(r, b, w, dense, p_s, p_own, p_x, y_s, gal_s, y_own, gal_own, flipped, flipped_own):
     parts = (p_s, p_own, p_x)
-    for d, other in enumerate(parts):
-        gal_own[:, d * w : (d + 1) * w] = dot(y_own[:, : r * b], other[...])
     part_rows(r, b, w, dense, p_s, parts, y_s, gal_s, flipped)
+    part_rows(r, b, w, dense, p_own, parts, y_own, gal_own, flipped_own)
 
 
 def galerkin_rows(w, span, gal, y, far_s, far_x):
@@ -306,24 +305,30 @@
     )
     far_x = swap(out_x, up + down)
     far_s = swap(out_s, chip)
-    shapes = [((w, 4 * w + span), BF16), ((w, total), BF16)]
-    scratch = [VMEM((w, total), BF16), VMEM((w, r * b), BF16)]
-    flops = 2 * r * b * r * b * 4 * w
-    ready = (par, dense, p_s, p_own, p_x, far_s)
-    sum_odd, y_own = call(
-        functools.partial(cross_kernel, 1, r, b, w), ready, "svvvvv",
+    shapes = [((w, total), BF16), ((w, 3 * w), F32)]
+    scratch = [VMEM((w, r * b), BF16)]
+    flops = 2 * r * b * r * b * 2 * w
+    ready = (par, dense, p_s, p_own, p_x)
+
+    def outer(parity, gal, y):
+        return call(
+            functools.partial(outer_kernel, parity, w, span), (par, gal, y, far_s), "svvv",
+            [((w, 4 * w + span), BF16)], flops=2 * w * span * 3 * w, limit=16 << 20,
+        )[0]
+
+    y_x, gal_x = call(
+        functools.partial(cross_kernel, 1, r, b, w), ready, "svvvv",
         shapes, scratch=scratch, flops=flops, limit=24 << 20,
     )
-    from_odd = swap(sum_odd, up)
-    sum_even, y_own = call(
-        functools.partial(cross_kernel, 0, r, b, w), ready + (y_own,), "svvvvvv",
-        shapes, scratch=scratch, flops=flops, limit=24 << 20, aliases={6: 1},
-    )
-    from_even = swap(sum_even, down)
-    y_s, gal_s, gal_own = call(
-        functools.partial(rest_kernel, r, b, w), (dense, p_s, p_own, p_x, y_own), "vvvvv",
-        [((w, total), BF16), ((w, 3 * w), F32), ((w, 3 * w), F32)], scratch=[VMEM((w, r * b), BF16)],
-        flops=2 * r * b * r * b * 2 * w, limit=24 << 20,
+    from_odd = swap(outer(1, gal_x, y_x), up)
+    y_x, gal_x = call(
+        functools.partial(cross_kernel, 0, r, b, w), ready + (y_x, gal_x), "svvvvvv",
+        shapes, scratch=scratch, flops=flops, limit=24 << 20, aliases={5: 0, 6: 1},
+    )
+    from_even = swap(outer(0, gal_x, y_x), down)
+    y_s, gal_s, y_own, gal_own = call(
+        functools.partial(rest_kernel, r, b, w), (dense, p_s, p_own, p_x), "vvvv",
+        shapes + shapes, scratch=scratch + scratch, flops=2 * flops, limit=24 << 20,
     )
     (sum_s,) = call(
         functools.partial(chip_kernel, w, span), (gal_s, y_s, far_s, far_x), "vvvv",

time: 54.1 us -> 47.5 us (0.88)
  waiting for transfers between devices: 11 us -> 2.19 us
  starting transfers between devices: 22 us -> 24 us
    ppermute x7, waiting for transfers between devices: 11 us -> 2.19 us  [swap(): return lax.ppermute(x, AXES, route)]
    ppermute x7, starting transfers between devices: 22 us -> 24 us  [swap(): return lax.ppermute(x, AXES, route)]
    pallas_call x10 -> x12, Pallas kernels: 19.9 us -> 19.9 us  [call(): pl.pallas_call(kernel, out_shape=[jax.ShapeDtypeStruct(*o) for o in outs]...]
  transfers between devices with their start and end apart: 7 -> 7, of which waited for: 3 -> 2; matrix products, arithmetic and copies ran while one was open for 0% -> 0% of each run, Pallas kernels for 29% -> 34%
where the time goes in v5:
time: 47.5 us; the launch traced here: 47.1 us
  starting transfers between devices  24 us (51%)
  Pallas kernels  19.9 us (42%)
  waiting for transfers between devices  2.19 us (5%)
  between operations  0.99 us (2%)
    ppermute x7, starting transfers between devices, swap(): return lax.ppermute(x, AXES, route)  24 us
    pallas_call x12, Pallas kernels, call(): pl.pallas_call(kernel, out_shape=[jax.ShapeDtypeStruct(*o) for o in outs]...  19.9 us
    ppermute x7, waiting for transfers between devices, swap(): return lax.ppermute(x, AXES, route)  2.19 us
  transfers between devices with their start and end apart: 7, of which 2 were waited for; matrix products, arithmetic and copies ran while one was open for 0% of the time, Pallas kernels for 34%

profile of v5, /device:TPU:6, one launch (start us, length us, event | category | flops | bytes accessed | tf_op | source)
XLA Modules:
  0.0 47.1 jit_solution(9542465898618767948)
XLA Ops:
  0.0 1.0 %shard_map.73.pay = bf16[1568,128]{1,0:T(8,128)(2,1)S(1)} custom-call(s32[12]{0:T(128)} %agg_hbm.3, s32[1,2,3]{2,1,0:T(2,128)} %ghost.3, bf16[1536,128]{1,0:T(8,128)(2,1)} %bitcast.4), custom_call_target="tpu_custom_call" | custom-call | flops 1 | bytes 393288 | tf_op jit(solution)/shard_map/pallas_call | solution.py:25
  1.0 0.1 collective-permute-start
  1.1 10.6 %collective-permute-start.1 = (bf16[1568,128]{1,0:T(8,128)(2,1)S(1)}, bf16[1568,128]{1,0:T(8,128)(2,1)S(1)}, u32[]{:S(2)}, u32[]{:S(2)}) collective-permute-start(bf16[1568,128]{1,0:T(8,128)(2,1)S(1)} %shard_map.73.pay), channel_id=1, source_target_pairs={{1,2},{3,4},{5,6},{7,8},{9,10},{11,12},{13,14},{15,16},{17,18},{19... | collective-permute-start | bytes 1204232 | tf_op jit(solution)/shard_map/ppermute | solution.py:257
  12.4 0.0 copy-start
  12.4 4.8 %shard_map.74 = (bf16[1536,2304]{1,0:T(8,128)(2,1)S(1)}, bf16[1536,128]{1,0:T(8,128)(2,1)S(1)}, bf16[1536,256]{1,0:T(8,128)(2,1)S(1)}) custom-call(s32[1]{0:T(128)} %bitcast.par, f32[1]{0:T(128)S(6)} %copy.12.damp, s32[12]{0:T(128)} %agg_hbm.3, s32[12,9]{1,0:T(8,128)} %cols_hbm.1, bf16[12,9,128,128]{3,2,1,0:T(8,128)(2,1)} %vals_hbm.1, ...), custom_call_target="tpu_custom_call" | custom-call | flops 1207959552 | bytes 4334056 | tf_op jit(solution)/shard_map/pallas_call | solution.py:25
  17.1 0.0 collective-permute-done.pay.pay_s
  17.2 0.0 copy-done
  17.2 1.8 %shard_map.75.p_s = bf16[1536,256]{1,0:T(8,128)(2,1)S(1)} custom-call(s32[1,2,3]{2,1,0:T(2,128)S(1)} %copy-done, s32[1]{0:T(128)} %bitcast.par, f32[1]{0:T(128)S(6)} %copy.12.damp, bf16[1536,2304]{1,0:T(8,128)(2,1)S(1)} %get-tuple-element.19.dense, bf16[1536,128]{1,0:T(8,128)(2,1)S(1)} %get-tuple-element.20.inv, ...), custom_call_target="tpu_custom_call" | custom-call | flops 301989888 | bytes 7872544 | tf_op jit(solution)/shard_map/pallas_call | solution.py:25
  18.9 0.0 collective-permute-done.1.pay_x
  19.0 1.8 %shard_map.76 = (bf16[1536,256]{1,0:T(8,128)(2,1)S(1)}, bf16[384,768]{1,0:T(8,128)(2,1)S(1)}, bf16[384,768]{1,0:T(8,128)(2,1)S(1)}) custom-call(s32[1,2,3]{2,1,0:T(2,128)S(1)} %copy-done, s32[1]{0:T(128)} %bitcast.par, f32[1]{0:T(128)S(6)} %copy.12.damp, bf16[1536,2304]{1,0:T(8,128)(2,1)S(1)} %get-tuple-element.19.dense, ...), custom_call_target="tpu_custom_call" | custom-call | flops 301989888 | bytes 9846816 | tf_op jit(solution)/shard_map/pallas_call | solution.py:25
  20.8 0.1 collective-permute-start.2
  20.9 6.1 %collective-permute-start.3 = (bf16[384,768]{1,0:T(8,128)(2,1)S(1)}, bf16[384,768]{1,0:T(8,128)(2,1)S(1)}, u32[]{:S(2)}, u32[]{:S(2)}) collective-permute-start(bf16[384,768]{1,0:T(8,128)(2,1)S(1)} %get-tuple-element.26.sent_x), channel_id=1, source_target_pairs={{1,2},{3,4},{5,6},{7,8},{9,10},{11,12},{13,14},{15,16},{17,18},{19... | collective-permute-start | bytes 1769480 | tf_op jit(solution)/shard_map/ppermute | solution.py:257
  27.0 0.0 collective-permute-done.2.far_s
  27.1 1.3 %collective-permute-start.5 = (bf16[256,1408]{1,0:T(8,128)(2,1)S(1)}, bf16[256,1408]{1,0:T(8,128)(2,1)S(1)}, u32[]{:S(2)}, u32[]{:S(2)}) collective-permute-start(bf16[256,1408]{1,0:T(8,128)(2,1)S(1)} %shard_map.81), channel_id=1, source_target_pairs={{1,2},{3,4},{5,6},{7,8},{9,10},{11,12},{13,14},{15,16},{17,18},{19... | collective-permute-start | bytes 2162696 | tf_op jit(solution)/shard_map/ppermute | solution.py:257
  28.4 2.7 %shard_map.82 = (bf16[256,2304]{1,0:T(8,128)(2,1)S(1)}, f32[256,768]{1,0:T(8,128)S(1)}) custom-call(s32[1]{0:T(128)} %bitcast.par, bf16[1536,2304]{1,0:T(8,128)(2,1)S(1)} %get-tuple-element.19.dense, bf16[1536,256]{1,0:T(8,128)(2,1)S(1)} %shard_map.75.p_s, ...), custom_call_target="tpu_custom_call", output_to_operand_aliasing={{0}: (5, {}), {1}: (6, {})} | custom-call | flops 2415919104 | bytes 11403268 | tf_op jit(solution)/shard_map/pallas_call | solution.py:25
  31.0 0.4 shard_map.83
  31.4 5.7 %collective-permute-start.6 = (bf16[256,1408]{1,0:T(8,128)(2,1)S(1)}, bf16[256,1408]{1,0:T(8,128)(2,1)S(1)}, u32[]{:S(2)}, u32[]{:S(2)}) collective-permute-start(bf16[256,1408]{1,0:T(8,128)(2,1)S(1)} %shard_map.83), channel_id=1, source_target_pairs={{2,1},{4,3},{6,5},{8,7},{10,9},{12,11},{14,13},{16,15},{18,17},{20... | collective-permute-start | bytes 2162696 | tf_op jit(solution)/shard_map/ppermute | solution.py:257
  37.2 5.1 %shard_map.77 = (bf16[256,2304]{1,0:T(8,128)(2,1)S(1)}, f32[256,768]{1,0:T(8,128)S(1)}, bf16[256,2304]{1,0:T(8,128)(2,1)S(1)}, f32[256,768]{1,0:T(8,128)S(1)}) custom-call(bf16[1536,2304]{1,0:T(8,128)(2,1)S(1)} %get-tuple-element.19.dense, bf16[1536,256]{1,0:T(8,128)(2,1)S(1)} %shard_map.75.p_s, bf16[1536,256]{1,0:T(8,128)(2,1)S(1)} %get-tuple-element.21.p_own, ...), custom_call_target="tpu_custom_call" | custom-call | flops 4831838208 | bytes 9437184 | tf_op jit(solution)/shard_map/pallas_call | solution.py:25
  42.3 0.0 collective-permute-done.3.far_x
  42.3 0.6 %shard_map.78 = bf16[256,1280]{1,0:T(8,128)(2,1)S(1)} custom-call(f32[256,768]{1,0:T(8,128)S(1)} %get-tuple-element.27.gal, bf16[256,2304]{1,0:T(8,128)(2,1)S(1)} %get-tuple-element.28.y, bf16[384,768]{1,0:T(8,128)(2,1)S(1)} %collective-permute-done.2.far_s, bf16[384,768]{1,0:T(8,128)(2,1)S(1)} %collective-permute-done.3.far_x), custom_call_target="tpu_custom_call" | custom-call | flops 301989888 | bytes 3145728 | tf_op jit(solution)/shard_map/pallas_call | solution.py:25
  42.9 0.1 collective-permute-start.4
  43.0 2.1 %collective-permute-done.4.from_s = bf16[256,1280]{1,0:T(8,128)(2,1)S(1)} collective-permute-done((bf16[256,1280]{1,0:T(8,128)(2,1)S(1)}, bf16[256,1280]{1,0:T(8,128)(2,1)S(1)}, u32[]{:S(2)}, u32[]{:S(2)}) %collective-permute-start.4) | collective-permute-done | bytes 655392 | tf_op jit(solution)/shard_map/ppermute | solution.py:257
  45.1 0.6 %shard_map.79.mine = f32[256,1792]{1,0:T(8,128)S(1)} custom-call(f32[256,768]{1,0:T(8,128)S(1)} %get-tuple-element.23.gal, bf16[256,2304]{1,0:T(8,128)(2,1)S(1)} %get-tuple-element.24.y, bf16[384,768]{1,0:T(8,128)(2,1)S(1)} %collective-permute-done.2.far_s, bf16[384,768]{1,0:T(8,128)(2,1)S(1)} %collective-permute-done.3.far_x, ...), custom_call_target="tpu_custom_call" | custom-call | flops 301989888 | bytes 3801088 | tf_op jit(solution)/shard_map/pallas_call | solution.py:25
  45.6 0.1 collective-permute-done.6.from_even
  45.7 0.0 collective-permute-done.5.from_odd
  45.7 1.2 %shard_map.84 = bf16[256,1792]{1,0:T(8,128)(2,1)} custom-call(s32[1]{0:T(128)} %bitcast.par, f32[256,1792]{1,0:T(8,128)S(1)} %shard_map.79.mine, bf16[384,768]{1,0:T(8,128)(2,1)S(1)} %get-tuple-element.26.sent_x, bf16[256,1408]{1,0:T(8,128)(2,1)S(1)} %collective-permute-done.5.from_odd, bf16[256,1408]{1,0:T(8,128)(2,1)S(1)} %collective-permute-done.6.from_even), custom_call_target="tpu_custom_call" | custom-call | flops 150994944 | bytes 3866628 | tf_op jit(solution)/shard_map/pallas_call | solution.py:25
  (2 shorter events, 0.0 us)
Async XLA Ops:
  1.0 16.1 %collective-permute-start = (bf16[1568,128]{1,0:T(8,128)(2,1)S(1)}, bf16[1568,128]{1,0:T(8,128)(2,1)S(1)}, u32[]{:S(2)}, u32[]{:S(2)}) collective-permute-start(bf16[1568,128]{1,0:T(8,128)(2,1)S(1)} %shard_map.73.pay), channel_id=1, source_target_pairs={{0,1},{1,0},{2,3},{3,2},{4,5},{5,4},{6,7},{7,6},{8,9},{9,8},{10,11... | collective-permute-start | bytes 1204232 | tf_op jit(solution)/shard_map/ppermute | solution.py:257
  1.1 17.8 %collective-permute-start.1 = (bf16[1568,128]{1,0:T(8,128)(2,1)S(1)}, bf16[1568,128]{1,0:T(8,128)(2,1)S(1)}, u32[]{:S(2)}, u32[]{:S(2)}) collective-permute-start(bf16[1568,128]{1,0:T(8,128)(2,1)S(1)} %shard_map.73.pay), channel_id=1, source_target_pairs={{1,2},{3,4},{5,6},{7,8},{9,10},{11,12},{13,14},{15,16},{17,18},{19... | collective-permute-start | bytes 1204232 | tf_op jit(solution)/shard_map/ppermute | solution.py:257
  12.4 4.8 %copy-start = (s32[1,2,3]{2,1,0:T(2,128)S(1)}, s32[1,2,3]{2,1,0:T(2,128)}, u32[]{:S(2)}) copy-start(s32[1,2,3]{2,1,0:T(2,128)} %ghost.3) | copy-start | bytes 76
  20.8 6.3 %collective-permute-start.2 = (bf16[384,768]{1,0:T(8,128)(2,1)S(1)}, bf16[384,768]{1,0:T(8,128)(2,1)S(1)}, u32[]{:S(2)}, u32[]{:S(2)}) collective-permute-start(bf16[384,768]{1,0:T(8,128)(2,1)S(1)} %get-tuple-element.25), channel_id=1, source_target_pairs={{0,1},{1,0},{2,3},{3,2},{4,5},{5,4},{6,7},{7,6},{8,9},{9,8},{10,11... | collective-permute-start | bytes 1769480 | tf_op jit(solution)/shard_map/ppermute | solution.py:257
  20.9 21.4 %collective-permute-start.3 = (bf16[384,768]{1,0:T(8,128)(2,1)S(1)}, bf16[384,768]{1,0:T(8,128)(2,1)S(1)}, u32[]{:S(2)}, u32[]{:S(2)}) collective-permute-start(bf16[384,768]{1,0:T(8,128)(2,1)S(1)} %get-tuple-element.26.sent_x), channel_id=1, source_target_pairs={{1,2},{3,4},{5,6},{7,8},{9,10},{11,12},{13,14},{15,16},{17,18},{19... | collective-permute-start | bytes 1769480 | tf_op jit(solution)/shard_map/ppermute | solution.py:257
  27.1 18.7 %collective-permute-start.5 = (bf16[256,1408]{1,0:T(8,128)(2,1)S(1)}, bf16[256,1408]{1,0:T(8,128)(2,1)S(1)}, u32[]{:S(2)}, u32[]{:S(2)}) collective-permute-start(bf16[256,1408]{1,0:T(8,128)(2,1)S(1)} %shard_map.81), channel_id=1, source_target_pairs={{1,2},{3,4},{5,6},{7,8},{9,10},{11,12},{13,14},{15,16},{17,18},{19... | collective-permute-start | bytes 2162696 | tf_op jit(solution)/shard_map/ppermute | solution.py:257
  31.4 14.3 %collective-permute-start.6 = (bf16[256,1408]{1,0:T(8,128)(2,1)S(1)}, bf16[256,1408]{1,0:T(8,128)(2,1)S(1)}, u32[]{:S(2)}, u32[]{:S(2)}) collective-permute-start(bf16[256,1408]{1,0:T(8,128)(2,1)S(1)} %shard_map.83), channel_id=1, source_target_pairs={{2,1},{4,3},{6,5},{8,7},{10,9},{12,11},{14,13},{16,15},{18,17},{20... | collective-permute-start | bytes 2162696 | tf_op jit(solution)/shard_map/ppermute | solution.py:257
  42.9 2.2 %collective-permute-start.4 = (bf16[256,1280]{1,0:T(8,128)(2,1)S(1)}, bf16[256,1280]{1,0:T(8,128)(2,1)S(1)}, u32[]{:S(2)}, u32[]{:S(2)}) collective-permute-start(bf16[256,1280]{1,0:T(8,128)(2,1)S(1)} %shard_map.78), channel_id=1, source_target_pairs={{0,1},{1,0},{2,3},{3,2},{4,5},{5,4},{6,7},{7,6},{8,9},{9,8},{10,11... | collective-permute-start | bytes 1966088 | tf_op jit(solution)/shard_map/ppermute | solution.py:257

commit v6 on v5

--- a/solution.py
+++ b/solution.py
@@ -63,16 +63,18 @@
     copies[2].wait()
 
 
-def smooth(r, b, dense, cols, placed, inv, damp, target, base=None):
+def smooth(r, b, dense, cols, placed, inv, damp, half, target, base=None):
     step = 4
     for t in range(r // step):
-        half = dot(dense[t * step * b : (t + 1) * step * b, cols], placed).astype(BF16)
-        for q in range(step):
-            at = slice((t * step + q) * b, (t * step + q + 1) * b)
-            value = -damp[0] * dot(inv[at, :], half[q * b : (q + 1) * b, :])
-            if base is not None:
-                value = base[at, :].astype(F32) + value
-            target[at, :] = value.astype(BF16)
+        at = slice(t * step * b, (t + 1) * step * b)
+        half[at, :] = dot(dense[at, cols], placed[...]).astype(BF16)
+    factor = -damp[0:1, :]
+    for j in range(r):
+        at = slice(j * b, (j + 1) * b)
+        value = factor * dot(inv[at, :], half[at, :])
+        if base is not None:
+            value = base[at, :].astype(F32) + value
+        target[at, :] = value.astype(BF16)
 
 
 def place_ghosts(r, b, s, ghost, mine, pay, meta, placed):
@@ -94,18 +96,16 @@
 
 
 def own_kernel(
-    r, k, b, s, par, damp, agg_hbm, cols_hbm, vals_hbm, inv_hbm, pay, dense, inv, p_own, agg, cols, vals, placed, sems
+    r, k, b, s, index, damp_in, agg_hbm, cols_hbm, inv_hbm, vals_hbm, pay,
+    dense, inv, p_own, damp, agg, cols, vals, placed, half, sems,
 ):
     def fetch(j):
-        return pltpu.make_async_copy(vals_hbm.at[j], vals.at[j], sems.at[j])
-
-    others = [
-        pltpu.make_async_copy(cols_hbm, cols, sems.at[r]),
-        pltpu.make_async_copy(agg_hbm, agg, sems.at[r + 1]),
-        pltpu.make_async_copy(inv_hbm, inv, sems.at[r + 2]),
-    ]
-    others[0].start()
-    others[1].start()
+        return pltpu.make_async_copy(vals_hbm.at[j], vals.at[j], sems.at[3 + j])
+
+    pairs = ((cols_hbm, cols), (agg_hbm, agg), (inv_hbm, inv))
+    others = [pltpu.make_async_copy(src, dst, sems.at[i]) for i, (src, dst) in enumerate(pairs)]
+    for copy in others[:2]:
+        copy.start()
     for j in range(r):
         fetch(j).start()
     others[2].start()
@@ -115,8 +115,9 @@
         return carry
 
     lax.fori_loop(0, r, clear, 0)
-    others[0].wait()
-    others[1].wait()
+    for copy in others[:2]:
+        copy.wait()
+    damp[...] = jnp.full(damp.shape, damp_in[0], F32)
     zero = jnp.zeros((b, b), BF16)
     for j in range(r):
         own = slice(j * b, (j + 1) * b)
@@ -124,7 +125,7 @@
         here = agg[j]
         for c in range(CA):
             placed[own, c * b : (c + 1) * b] = jnp.where(here == c, block, zero)
-    odd = par[0]
+    odd = (index[0] & 1)
     left = s * (1 - odd)
 
     def row(j, carry):
@@ -138,20 +139,20 @@
 
     lax.fori_loop(0, r, row, 0)
     others[2].wait()
-    smooth(r, b, dense, slice(0, r * b), placed[...], inv, damp, p_own, placed)
-
-
-def near_kernel(r, b, s, ghost, par, damp, dense, inv, pay, p_s, meta, placed):
-    place_ghosts(r, b, s, ghost, 1 - par[0], pay, meta, placed)
-    smooth(r, b, dense, slice(r * b, (r + s) * b), placed[...], inv, damp, p_s)
-
-
-def far_kernel(r, b, s, w, ghost, par, damp, dense, inv, p_s, p_own, pay_s, pay_x, p_x, out_x, out_s, meta, near, placed):
-    odd = par[0]
+    smooth(r, b, dense, slice(0, r * b), placed, inv, damp, half, p_own, placed)
+
+
+def near_kernel(r, b, s, ghost, index, damp, dense, inv, pay, p_s, meta, placed, half):
+    place_ghosts(r, b, s, ghost, 1 - (index[0] & 1), pay, meta, placed)
+    smooth(r, b, dense, slice(r * b, (r + s) * b), placed, inv, damp, half, p_s)
+
+
+def far_kernel(r, b, s, w, ghost, index, damp, dense, inv, p_s, p_own, pay_s, pay_x, p_x, out_x, out_s, meta, near, placed, half):
+    odd = (index[0] & 1)
     place_ghosts(r, b, s, ghost, odd, pay_x, meta, placed)
     near[...] = pay_s[r * b :, :].astype(F32)
     wanted = (wanted_rows(r, s, 1 - odd, meta), wanted_rows(r, s, odd, near))
-    smooth(r, b, dense, slice((r + s) * b, (r + 2 * s) * b), placed[...], inv, damp, p_x)
+    smooth(r, b, dense, slice((r + s) * b, (r + 2 * s) * b), placed, inv, damp, half, p_x)
     for found, out in zip(wanted, (out_x, out_s)):
         for j in range(s):
             at = rows(found[j], b)
@@ -161,24 +162,24 @@
             out[to, 2 * w :] = p_x[at, :]
 
 
-def cross_kernel(parity, r, b, w, par, dense, p_s, p_own, p_x, *refs):
+def cross_kernel(ahead, group, r, b, w, index, dense, p_s, p_own, p_x, *refs):
     y, gal, flipped = refs[-3:]
 
-    @pl.when(par[0] == parity)
+    opens = (lax.rem(index[0], group) == 0) & (index[0] > 0)
+
+    @pl.when(opens if ahead else jnp.logical_not(opens))
     def _():
         part_rows(r, b, w, dense, p_x, (p_s, p_own, p_x), y, gal, flipped)
 
 
-def outer_kernel(parity, w, span, par, gal, y, far_s, out):
-    @pl.when(par[0] == parity)
-    def _():
-        own = y.shape[1] - 2 * span
-        by_s = dot(y[:, own : own + span], far_s[...])
-        out[:, :w] = by_s[:, 2 * w :].astype(BF16)
-        out[:, w : 2 * w] = (gal[:, :w] + by_s[:, w : 2 * w]).astype(BF16)
-        out[:, 2 * w : 3 * w] = (gal[:, w : 2 * w] + by_s[:, :w]).astype(BF16)
-        out[:, 3 * w : 4 * w] = gal[:, 2 * w :].astype(BF16)
-        out[:, 4 * w :] = y[:, own + span :]
+def outer_kernel(w, span, gal, y, far_s, out):
+    own = y.shape[1] - 2 * span
+    by_s = dot(y[:, own : own + span], far_s[...])
+    out[:, :w] = by_s[:, 2 * w :].astype(BF16)
+    out[:, w : 2 * w] = (gal[:, :w] + by_s[:, w : 2 * w]).astype(BF16)
+    out[:, 2 * w : 3 * w] = (gal[:, w : 2 * w] + by_s[:, :w]).astype(BF16)
+    out[:, 3 * w : 4 * w] = gal[:, 2 * w :].astype(BF16)
+    out[:, 4 * w :] = y[:, own + span :]
 
 
 def flip(r, b, p, flipped):
@@ -227,30 +228,21 @@
         out[:, (3 - u) * w : (4 - u) * w] = total
 
 
-def final_kernel(w, par, mine, sent_x, from_odd, from_even, out_hbm, out, sems):
-    def finish(sign, from_x):
-        back = dot(from_x[:, 4 * w :], sent_x[...])
-        copies = []
-        for u in (3, 2, -3, -2, -1, 0, 1):
-            total = mine[:, (3 - u) * w : (4 - u) * w]
-            if 0 <= 3 + u < 4:
-                total = total + from_x[:, (3 + u) * w : (4 + u) * w].astype(F32)
-            if abs(u) < 2:
-                total = total + back[:, (1 - u) * w : (2 - u) * w]
-            out[u + 3, :, :] = total.astype(BF16)
-            place = out_hbm.at[:, (3 + sign * u) * w : (4 + sign * u) * w]
-            copies.append(pltpu.make_async_copy(out.at[u + 3], place, sems.at[u + 3]))
-            copies[-1].start()
-        for copy in copies:
-            copy.wait()
-
-    @pl.when(par[0] == 0)
-    def _():
-        finish(1, from_odd)
-
-    @pl.when(par[0] == 1)
-    def _():
-        finish(-1, from_even)
+def final_kernel(w, index, mine, sent_x, from_x, out_hbm, out, sems):
+    sign = 1 - 2 * (index[0] & 1)
+    back = dot(from_x[:, 4 * w :], sent_x[...])
+    copies = []
+    for u in (3, 2, -3, -2, -1, 0, 1):
+        total = mine[:, (3 - u) * w : (4 - u) * w]
+        if 0 <= 3 + u < 4:
+            total = total + from_x[:, (3 + u) * w : (4 + u) * w].astype(F32)
+        if abs(u) < 2:
+            total = total + back[:, (1 - u) * w : (2 - u) * w]
+        out[u + 3, :, :] = total.astype(BF16)
+        copies.append(pltpu.make_async_copy(out.at[u + 3], out_hbm.at[:, rows(3 + sign * u, w)], sems.at[u + 3]))
+        copies[-1].start()
+    for copy in copies:
+        copy.wait()
 
 
 def swap(x, route):
@@ -265,10 +257,11 @@
     span = s * b
     devices = lax.axis_size(AXES)
     chip = [(i, i ^ 1) for i in range(devices) if i ^ 1 < devices]
-    up = [(i, i + 1) for i in range(1, devices - 1, 2)]
-    down = [(j, i) for i, j in up]
-    _, dev = (lax.axis_index(a) for a in AXES)
-    par = (dev & 1).astype(jnp.int32).reshape(1)
+    cross = []
+    for i in range(1, devices - 1, 2):
+        cross += [(i, i + 1), (i + 1, i)]
+    index = lax.axis_index(AXES).astype(jnp.int32).reshape(1)
+    group = lax.axis_size(AXES[1])
     tent = tentative.reshape(r * b, b)
     inv = inverse_diagonal.reshape(r * b, b)
     dma = pltpu.SemaphoreType.DMA
@@ -279,53 +272,49 @@
         [((r * b + META, b), BF16)],
         scratch=[SMEM((r,), jnp.int32), SMEM((1, 2, s), jnp.int32), dma((3,))], limit=2 << 20,
     )
-    pay_x = swap(pay, up + down)
+    pay_x = swap(pay, cross)
     pay_s = swap(pay, chip)
-    dense, inv, p_own = call(
+    dense, inv, p_own, damp = call(
         functools.partial(own_kernel, r, k, b, s),
-        (par, damping, aggregate, block_columns, block_values, inv, pay), "sshhhhv",
-        [((r * b, total), BF16), ((r * b, b), BF16), ((r * b, w), BF16)],
+        (index, damping, aggregate, block_columns, inv, block_values, pay), "sshhhhv",
+        [((r * b, total), BF16), ((r * b, b), BF16), ((r * b, w), BF16), ((8, w), F32)],
         scratch=[
-            SMEM((r,), jnp.int32), SMEM((r, k), jnp.int32), VMEM((r, k, b, b), BF16), VMEM((r * b, w), BF16),
-            dma((r + 3,)),
+            SMEM((r,), jnp.int32), SMEM((r, k), jnp.int32), VMEM((r, k, b, b), BF16),
+            VMEM((r * b, w), BF16), VMEM((r * b, w), BF16), dma((r + 3,)),
         ],
         flops=2 * r * b * r * b * w, limit=24 << 20,
     )
     (p_s,) = call(
-        functools.partial(near_kernel, r, b, s), (ghost_rows, par, damping, dense, inv, pay_s), "sssvvv",
-        [((r * b, w), BF16)], scratch=[VMEM((META, b), F32), VMEM((span, w), BF16)],
+        functools.partial(near_kernel, r, b, s), (ghost_rows, index, damp, dense, inv, pay_s), "ssvvvv",
+        [((r * b, w), BF16)], scratch=[VMEM((META, b), F32), VMEM((span, w), BF16), VMEM((r * b, w), BF16)],
         flops=2 * r * b * span * w, limit=24 << 20,
     )
     p_x, out_x, out_s = call(
         functools.partial(far_kernel, r, b, s, w),
-        (ghost_rows, par, damping, dense, inv, p_s, p_own, pay_s, pay_x), "sssvvvvvv",
+        (ghost_rows, index, damp, dense, inv, p_s, p_own, pay_s, pay_x), "ssvvvvvvv",
         [((r * b, w), BF16), ((span, 3 * w), BF16), ((span, 3 * w), BF16)],
-        scratch=[VMEM((META, b), F32), VMEM((META, b), F32), VMEM((span, w), BF16)],
+        scratch=[VMEM((META, b), F32), VMEM((META, b), F32), VMEM((span, w), BF16), VMEM((r * b, w), BF16)],
         flops=2 * r * b * span * w, limit=24 << 20,
     )
-    far_x = swap(out_x, up + down)
+    far_x = swap(out_x, cross)
     far_s = swap(out_s, chip)
     shapes = [((w, total), BF16), ((w, 3 * w), F32)]
     scratch = [VMEM((w, r * b), BF16)]
     flops = 2 * r * b * r * b * 2 * w
-    ready = (par, dense, p_s, p_own, p_x)
-
-    def outer(parity, gal, y):
-        return call(
-            functools.partial(outer_kernel, parity, w, span), (par, gal, y, far_s), "svvv",
-            [((w, 4 * w + span), BF16)], flops=2 * w * span * 3 * w, limit=16 << 20,
-        )[0]
-
+    ready = (index, dense, p_s, p_own, p_x)
     y_x, gal_x = call(
-        functools.partial(cross_kernel, 1, r, b, w), ready, "svvvv",
+        functools.partial(cross_kernel, True, group, r, b, w), ready, "svvvv",
         shapes, scratch=scratch, flops=flops, limit=24 << 20,
     )
-    from_odd = swap(outer(1, gal_x, y_x), up)
     y_x, gal_x = call(
-        functools.partial(cross_kernel, 0, r, b, w), ready + (y_x, gal_x), "svvvvvv",
+        functools.partial(cross_kernel, False, group, r, b, w), ready + (y_x, gal_x), "svvvvvv",
         shapes, scratch=scratch, flops=flops, limit=24 << 20, aliases={5: 0, 6: 1},
     )
-    from_even = swap(outer(0, gal_x, y_x), down)
+    (sum_x,) = call(
+        functools.partial(outer_kernel, w, span), (gal_x, y_x, far_s), "vvv",
+        [((w, 4 * w + span), BF16)], flops=2 * w * span * 3 * w, limit=16 << 20,
+    )
+    from_x = swap(sum_x, cross)
     y_s, gal_s, y_own, gal_own = call(
         functools.partial(rest_kernel, r, b, w), (dense, p_s, p_own, p_x), "vvvv",
         shapes + shapes, scratch=scratch + scratch, flops=2 * flops, limit=24 << 20,
@@ -340,7 +329,7 @@
         [((w, 7 * w), F32)], flops=4 * w * span * 3 * w, limit=16 << 20,
     )
     (out,) = call(
-        functools.partial(final_kernel, w), (par, mine, out_x, from_odd, from_even), "svvvv",
+        functools.partial(final_kernel, w), (index, mine, out_x, from_x), "svvv",
         [((w, 7 * w), BF16)], scratch=[VMEM((7, w, w), BF16), dma((7,))],
         flops=2 * w * span * 3 * w, limit=16 << 20, out_space=pltpu.HBM,
     )

time: 47.5 us -> 48.1 us (1.013)
  waiting for transfers between devices: 2.19 us -> 7.8 us
  starting transfers between devices: 24 us -> 20.8 us
  Pallas kernels: 19.9 us -> 18.3 us
    ppermute x7 -> x6, waiting for transfers between devices: 2.19 us -> 7.8 us  [swap(): return lax.ppermute(x, AXES, route)]
    ppermute x7 -> x6, starting transfers between devices: 24 us -> 20.8 us  [swap(): return lax.ppermute(x, AXES, route)]
    pallas_call x12 -> x11, Pallas kernels: 19.9 us -> 18.3 us  [call(): pl.pallas_call(kernel, out_shape=[jax.ShapeDtypeStruct(*o) for o in outs]...]
  transfers between devices with their start and end apart: 7 -> 6, of which waited for: 2 -> 2; matrix products, arithmetic and copies ran while one was open for 0% -> 0% of each run, Pallas kernels for 34% -> 31%
where the time goes in v6:
time: 48.1 us; the launch traced here: 47.9 us
  starting transfers between devices  20.8 us (43%)
  Pallas kernels  18.3 us (38%)
  waiting for transfers between devices  7.8 us (16%)
  between operations  0.98 us (2%)
    ppermute x6, starting transfers between devices, swap(): return lax.ppermute(x, AXES, route)  20.8 us
    pallas_call x11, Pallas kernels, call(): pl.pallas_call(kernel, out_shape=[jax.ShapeDtypeStruct(*o) for o in outs]...  18.3 us
    ppermute x6, waiting for transfers between devices, swap(): return lax.ppermute(x, AXES, route)  7.8 us
  transfers between devices with their start and end apart: 6, of which 2 were waited for; matrix products, arithmetic and copies ran while one was open for 0% of the time, Pallas kernels for 31%

profile of v6, /device:TPU:6, one launch (start us, length us, event | category | flops | bytes accessed | tf_op | source)
XLA Modules:
  0.0 47.9 jit_solution(4811315495046892297)
XLA Ops:
  0.0 1.0 %shard_map.73.pay = bf16[1568,128]{1,0:T(8,128)(2,1)S(1)} custom-call(s32[12]{0:T(128)} %agg_hbm.3, s32[1,2,3]{2,1,0:T(2,128)} %ghost.3, bf16[1536,128]{1,0:T(8,128)(2,1)} %bitcast.4), custom_call_target="tpu_custom_call" | custom-call | flops 1 | bytes 393288 | tf_op jit(solution)/shard_map/pallas_call | solution.py:25
  1.0 0.1 collective-permute-start
  1.1 10.6 %collective-permute-start.1 = (bf16[1568,128]{1,0:T(8,128)(2,1)S(1)}, bf16[1568,128]{1,0:T(8,128)(2,1)S(1)}, u32[]{:S(2)}, u32[]{:S(2)}) collective-permute-start(bf16[1568,128]{1,0:T(8,128)(2,1)S(1)} %shard_map.73.pay), channel_id=1, source_target_pairs={{1,2},{2,1},{3,4},{4,3},{5,6},{6,5},{7,8},{8,7},{9,10},{10,9},{11,... | collective-permute-start | bytes 1204232 | tf_op jit(solution)/shard_map/ppermute | solution.py:249
  12.4 0.0 copy-start
  12.4 3.9 %shard_map.74 = (bf16[1536,2304]{1,0:T(8,128)(2,1)S(1)}, bf16[1536,128]{1,0:T(8,128)(2,1)S(1)}, bf16[1536,256]{1,0:T(8,128)(2,1)S(1)}, f32[8,256]{1,0:T(8,128)S(1)}) custom-call(s32[1]{0:T(128)} %bitcast.index, f32[1]{0:T(128)S(6)} %copy.12.damp_in, s32[12]{0:T(128)} %agg_hbm.3, s32[12,9]{1,0:T(8,128)} %cols_hbm.1, bf16[1536,128]{1,0:T(8,128)(2,1)} %bitcast.5, ...), custom_call_target="tpu_custom_call" | custom-call | flops 1207959552 | bytes 4334056 | tf_op jit(solution)/shard_map/pallas_call | solution.py:25
  16.3 0.0 collective-permute-done.pay.pay_s
  16.3 0.0 copy-done
  16.3 1.4 %shard_map.75.p_s = bf16[1536,256]{1,0:T(8,128)(2,1)S(1)} custom-call(s32[1,2,3]{2,1,0:T(2,128)S(1)} %copy-done, s32[1]{0:T(128)} %bitcast.index, f32[8,256]{1,0:T(8,128)S(1)} %get-tuple-element.21.damp, bf16[1536,2304]{1,0:T(8,128)(2,1)S(1)} %get-tuple-element.20.dense, bf16[1536,128]{1,0:T(8,128)(2,1)S(1)} %get-tuple-element.22.inv, ...), custom_call_target="tpu_custom_call" | custom-call | flops 301989888 | bytes 7880732 | tf_op jit(solution)/shard_map/pallas_call | solution.py:25
  17.8 0.0 collective-permute-done.1.pay_x
  17.8 1.5 %shard_map.76 = (bf16[1536,256]{1,0:T(8,128)(2,1)S(1)}, bf16[384,768]{1,0:T(8,128)(2,1)S(1)}, bf16[384,768]{1,0:T(8,128)(2,1)S(1)}) custom-call(s32[1,2,3]{2,1,0:T(2,128)S(1)} %copy-done, s32[1]{0:T(128)} %bitcast.index, f32[8,256]{1,0:T(8,128)S(1)} %get-tuple-element.21.damp, bf16[1536,2304]{1,0:T(8,128)(2,1)S(1)} %get-tuple-element.20.dense, ...), custom_call_target="tpu_custom_call" | custom-call | flops 301989888 | bytes 9855004 | tf_op jit(solution)/shard_map/pallas_call | solution.py:25
  19.3 0.1 collective-permute-start.2
  19.4 7.3 %collective-permute-start.3 = (bf16[384,768]{1,0:T(8,128)(2,1)S(1)}, bf16[384,768]{1,0:T(8,128)(2,1)S(1)}, u32[]{:S(2)}, u32[]{:S(2)}) collective-permute-start(bf16[384,768]{1,0:T(8,128)(2,1)S(1)} %get-tuple-element.28.sent_x), channel_id=1, source_target_pairs={{1,2},{2,1},{3,4},{4,3},{5,6},{6,5},{7,8},{8,7},{9,10},{10,9},{11,... | collective-permute-start | bytes 1769480 | tf_op jit(solution)/shard_map/ppermute | solution.py:249
  26.7 2.7 %shard_map.80 = (bf16[256,2304]{1,0:T(8,128)(2,1)S(1)}, f32[256,768]{1,0:T(8,128)S(1)}) custom-call(s32[1]{0:T(128)} %bitcast.index, bf16[1536,2304]{1,0:T(8,128)(2,1)S(1)} %get-tuple-element.20.dense, bf16[1536,256]{1,0:T(8,128)(2,1)S(1)} %shard_map.75.p_s, bf16[1536,256]{1,0:T(8,128)(2,1)S(1)} %get-tuple-element.23.p_own, ...), custom_call_target="tpu_custom_call" | custom-call | flops 2415919104 | bytes 9437188 | tf_op jit(solution)/shard_map/pallas_call | solution.py:25
  29.4 0.0 collective-permute-done.2.far_s
  29.4 0.4 shard_map.82
  29.7 2.7 %collective-permute-start.5 = (bf16[256,1408]{1,0:T(8,128)(2,1)S(1)}, bf16[256,1408]{1,0:T(8,128)(2,1)S(1)}, u32[]{:S(2)}, u32[]{:S(2)}) collective-permute-start(bf16[256,1408]{1,0:T(8,128)(2,1)S(1)} %shard_map.82), channel_id=1, source_target_pairs={{1,2},{2,1},{3,4},{4,3},{5,6},{6,5},{7,8},{8,7},{9,10},{10,9},{11,... | collective-permute-start | bytes 2162696 | tf_op jit(solution)/shard_map/ppermute | solution.py:249
  32.4 5.1 %shard_map.77 = (bf16[256,2304]{1,0:T(8,128)(2,1)S(1)}, f32[256,768]{1,0:T(8,128)S(1)}, bf16[256,2304]{1,0:T(8,128)(2,1)S(1)}, f32[256,768]{1,0:T(8,128)S(1)}) custom-call(bf16[1536,2304]{1,0:T(8,128)(2,1)S(1)} %get-tuple-element.20.dense, bf16[1536,256]{1,0:T(8,128)(2,1)S(1)} %shard_map.75.p_s, bf16[1536,256]{1,0:T(8,128)(2,1)S(1)} %get-tuple-element.23.p_own, ...), custom_call_target="tpu_custom_call" | custom-call | flops 4831838208 | bytes 9437184 | tf_op jit(solution)/shard_map/pallas_call | solution.py:25
  37.5 0.0 collective-permute-done.3.far_x
  37.5 0.6 %shard_map.78 = bf16[256,1280]{1,0:T(8,128)(2,1)S(1)} custom-call(f32[256,768]{1,0:T(8,128)S(1)} %get-tuple-element.29.gal, bf16[256,2304]{1,0:T(8,128)(2,1)S(1)} %get-tuple-element.30.y, bf16[384,768]{1,0:T(8,128)(2,1)S(1)} %collective-permute-done.2.far_s, bf16[384,768]{1,0:T(8,128)(2,1)S(1)} %collective-permute-done.3.far_x), custom_call_target="tpu_custom_call" | custom-call | flops 301989888 | bytes 3145728 | tf_op jit(solution)/shard_map/pallas_call | solution.py:25
  38.1 0.1 collective-permute-start.4
  38.2 2.1 %collective-permute-done.4.from_s = bf16[256,1280]{1,0:T(8,128)(2,1)S(1)} collective-permute-done((bf16[256,1280]{1,0:T(8,128)(2,1)S(1)}, bf16[256,1280]{1,0:T(8,128)(2,1)S(1)}, u32[]{:S(2)}, u32[]{:S(2)}) %collective-permute-start.4) | collective-permute-done | bytes 655392 | tf_op jit(solution)/shard_map/ppermute | solution.py:249
  40.3 0.6 %shard_map.79.mine = f32[256,1792]{1,0:T(8,128)S(1)} custom-call(f32[256,768]{1,0:T(8,128)S(1)} %get-tuple-element.25.gal, bf16[256,2304]{1,0:T(8,128)(2,1)S(1)} %get-tuple-element.26.y, bf16[384,768]{1,0:T(8,128)(2,1)S(1)} %collective-permute-done.2.far_s, bf16[384,768]{1,0:T(8,128)(2,1)S(1)} %collective-permute-done.3.far_x, ...), custom_call_target="tpu_custom_call" | custom-call | flops 301989888 | bytes 3801088 | tf_op jit(solution)/shard_map/pallas_call | solution.py:25
  40.9 5.7 %collective-permute-done.5.from_x = bf16[256,1408]{1,0:T(8,128)(2,1)S(1)} collective-permute-done((bf16[256,1408]{1,0:T(8,128)(2,1)S(1)}, bf16[256,1408]{1,0:T(8,128)(2,1)S(1)}, u32[]{:S(2)}, u32[]{:S(2)}) %collective-permute-start.5) | collective-permute-done | bytes 720928 | tf_op jit(solution)/shard_map/ppermute | solution.py:249
  46.6 1.2 %shard_map.83 = bf16[256,1792]{1,0:T(8,128)(2,1)} custom-call(s32[1]{0:T(128)} %bitcast.index, f32[256,1792]{1,0:T(8,128)S(1)} %shard_map.79.mine, bf16[384,768]{1,0:T(8,128)(2,1)S(1)} %get-tuple-element.28.sent_x, bf16[256,1408]{1,0:T(8,128)(2,1)S(1)} %collective-permute-done.5.from_x), custom_call_target="tpu_custom_call" | custom-call | flops 150994944 | bytes 3145732 | tf_op jit(solution)/shard_map/pallas_call | solution.py:25
  (1 shorter events, 0.0 us)
Async XLA Ops:
  1.0 15.3 %collective-permute-start = (bf16[1568,128]{1,0:T(8,128)(2,1)S(1)}, bf16[1568,128]{1,0:T(8,128)(2,1)S(1)}, u32[]{:S(2)}, u32[]{:S(2)}) collective-permute-start(bf16[1568,128]{1,0:T(8,128)(2,1)S(1)} %shard_map.73.pay), channel_id=1, source_target_pairs={{0,1},{1,0},{2,3},{3,2},{4,5},{5,4},{6,7},{7,6},{8,9},{9,8},{10,11... | collective-permute-start | bytes 1204232 | tf_op jit(solution)/shard_map/ppermute | solution.py:249
  1.1 16.7 %collective-permute-start.1 = (bf16[1568,128]{1,0:T(8,128)(2,1)S(1)}, bf16[1568,128]{1,0:T(8,128)(2,1)S(1)}, u32[]{:S(2)}, u32[]{:S(2)}) collective-permute-start(bf16[1568,128]{1,0:T(8,128)(2,1)S(1)} %shard_map.73.pay), channel_id=1, source_target_pairs={{1,2},{2,1},{3,4},{4,3},{5,6},{6,5},{7,8},{8,7},{9,10},{10,9},{11,... | collective-permute-start | bytes 1204232 | tf_op jit(solution)/shard_map/ppermute | solution.py:249
  12.4 4.0 %copy-start = (s32[1,2,3]{2,1,0:T(2,128)S(1)}, s32[1,2,3]{2,1,0:T(2,128)}, u32[]{:S(2)}) copy-start(s32[1,2,3]{2,1,0:T(2,128)} %ghost.3) | copy-start | bytes 76
  19.3 10.1 %collective-permute-start.2 = (bf16[384,768]{1,0:T(8,128)(2,1)S(1)}, bf16[384,768]{1,0:T(8,128)(2,1)S(1)}, u32[]{:S(2)}, u32[]{:S(2)}) collective-permute-start(bf16[384,768]{1,0:T(8,128)(2,1)S(1)} %get-tuple-element.27), channel_id=1, source_target_pairs={{0,1},{1,0},{2,3},{3,2},{4,5},{5,4},{6,7},{7,6},{8,9},{9,8},{10,11... | collective-permute-start | bytes 1769480 | tf_op jit(solution)/shard_map/ppermute | solution.py:249
  19.4 18.2 %collective-permute-start.3 = (bf16[384,768]{1,0:T(8,128)(2,1)S(1)}, bf16[384,768]{1,0:T(8,128)(2,1)S(1)}, u32[]{:S(2)}, u32[]{:S(2)}) collective-permute-start(bf16[384,768]{1,0:T(8,128)(2,1)S(1)} %get-tuple-element.28.sent_x), channel_id=1, source_target_pairs={{1,2},{2,1},{3,4},{4,3},{5,6},{6,5},{7,8},{8,7},{9,10},{10,9},{11,... | collective-permute-start | bytes 1769480 | tf_op jit(solution)/shard_map/ppermute | solution.py:249
  29.7 16.8 %collective-permute-start.5 = (bf16[256,1408]{1,0:T(8,128)(2,1)S(1)}, bf16[256,1408]{1,0:T(8,128)(2,1)S(1)}, u32[]{:S(2)}, u32[]{:S(2)}) collective-permute-start(bf16[256,1408]{1,0:T(8,128)(2,1)S(1)} %shard_map.82), channel_id=1, source_target_pairs={{1,2},{2,1},{3,4},{4,3},{5,6},{6,5},{7,8},{8,7},{9,10},{10,9},{11,... | collective-permute-start | bytes 2162696 | tf_op jit(solution)/shard_map/ppermute | solution.py:249
  38.1 2.2 %collective-permute-start.4 = (bf16[256,1280]{1,0:T(8,128)(2,1)S(1)}, bf16[256,1280]{1,0:T(8,128)(2,1)S(1)}, u32[]{:S(2)}, u32[]{:S(2)}) collective-permute-start(bf16[256,1280]{1,0:T(8,128)(2,1)S(1)} %shard_map.78), channel_id=1, source_target_pairs={{0,1},{1,0},{2,3},{3,2},{4,5},{5,4},{6,7},{7,6},{8,9},{9,8},{10,11... | collective-permute-start | bytes 1966088 | tf_op jit(solution)/shard_map/ppermute | solution.py:249

commit v7 on v6

--- a/solution.py
+++ b/solution.py
@@ -42,7 +42,9 @@
     return jnp.dot(a, b, preferred_element_type=F32)
 
 
-def pack_kernel(r, b, s, agg_hbm, ghost_hbm, tent_hbm, out, agg, ghost, sems):
+def pack_kernel(
+    group, r, b, s, index, agg_hbm, ghost_hbm, tent_hbm, vals_hbm, out, dense, vals, agg, ghost, sems, fetch_sems
+):
     copies = [
         pltpu.make_async_copy(agg_hbm, agg, sems.at[0]),
         pltpu.make_async_copy(ghost_hbm, ghost, sems.at[1]),
@@ -60,7 +62,34 @@
         for j in range(s):
             meta = jnp.where(sub == 16 + 8 * side + j, ghost[0, side, j].astype(F32), meta)
     out[r * b :, :] = meta.astype(BF16)
+
+    @pl.when(opens_group(index, group))
+    def _():
+        fetches = fetch_blocks(r, vals_hbm, vals, fetch_sems)
+        clear_rows(r, b, dense)
+        for copy in fetches:
+            copy.wait()
+
     copies[2].wait()
+
+
+def opens_group(index, group):
+    return (lax.rem(index[0], group) == 0) & (index[0] > 0)
+
+
+def fetch_blocks(r, vals_hbm, vals, sems):
+    copies = [pltpu.make_async_copy(vals_hbm.at[j], vals.at[j], sems.at[j]) for j in range(r)]
+    for copy in copies:
+        copy.start()
+    return copies
+
+
+def clear_rows(r, b, dense):
+    def clear(j, carry):
+        dense[rows(j, b), :] = jnp.zeros((b, dense.shape[1]), BF16)
+        return carry
+
+    lax.fori_loop(0, r, clear, 0)
 
 
 def smooth(r, b, dense, cols, placed, inv, damp, half, target, base=None):
@@ -96,25 +125,21 @@
 
 
 def own_kernel(
-    r, k, b, s, index, damp_in, agg_hbm, cols_hbm, inv_hbm, vals_hbm, pay,
-    dense, inv, p_own, damp, agg, cols, vals, placed, half, sems,
+    group, r, k, b, s, index, damp_in, agg_hbm, cols_hbm, inv_hbm, vals_hbm, pay, dense_in, vals_in,
+    dense, vals, inv, p_own, damp, agg, cols, placed, half, sems, fetch_sems,
 ):
-    def fetch(j):
-        return pltpu.make_async_copy(vals_hbm.at[j], vals.at[j], sems.at[3 + j])
-
     pairs = ((cols_hbm, cols), (agg_hbm, agg), (inv_hbm, inv))
     others = [pltpu.make_async_copy(src, dst, sems.at[i]) for i, (src, dst) in enumerate(pairs)]
-    for copy in others[:2]:
+    for copy in others:
         copy.start()
-    for j in range(r):
-        fetch(j).start()
-    others[2].start()
-
-    def clear(j, carry):
-        dense[rows(j, b), :] = jnp.zeros((b, (r + 2 * s) * b), BF16)
-        return carry
-
-    lax.fori_loop(0, r, clear, 0)
+
+    @pl.when(jnp.logical_not(opens_group(index, group)))
+    def _():
+        fetches = fetch_blocks(r, vals_hbm, vals, fetch_sems)
+        clear_rows(r, b, dense)
+        for copy in fetches:
+            copy.wait()
+
     for copy in others[:2]:
         copy.wait()
     damp[...] = jnp.full(damp.shape, damp_in[0], F32)
@@ -129,7 +154,6 @@
     left = s * (1 - odd)
 
     def row(j, carry):
-        fetch(j).wait()
         at = rows(j, b)
         for e in range(k):
             c = cols[j, e]
@@ -165,7 +189,7 @@
 def cross_kernel(ahead, group, r, b, w, index, dense, p_s, p_own, p_x, *refs):
     y, gal, flipped = refs[-3:]
 
-    opens = (lax.rem(index[0], group) == 0) & (index[0] > 0)
+    opens = opens_group(index, group)
 
     @pl.when(opens if ahead else jnp.logical_not(opens))
     def _():
@@ -195,10 +219,9 @@
         gal[:, d * w : (d + 1) * w] = dot(y[:, : r * b], other[...])
 
 
-def rest_kernel(r, b, w, dense, p_s, p_own, p_x, y_s, gal_s, y_own, gal_own, flipped, flipped_own):
+def rest_kernel(which, r, b, w, dense, p_s, p_own, p_x, y, gal, flipped):
     parts = (p_s, p_own, p_x)
-    part_rows(r, b, w, dense, p_s, parts, y_s, gal_s, flipped)
-    part_rows(r, b, w, dense, p_own, parts, y_own, gal_own, flipped_own)
+    part_rows(r, b, w, dense, parts[which], parts, y, gal, flipped)
 
 
 def galerkin_rows(w, span, gal, y, far_s, far_x):
@@ -267,22 +290,23 @@
     dma = pltpu.SemaphoreType.DMA
     total = (r + 2 * s) * b
 
-    (pay,) = call(
-        functools.partial(pack_kernel, r, b, s), (aggregate, ghost_rows, tent), "hhh",
-        [((r * b + META, b), BF16)],
-        scratch=[SMEM((r,), jnp.int32), SMEM((1, 2, s), jnp.int32), dma((3,))], limit=2 << 20,
+    dense_shape, vals_shape = ((r * b, total), BF16), ((r, k, b, b), BF16)
+    pay, dense, vals = call(
+        functools.partial(pack_kernel, group, r, b, s), (index, aggregate, ghost_rows, tent, block_values), "shhhh",
+        [((r * b + META, b), BF16), dense_shape, vals_shape],
+        scratch=[SMEM((r,), jnp.int32), SMEM((1, 2, s), jnp.int32), dma((3,)), dma((r,))], limit=12 << 20,
     )
     pay_x = swap(pay, cross)
     pay_s = swap(pay, chip)
-    dense, inv, p_own, damp = call(
-        functools.partial(own_kernel, r, k, b, s),
-        (index, damping, aggregate, block_columns, inv, block_values, pay), "sshhhhv",
-        [((r * b, total), BF16), ((r * b, b), BF16), ((r * b, w), BF16), ((8, w), F32)],
+    dense, _, inv, p_own, damp = call(
+        functools.partial(own_kernel, group, r, k, b, s),
+        (index, damping, aggregate, block_columns, inv, block_values, pay, dense, vals), "sshhhhvvv",
+        [dense_shape, vals_shape, ((r * b, b), BF16), ((r * b, w), BF16), ((8, w), F32)],
         scratch=[
-            SMEM((r,), jnp.int32), SMEM((r, k), jnp.int32), VMEM((r, k, b, b), BF16),
-            VMEM((r * b, w), BF16), VMEM((r * b, w), BF16), dma((r + 3,)),
+            SMEM((r,), jnp.int32), SMEM((r, k), jnp.int32), VMEM((r * b, w), BF16), VMEM((r * b, w), BF16),
+            dma((3,)), dma((r,)),
         ],
-        flops=2 * r * b * r * b * w, limit=24 << 20,
+        flops=2 * r * b * r * b * w, limit=24 << 20, aliases={7: 0, 8: 1},
     )
     (p_s,) = call(
         functools.partial(near_kernel, r, b, s), (ghost_rows, index, damp, dense, inv, pay_s), "ssvvvv",
@@ -315,15 +339,20 @@
         [((w, 4 * w + span), BF16)], flops=2 * w * span * 3 * w, limit=16 << 20,
     )
     from_x = swap(sum_x, cross)
-    y_s, gal_s, y_own, gal_own = call(
-        functools.partial(rest_kernel, r, b, w), (dense, p_s, p_own, p_x), "vvvv",
-        shapes + shapes, scratch=scratch + scratch, flops=2 * flops, limit=24 << 20,
-    )
+
+    def rest(which):
+        return call(
+            functools.partial(rest_kernel, which, r, b, w), (dense, p_s, p_own, p_x), "vvvv",
+            shapes, scratch=scratch, flops=flops, limit=24 << 20,
+        )
+
+    y_s, gal_s = rest(0)
     (sum_s,) = call(
         functools.partial(chip_kernel, w, span), (gal_s, y_s, far_s, far_x), "vvvv",
         [((w, 5 * w), BF16)], flops=4 * w * span * 3 * w, limit=16 << 20,
     )
     from_s = swap(sum_s, chip)
+    y_own, gal_own = rest(1)
     (mine,) = call(
         functools.partial(inner_kernel, w, span), (gal_own, y_own, far_s, far_x, from_s), "vvvvv",
         [((w, 7 * w), F32)], flops=4 * w * span * 3 * w, limit=16 << 20,

time: 48.1 us -> 48.2 us (level)
  Pallas kernels: 18.3 us -> 20 us
  starting transfers between devices: 20.8 us -> 19.1 us
    pallas_call x11 -> x12, Pallas kernels: 18.3 us -> 20 us  [call(): pl.pallas_call(kernel, out_shape=[jax.ShapeDtypeStruct(*o) for o in outs]...]
    ppermute x6, starting transfers between devices: 20.8 us -> 19.1 us  [swap(): return lax.ppermute(x, AXES, route)]
  transfers between devices with their start and end apart: 6 -> 6, of which waited for: 2 -> 1; matrix products, arithmetic and copies ran while one was open for 0% -> 0% of each run, Pallas kernels for 31% -> 30%
where the time goes in v7:
time: 48.2 us; the launch traced here: 48 us
  Pallas kernels  20 us (41%)
  starting transfers between devices  19.1 us (40%)
  waiting for transfers between devices  7.88 us (16%)
  between operations  0.99 us (2%)
    pallas_call x12, Pallas kernels, call(): pl.pallas_call(kernel, out_shape=[jax.ShapeDtypeStruct(*o) for o in outs]...  20 us
    ppermute x6, starting transfers between devices, swap(): return lax.ppermute(x, AXES, route)  19.1 us
    ppermute x6, waiting for transfers between devices, swap(): return lax.ppermute(x, AXES, route)  7.88 us
  transfers between devices with their start and end apart: 6, of which 1 were waited for; matrix products, arithmetic and copies ran while one was open for 0% of the time, Pallas kernels for 30%

profile of v7, /device:TPU:6, one launch (start us, length us, event | category | flops | bytes accessed | tf_op | source)
XLA Modules:
  0.0 48.0 jit_solution(2699082371364818435)
XLA Ops:
  0.0 2.8 %shard_map.73 = (bf16[1568,128]{1,0:T(8,128)(2,1)S(1)}, bf16[1536,2304]{1,0:T(8,128)(2,1)S(1)}, bf16[12,9,128,128]{3,2,1,0:T(8,128)(2,1)S(1)}) custom-call(s32[1]{0:T(128)} %bitcast.index, s32[12]{0:T(128)} %agg_hbm.3, s32[1,2,3]{2,1,0:T(2,128)} %ghost.3, bf16[1536,128]{1,0:T(8,128)(2,1)} %bitcast.4, bf16[12,9,128,128]{3,2,1,0:T(8,128)(2,1)} %vals_hbm.3), custom_call_target="tpu_custom_call" | custom-call | flops 1 | bytes 3932236 | tf_op jit(solution)/shard_map/pallas_call | solution.py:25
  2.8 0.1 collective-permute-start
  2.9 8.9 %collective-permute-start.1 = (bf16[1568,128]{1,0:T(8,128)(2,1)S(1)}, bf16[1568,128]{1,0:T(8,128)(2,1)S(1)}, u32[]{:S(2)}, u32[]{:S(2)}) collective-permute-start(bf16[1568,128]{1,0:T(8,128)(2,1)S(1)} %get-tuple-element.23.pay), channel_id=1, source_target_pairs={{1,2},{2,1},{3,4},{4,3},{5,6},{6,5},{7,8},{8,7},{9,10},{10,9},{11,... | collective-permute-start | bytes 1204232 | tf_op jit(solution)/shard_map/ppermute | solution.py:272
  12.5 0.0 copy-start
  12.5 3.6 %shard_map.74 = (bf16[1536,2304]{1,0:T(8,128)(2,1)S(1)}, bf16[12,9,128,128]{3,2,1,0:T(8,128)(2,1)S(1)}, bf16[1536,128]{1,0:T(8,128)(2,1)S(1)}, bf16[1536,256]{1,0:T(8,128)(2,1)S(1)}, f32[8,256]{1,0:T(8,128)S(1)}) custom-call(s32[1]{0:T(128)} %bitcast.index, f32[1]{0:T(128)S(6)} %copy.16.damp_in, ...), custom_call_target="tpu_custom_call", output_to_operand_aliasing={{0}: (7, {}), {1}: (8, {})} | custom-call | flops 1207959552 | bytes 14950888 | tf_op jit(solution)/shard_map/pallas_call | solution.py:25
  16.1 0.0 collective-permute-done.pay.pay_s
  16.1 0.0 copy-done
  16.1 1.4 %shard_map.75.p_s = bf16[1536,256]{1,0:T(8,128)(2,1)S(1)} custom-call(s32[1,2,3]{2,1,0:T(2,128)S(1)} %copy-done, s32[1]{0:T(128)} %bitcast.index, f32[8,256]{1,0:T(8,128)S(1)} %get-tuple-element.27.damp, bf16[1536,2304]{1,0:T(8,128)(2,1)S(1)} %get-tuple-element.26.dense, bf16[1536,128]{1,0:T(8,128)(2,1)S(1)} %get-tuple-element.28.inv, ...), custom_call_target="tpu_custom_call" | custom-call | flops 301989888 | bytes 7880732 | tf_op jit(solution)/shard_map/pallas_call | solution.py:25
  17.6 0.0 collective-permute-done.1.pay_x
  17.6 1.5 %shard_map.76 = (bf16[1536,256]{1,0:T(8,128)(2,1)S(1)}, bf16[384,768]{1,0:T(8,128)(2,1)S(1)}, bf16[384,768]{1,0:T(8,128)(2,1)S(1)}) custom-call(s32[1,2,3]{2,1,0:T(2,128)S(1)} %copy-done, s32[1]{0:T(128)} %bitcast.index, f32[8,256]{1,0:T(8,128)S(1)} %get-tuple-element.27.damp, bf16[1536,2304]{1,0:T(8,128)(2,1)S(1)} %get-tuple-element.26.dense, ...), custom_call_target="tpu_custom_call" | custom-call | flops 301989888 | bytes 9855004 | tf_op jit(solution)/shard_map/pallas_call | solution.py:25
  19.0 0.1 collective-permute-start.2
  19.1 7.6 %collective-permute-start.3 = (bf16[384,768]{1,0:T(8,128)(2,1)S(1)}, bf16[384,768]{1,0:T(8,128)(2,1)S(1)}, u32[]{:S(2)}, u32[]{:S(2)}) collective-permute-start(bf16[384,768]{1,0:T(8,128)(2,1)S(1)} %get-tuple-element.34.sent_x), channel_id=1, source_target_pairs={{1,2},{2,1},{3,4},{4,3},{5,6},{6,5},{7,8},{8,7},{9,10},{10,9},{11,... | collective-permute-start | bytes 1769480 | tf_op jit(solution)/shard_map/ppermute | solution.py:272
  26.8 2.7 %shard_map.81 = (bf16[256,2304]{1,0:T(8,128)(2,1)S(1)}, f32[256,768]{1,0:T(8,128)S(1)}) custom-call(s32[1]{0:T(128)} %bitcast.index, bf16[1536,2304]{1,0:T(8,128)(2,1)S(1)} %get-tuple-element.26.dense, bf16[1536,256]{1,0:T(8,128)(2,1)S(1)} %shard_map.75.p_s, bf16[1536,256]{1,0:T(8,128)(2,1)S(1)} %get-tuple-element.29.p_own, ...), custom_call_target="tpu_custom_call" | custom-call | flops 2415919104 | bytes 9437188 | tf_op jit(solution)/shard_map/pallas_call | solution.py:25
  29.5 0.0 collective-permute-done.2.far_s
  29.5 0.4 shard_map.83
  29.9 2.2 %collective-permute-start.5 = (bf16[256,1408]{1,0:T(8,128)(2,1)S(1)}, bf16[256,1408]{1,0:T(8,128)(2,1)S(1)}, u32[]{:S(2)}, u32[]{:S(2)}) collective-permute-start(bf16[256,1408]{1,0:T(8,128)(2,1)S(1)} %shard_map.83), channel_id=1, source_target_pairs={{1,2},{2,1},{3,4},{4,3},{5,6},{6,5},{7,8},{8,7},{9,10},{10,9},{11,... | collective-permute-start | bytes 2162696 | tf_op jit(solution)/shard_map/ppermute | solution.py:272
  32.0 2.7 %shard_map.78 = (bf16[256,2304]{1,0:T(8,128)(2,1)S(1)}, f32[256,768]{1,0:T(8,128)S(1)}) custom-call(bf16[1536,2304]{1,0:T(8,128)(2,1)S(1)} %get-tuple-element.26.dense, bf16[1536,256]{1,0:T(8,128)(2,1)S(1)} %shard_map.75.p_s, bf16[1536,256]{1,0:T(8,128)(2,1)S(1)} %get-tuple-element.29.p_own, bf16[1536,256]{1,0:T(8,128)(2,1)S(1)} %get-tuple-element.30.p_x), custom_call_target="tpu_custom_call" | custom-call | flops 2415919104 | bytes 9437184 | tf_op jit(solution)/shard_map/pallas_call | solution.py:25
  34.7 0.0 collective-permute-done.3.far_x
  34.7 0.6 %shard_map.79 = bf16[256,1280]{1,0:T(8,128)(2,1)S(1)} custom-call(f32[256,768]{1,0:T(8,128)S(1)} %get-tuple-element.35.gal, bf16[256,2304]{1,0:T(8,128)(2,1)S(1)} %get-tuple-element.36.y, bf16[384,768]{1,0:T(8,128)(2,1)S(1)} %collective-permute-done.2.far_s, bf16[384,768]{1,0:T(8,128)(2,1)S(1)} %collective-permute-done.3.far_x), custom_call_target="tpu_custom_call" | custom-call | flops 301989888 | bytes 3145728 | tf_op jit(solution)/shard_map/pallas_call | solution.py:25
  35.3 0.3 collective-permute-start.4
  35.6 2.7 %shard_map.77 = (bf16[256,2304]{1,0:T(8,128)(2,1)S(1)}, f32[256,768]{1,0:T(8,128)S(1)}) custom-call(bf16[1536,2304]{1,0:T(8,128)(2,1)S(1)} %get-tuple-element.26.dense, bf16[1536,256]{1,0:T(8,128)(2,1)S(1)} %shard_map.75.p_s, bf16[1536,256]{1,0:T(8,128)(2,1)S(1)} %get-tuple-element.29.p_own, bf16[1536,256]{1,0:T(8,128)(2,1)S(1)} %get-tuple-element.30.p_x), custom_call_target="tpu_custom_call" | custom-call | flops 2415919104 | bytes 9437184 | tf_op jit(solution)/shard_map/pallas_call | solution.py:25
  38.2 0.0 collective-permute-done.4.from_s
  38.2 0.6 %shard_map.80.mine = f32[256,1792]{1,0:T(8,128)S(1)} custom-call(f32[256,768]{1,0:T(8,128)S(1)} %get-tuple-element.31.gal, bf16[256,2304]{1,0:T(8,128)(2,1)S(1)} %get-tuple-element.32.y, bf16[384,768]{1,0:T(8,128)(2,1)S(1)} %collective-permute-done.2.far_s, bf16[384,768]{1,0:T(8,128)(2,1)S(1)} %collective-permute-done.3.far_x, ...), custom_call_target="tpu_custom_call" | custom-call | flops 301989888 | bytes 3801088 | tf_op jit(solution)/shard_map/pallas_call | solution.py:25
  38.8 7.9 %collective-permute-done.5.from_x = bf16[256,1408]{1,0:T(8,128)(2,1)S(1)} collective-permute-done((bf16[256,1408]{1,0:T(8,128)(2,1)S(1)}, bf16[256,1408]{1,0:T(8,128)(2,1)S(1)}, u32[]{:S(2)}, u32[]{:S(2)}) %collective-permute-start.5) | collective-permute-done | bytes 720928 | tf_op jit(solution)/shard_map/ppermute | solution.py:272
  46.7 1.2 %shard_map.84 = bf16[256,1792]{1,0:T(8,128)(2,1)} custom-call(s32[1]{0:T(128)} %bitcast.index, f32[256,1792]{1,0:T(8,128)S(1)} %shard_map.80.mine, bf16[384,768]{1,0:T(8,128)(2,1)S(1)} %get-tuple-element.34.sent_x, bf16[256,1408]{1,0:T(8,128)(2,1)S(1)} %collective-permute-done.5.from_x), custom_call_target="tpu_custom_call" | custom-call | flops 150994944 | bytes 3145732 | tf_op jit(solution)/shard_map/pallas_call | solution.py:25
  (1 shorter events, 0.0 us)
Async XLA Ops:
  2.8 13.3 %collective-permute-start = (bf16[1568,128]{1,0:T(8,128)(2,1)S(1)}, bf16[1568,128]{1,0:T(8,128)(2,1)S(1)}, u32[]{:S(2)}, u32[]{:S(2)}) collective-permute-start(bf16[1568,128]{1,0:T(8,128)(2,1)S(1)} %get-tuple-element.23.pay), channel_id=1, source_target_pairs={{0,1},{1,0},{2,3},{3,2},{4,5},{5,4},{6,7},{7,6},{8,9},{9,8},{10,11... | collective-permute-start | bytes 1204232 | tf_op jit(solution)/shard_map/ppermute | solution.py:272
  2.9 14.7 %collective-permute-start.1 = (bf16[1568,128]{1,0:T(8,128)(2,1)S(1)}, bf16[1568,128]{1,0:T(8,128)(2,1)S(1)}, u32[]{:S(2)}, u32[]{:S(2)}) collective-permute-start(bf16[1568,128]{1,0:T(8,128)(2,1)S(1)} %get-tuple-element.23.pay), channel_id=1, source_target_pairs={{1,2},{2,1},{3,4},{4,3},{5,6},{6,5},{7,8},{8,7},{9,10},{10,9},{11,... | collective-permute-start | bytes 1204232 | tf_op jit(solution)/shard_map/ppermute | solution.py:272
  12.5 3.7 %copy-start = (s32[1,2,3]{2,1,0:T(2,128)S(1)}, s32[1,2,3]{2,1,0:T(2,128)}, u32[]{:S(2)}) copy-start(s32[1,2,3]{2,1,0:T(2,128)} %ghost.3) | copy-start | bytes 76
  19.0 10.4 %collective-permute-start.2 = (bf16[384,768]{1,0:T(8,128)(2,1)S(1)}, bf16[384,768]{1,0:T(8,128)(2,1)S(1)}, u32[]{:S(2)}, u32[]{:S(2)}) collective-permute-start(bf16[384,768]{1,0:T(8,128)(2,1)S(1)} %get-tuple-element.33), channel_id=1, source_target_pairs={{0,1},{1,0},{2,3},{3,2},{4,5},{5,4},{6,7},{7,6},{8,9},{9,8},{10,11... | collective-permute-start | bytes 1769480 | tf_op jit(solution)/shard_map/ppermute | solution.py:272
  19.1 15.5 %collective-permute-start.3 = (bf16[384,768]{1,0:T(8,128)(2,1)S(1)}, bf16[384,768]{1,0:T(8,128)(2,1)S(1)}, u32[]{:S(2)}, u32[]{:S(2)}) collective-permute-start(bf16[384,768]{1,0:T(8,128)(2,1)S(1)} %get-tuple-element.34.sent_x), channel_id=1, source_target_pairs={{1,2},{2,1},{3,4},{4,3},{5,6},{6,5},{7,8},{8,7},{9,10},{10,9},{11,... | collective-permute-start | bytes 1769480 | tf_op jit(solution)/shard_map/ppermute | solution.py:272
  29.9 16.8 %collective-permute-start.5 = (bf16[256,1408]{1,0:T(8,128)(2,1)S(1)}, bf16[256,1408]{1,0:T(8,128)(2,1)S(1)}, u32[]{:S(2)}, u32[]{:S(2)}) collective-permute-start(bf16[256,1408]{1,0:T(8,128)(2,1)S(1)} %shard_map.83), channel_id=1, source_target_pairs={{1,2},{2,1},{3,4},{4,3},{5,6},{6,5},{7,8},{8,7},{9,10},{10,9},{11,... | collective-permute-start | bytes 2162696 | tf_op jit(solution)/shard_map/ppermute | solution.py:272
  35.3 2.9 %collective-permute-start.4 = (bf16[256,1280]{1,0:T(8,128)(2,1)S(1)}, bf16[256,1280]{1,0:T(8,128)(2,1)S(1)}, u32[]{:S(2)}, u32[]{:S(2)}) collective-permute-start(bf16[256,1280]{1,0:T(8,128)(2,1)S(1)} %shard_map.79), channel_id=1, source_target_pairs={{0,1},{1,0},{2,3},{3,2},{4,5},{5,4},{6,7},{7,6},{8,9},{9,8},{10,11... | collective-permute-start | bytes 1966088 | tf_op jit(solution)/shard_map/ppermute | solution.py:272

commit v8 on v6

--- a/solution.py
+++ b/solution.py
@@ -63,9 +63,11 @@
     copies[2].wait()
 
 
-def smooth(r, b, dense, cols, placed, inv, damp, half, target, base=None):
+def smooth(r, b, dense, cols, placed, inv, damp, half, target, base=None, before=None):
     step = 4
     for t in range(r // step):
+        if before is not None:
+            before(range(t * step, (t + 1) * step))
         at = slice(t * step * b, (t + 1) * step * b)
         half[at, :] = dot(dense[at, cols], placed[...]).astype(BF16)
     factor = -damp[0:1, :]
@@ -97,26 +99,41 @@
 
 def own_kernel(
     r, k, b, s, index, damp_in, agg_hbm, cols_hbm, inv_hbm, vals_hbm, pay,
-    dense, inv, p_own, damp, agg, cols, vals, placed, half, sems,
+    dense, inv, p_own, damp, agg, cols, placed, half, sems, block_sems,
 ):
-    def fetch(j):
-        return pltpu.make_async_copy(vals_hbm.at[j], vals.at[j], sems.at[3 + j])
-
     pairs = ((cols_hbm, cols), (agg_hbm, agg), (inv_hbm, inv))
     others = [pltpu.make_async_copy(src, dst, sems.at[i]) for i, (src, dst) in enumerate(pairs)]
-    for copy in others[:2]:
+    for copy in others:
         copy.start()
-    for j in range(r):
-        fetch(j).start()
-    others[2].start()
 
     def clear(j, carry):
         dense[rows(j, b), :] = jnp.zeros((b, (r + 2 * s) * b), BF16)
         return carry
 
     lax.fori_loop(0, r, clear, 0)
-    for copy in others[:2]:
-        copy.wait()
+    others[0].wait()
+    left = s * (1 - (index[0] & 1))
+
+    def fetch(j, e):
+        c = cols[j, e]
+        c = jnp.where(c < r, c, jnp.where(c < r + s, c + left, c - left))
+        return pltpu.make_async_copy(vals_hbm.at[j, e], dense.at[rows(j, b), rows(c, b)], block_sems.at[j, e])
+
+    def start(j, carry):
+        for e in range(k):
+            fetch(j, e).start()
+        return carry
+
+    def wait(found):
+        def finish(j, carry):
+            for e in range(k):
+                fetch(j, e).wait()
+            return carry
+
+        lax.fori_loop(found.start, found.stop, finish, 0)
+
+    lax.fori_loop(0, r, start, 0)
+    others[1].wait()
     damp[...] = jnp.full(damp.shape, damp_in[0], F32)
     zero = jnp.zeros((b, b), BF16)
     for j in range(r):
@@ -125,21 +142,8 @@
         here = agg[j]
         for c in range(CA):
             placed[own, c * b : (c + 1) * b] = jnp.where(here == c, block, zero)
-    odd = (index[0] & 1)
-    left = s * (1 - odd)
-
-    def row(j, carry):
-        fetch(j).wait()
-        at = rows(j, b)
-        for e in range(k):
-            c = cols[j, e]
-            c = jnp.where(c < r, c, jnp.where(c < r + s, c + left, c - left))
-            dense[at, rows(c, b)] = vals[j, e]
-        return carry
-
-    lax.fori_loop(0, r, row, 0)
     others[2].wait()
-    smooth(r, b, dense, slice(0, r * b), placed, inv, damp, half, p_own, placed)
+    smooth(r, b, dense, slice(0, r * b), placed, inv, damp, half, p_own, placed, wait)
 
 
 def near_kernel(r, b, s, ghost, index, damp, dense, inv, pay, p_s, meta, placed, half):
@@ -195,10 +199,9 @@
         gal[:, d * w : (d + 1) * w] = dot(y[:, : r * b], other[...])
 
 
-def rest_kernel(r, b, w, dense, p_s, p_own, p_x, y_s, gal_s, y_own, gal_own, flipped, flipped_own):
+def rest_kernel(which, r, b, w, dense, p_s, p_own, p_x, y, gal, flipped):
     parts = (p_s, p_own, p_x)
-    part_rows(r, b, w, dense, p_s, parts, y_s, gal_s, flipped)
-    part_rows(r, b, w, dense, p_own, parts, y_own, gal_own, flipped_own)
+    part_rows(r, b, w, dense, parts[which], parts, y, gal, flipped)
 
 
 def galerkin_rows(w, span, gal, y, far_s, far_x):
@@ -279,8 +282,8 @@
         (index, damping, aggregate, block_columns, inv, block_values, pay), "sshhhhv",
         [((r * b, total), BF16), ((r * b, b), BF16), ((r * b, w), BF16), ((8, w), F32)],
         scratch=[
-            SMEM((r,), jnp.int32), SMEM((r, k), jnp.int32), VMEM((r, k, b, b), BF16),
-            VMEM((r * b, w), BF16), VMEM((r * b, w), BF16), dma((r + 3,)),
+            SMEM((r,), jnp.int32), SMEM((r, k), jnp.int32), VMEM((r * b, w), BF16), VMEM((r * b, w), BF16),
+            dma((3,)), dma((r, k)),
         ],
         flops=2 * r * b * r * b * w, limit=24 << 20,
     )
@@ -315,15 +318,20 @@
         [((w, 4 * w + span), BF16)], flops=2 * w * span * 3 * w, limit=16 << 20,
     )
     from_x = swap(sum_x, cross)
-    y_s, gal_s, y_own, gal_own = call(
-        functools.partial(rest_kernel, r, b, w), (dense, p_s, p_own, p_x), "vvvv",
-        shapes + shapes, scratch=scratch + scratch, flops=2 * flops, limit=24 << 20,
-    )
+
+    def rest(which):
+        return call(
+            functools.partial(rest_kernel, which, r, b, w), (dense, p_s, p_own, p_x), "vvvv",
+            shapes, scratch=scratch, flops=flops, limit=24 << 20,
+        )
+
+    y_s, gal_s = rest(0)
     (sum_s,) = call(
         functools.partial(chip_kernel, w, span), (gal_s, y_s, far_s, far_x), "vvvv",
         [((w, 5 * w), BF16)], flops=4 * w * span * 3 * w, limit=16 << 20,
     )
     from_s = swap(sum_s, chip)
+    y_own, gal_own = rest(1)
     (mine,) = call(
         functools.partial(inner_kernel, w, span), (gal_own, y_own, far_s, far_x, from_s), "vvvvv",
         [((w, 7 * w), F32)], flops=4 * w * span * 3 * w, limit=16 << 20,

time: 48.1 us -> 48.1 us (level)
  waiting for transfers between devices: 7.8 us -> 5.6 us
  Pallas kernels: 18.3 us -> 20.5 us
    ppermute x6, waiting for transfers between devices: 7.8 us -> 5.6 us  [swap(): return lax.ppermute(x, AXES, route)]
    pallas_call x11 -> x12, Pallas kernels: 18.3 us -> 20.5 us  [call(): pl.pallas_call(kernel, out_shape=[jax.ShapeDtypeStruct(*o) for o in outs]...]
  transfers between devices with their start and end apart: 6 -> 6, of which waited for: 2 -> 1; matrix products, arithmetic and copies ran while one was open for 0% -> 0% of each run, Pallas kernels for 31% -> 35%
where the time goes in v8:
time: 48.1 us; the launch traced here: 47.9 us
  starting transfers between devices  20.8 us (43%)
  Pallas kernels  20.5 us (43%)
  waiting for transfers between devices  5.6 us (12%)
  between operations  0.99 us (2%)
    ppermute x6, starting transfers between devices, swap(): return lax.ppermute(x, AXES, route)  20.8 us
    pallas_call x12, Pallas kernels, call(): pl.pallas_call(kernel, out_shape=[jax.ShapeDtypeStruct(*o) for o in outs]...  20.5 us
    ppermute x6, waiting for transfers between devices, swap(): return lax.ppermute(x, AXES, route)  5.6 us
  transfers between devices with their start and end apart: 6, of which 1 were waited for; matrix products, arithmetic and copies ran while one was open for 0% of the time, Pallas kernels for 35%

profile of v8, /device:TPU:6, one launch (start us, length us, event | category | flops | bytes accessed | tf_op | source)
XLA Modules:
  0.0 47.9 jit_solution(13641277733955540761)
XLA Ops:
  0.0 1.0 %shard_map.73.pay = bf16[1568,128]{1,0:T(8,128)(2,1)S(1)} custom-call(s32[12]{0:T(128)} %agg_hbm.3, s32[1,2,3]{2,1,0:T(2,128)} %ghost.3, bf16[1536,128]{1,0:T(8,128)(2,1)} %bitcast.4), custom_call_target="tpu_custom_call" | custom-call | flops 1 | bytes 393288 | tf_op jit(solution)/shard_map/pallas_call | solution.py:25
  1.0 0.1 collective-permute-start
  1.1 10.6 %collective-permute-start.1 = (bf16[1568,128]{1,0:T(8,128)(2,1)S(1)}, bf16[1568,128]{1,0:T(8,128)(2,1)S(1)}, u32[]{:S(2)}, u32[]{:S(2)}) collective-permute-start(bf16[1568,128]{1,0:T(8,128)(2,1)S(1)} %shard_map.73.pay), channel_id=1, source_target_pairs={{1,2},{2,1},{3,4},{4,3},{5,6},{6,5},{7,8},{8,7},{9,10},{10,9},{11,... | collective-permute-start | bytes 1204232 | tf_op jit(solution)/shard_map/ppermute | solution.py:252
  12.4 0.0 copy-start
  12.4 5.9 %shard_map.74 = (bf16[1536,2304]{1,0:T(8,128)(2,1)S(1)}, bf16[1536,128]{1,0:T(8,128)(2,1)S(1)}, bf16[1536,256]{1,0:T(8,128)(2,1)S(1)}, f32[8,256]{1,0:T(8,128)S(1)}) custom-call(s32[1]{0:T(128)} %bitcast.index, f32[1]{0:T(128)S(6)} %copy.12.damp_in, s32[12]{0:T(128)} %agg_hbm.3, s32[12,9]{1,0:T(8,128)} %cols_hbm.1, bf16[1536,128]{1,0:T(8,128)(2,1)} %bitcast.5, ...), custom_call_target="tpu_custom_call" | custom-call | flops 1207959552 | bytes 4334056 | tf_op jit(solution)/shard_map/pallas_call | solution.py:25
  18.3 0.0 collective-permute-done.pay.pay_s
  18.3 0.0 copy-done
  18.3 1.4 %shard_map.75.p_s = bf16[1536,256]{1,0:T(8,128)(2,1)S(1)} custom-call(s32[1,2,3]{2,1,0:T(2,128)S(1)} %copy-done, s32[1]{0:T(128)} %bitcast.index, f32[8,256]{1,0:T(8,128)S(1)} %get-tuple-element.21.damp, bf16[1536,2304]{1,0:T(8,128)(2,1)S(1)} %get-tuple-element.20.dense, bf16[1536,128]{1,0:T(8,128)(2,1)S(1)} %get-tuple-element.22.inv, ...), custom_call_target="tpu_custom_call" | custom-call | flops 301989888 | bytes 7880732 | tf_op jit(solution)/shard_map/pallas_call | solution.py:25
  19.8 0.0 collective-permute-done.1.pay_x
  19.8 1.5 %shard_map.76 = (bf16[1536,256]{1,0:T(8,128)(2,1)S(1)}, bf16[384,768]{1,0:T(8,128)(2,1)S(1)}, bf16[384,768]{1,0:T(8,128)(2,1)S(1)}) custom-call(s32[1,2,3]{2,1,0:T(2,128)S(1)} %copy-done, s32[1]{0:T(128)} %bitcast.index, f32[8,256]{1,0:T(8,128)S(1)} %get-tuple-element.21.damp, bf16[1536,2304]{1,0:T(8,128)(2,1)S(1)} %get-tuple-element.20.dense, ...), custom_call_target="tpu_custom_call" | custom-call | flops 301989888 | bytes 9855004 | tf_op jit(solution)/shard_map/pallas_call | solution.py:25
  21.2 0.1 collective-permute-start.2
  21.3 5.3 %collective-permute-start.3 = (bf16[384,768]{1,0:T(8,128)(2,1)S(1)}, bf16[384,768]{1,0:T(8,128)(2,1)S(1)}, u32[]{:S(2)}, u32[]{:S(2)}) collective-permute-start(bf16[384,768]{1,0:T(8,128)(2,1)S(1)} %get-tuple-element.28.sent_x), channel_id=1, source_target_pairs={{1,2},{2,1},{3,4},{4,3},{5,6},{6,5},{7,8},{8,7},{9,10},{10,9},{11,... | collective-permute-start | bytes 1769480 | tf_op jit(solution)/shard_map/ppermute | solution.py:252
  26.7 2.6 %shard_map.81 = (bf16[256,2304]{1,0:T(8,128)(2,1)S(1)}, f32[256,768]{1,0:T(8,128)S(1)}) custom-call(s32[1]{0:T(128)} %bitcast.index, bf16[1536,2304]{1,0:T(8,128)(2,1)S(1)} %get-tuple-element.20.dense, bf16[1536,256]{1,0:T(8,128)(2,1)S(1)} %shard_map.75.p_s, bf16[1536,256]{1,0:T(8,128)(2,1)S(1)} %get-tuple-element.23.p_own, ...), custom_call_target="tpu_custom_call" | custom-call | flops 2415919104 | bytes 9437188 | tf_op jit(solution)/shard_map/pallas_call | solution.py:25
  29.4 0.0 collective-permute-done.2.far_s
  29.4 0.4 shard_map.83
  29.7 4.5 %collective-permute-start.5 = (bf16[256,1408]{1,0:T(8,128)(2,1)S(1)}, bf16[256,1408]{1,0:T(8,128)(2,1)S(1)}, u32[]{:S(2)}, u32[]{:S(2)}) collective-permute-start(bf16[256,1408]{1,0:T(8,128)(2,1)S(1)} %shard_map.83), channel_id=1, source_target_pairs={{1,2},{2,1},{3,4},{4,3},{5,6},{6,5},{7,8},{8,7},{9,10},{10,9},{11,... | collective-permute-start | bytes 2162696 | tf_op jit(solution)/shard_map/ppermute | solution.py:252
  34.2 2.7 %shard_map.78 = (bf16[256,2304]{1,0:T(8,128)(2,1)S(1)}, f32[256,768]{1,0:T(8,128)S(1)}) custom-call(bf16[1536,2304]{1,0:T(8,128)(2,1)S(1)} %get-tuple-element.20.dense, bf16[1536,256]{1,0:T(8,128)(2,1)S(1)} %shard_map.75.p_s, bf16[1536,256]{1,0:T(8,128)(2,1)S(1)} %get-tuple-element.23.p_own, bf16[1536,256]{1,0:T(8,128)(2,1)S(1)} %get-tuple-element.24.p_x), custom_call_target="tpu_custom_call" | custom-call | flops 2415919104 | bytes 9437184 | tf_op jit(solution)/shard_map/pallas_call | solution.py:25
  36.9 0.0 collective-permute-done.3.far_x
  36.9 0.6 %shard_map.79 = bf16[256,1280]{1,0:T(8,128)(2,1)S(1)} custom-call(f32[256,768]{1,0:T(8,128)S(1)} %get-tuple-element.29.gal, bf16[256,2304]{1,0:T(8,128)(2,1)S(1)} %get-tuple-element.30.y, bf16[384,768]{1,0:T(8,128)(2,1)S(1)} %collective-permute-done.2.far_s, bf16[384,768]{1,0:T(8,128)(2,1)S(1)} %collective-permute-done.3.far_x), custom_call_target="tpu_custom_call" | custom-call | flops 301989888 | bytes 3145728 | tf_op jit(solution)/shard_map/pallas_call | solution.py:25
  37.5 0.3 collective-permute-start.4
  37.7 2.7 %shard_map.77 = (bf16[256,2304]{1,0:T(8,128)(2,1)S(1)}, f32[256,768]{1,0:T(8,128)S(1)}) custom-call(bf16[1536,2304]{1,0:T(8,128)(2,1)S(1)} %get-tuple-element.20.dense, bf16[1536,256]{1,0:T(8,128)(2,1)S(1)} %shard_map.75.p_s, bf16[1536,256]{1,0:T(8,128)(2,1)S(1)} %get-tuple-element.23.p_own, bf16[1536,256]{1,0:T(8,128)(2,1)S(1)} %get-tuple-element.24.p_x), custom_call_target="tpu_custom_call" | custom-call | flops 2415919104 | bytes 9437184 | tf_op jit(solution)/shard_map/pallas_call | solution.py:25
  40.4 0.0 collective-permute-done.4.from_s
  40.4 0.6 %shard_map.80.mine = f32[256,1792]{1,0:T(8,128)S(1)} custom-call(f32[256,768]{1,0:T(8,128)S(1)} %get-tuple-element.25.gal, bf16[256,2304]{1,0:T(8,128)(2,1)S(1)} %get-tuple-element.26.y, bf16[384,768]{1,0:T(8,128)(2,1)S(1)} %collective-permute-done.2.far_s, bf16[384,768]{1,0:T(8,128)(2,1)S(1)} %collective-permute-done.3.far_x, ...), custom_call_target="tpu_custom_call" | custom-call | flops 301989888 | bytes 3801088 | tf_op jit(solution)/shard_map/pallas_call | solution.py:25
  41.0 5.6 %collective-permute-done.5.from_x = bf16[256,1408]{1,0:T(8,128)(2,1)S(1)} collective-permute-done((bf16[256,1408]{1,0:T(8,128)(2,1)S(1)}, bf16[256,1408]{1,0:T(8,128)(2,1)S(1)}, u32[]{:S(2)}, u32[]{:S(2)}) %collective-permute-start.5) | collective-permute-done | bytes 720928 | tf_op jit(solution)/shard_map/ppermute | solution.py:252
  46.6 1.2 %shard_map.84 = bf16[256,1792]{1,0:T(8,128)(2,1)} custom-call(s32[1]{0:T(128)} %bitcast.index, f32[256,1792]{1,0:T(8,128)S(1)} %shard_map.80.mine, bf16[384,768]{1,0:T(8,128)(2,1)S(1)} %get-tuple-element.28.sent_x, bf16[256,1408]{1,0:T(8,128)(2,1)S(1)} %collective-permute-done.5.from_x), custom_call_target="tpu_custom_call" | custom-call | flops 150994944 | bytes 3145732 | tf_op jit(solution)/shard_map/pallas_call | solution.py:25
  (1 shorter events, 0.0 us)
Async XLA Ops:
  1.0 17.3 %collective-permute-start = (bf16[1568,128]{1,0:T(8,128)(2,1)S(1)}, bf16[1568,128]{1,0:T(8,128)(2,1)S(1)}, u32[]{:S(2)}, u32[]{:S(2)}) collective-permute-start(bf16[1568,128]{1,0:T(8,128)(2,1)S(1)} %shard_map.73.pay), channel_id=1, source_target_pairs={{0,1},{1,0},{2,3},{3,2},{4,5},{5,4},{6,7},{7,6},{8,9},{9,8},{10,11... | collective-permute-start | bytes 1204232 | tf_op jit(solution)/shard_map/ppermute | solution.py:252
  1.1 18.6 %collective-permute-start.1 = (bf16[1568,128]{1,0:T(8,128)(2,1)S(1)}, bf16[1568,128]{1,0:T(8,128)(2,1)S(1)}, u32[]{:S(2)}, u32[]{:S(2)}) collective-permute-start(bf16[1568,128]{1,0:T(8,128)(2,1)S(1)} %shard_map.73.pay), channel_id=1, source_target_pairs={{1,2},{2,1},{3,4},{4,3},{5,6},{6,5},{7,8},{8,7},{9,10},{10,9},{11,... | collective-permute-start | bytes 1204232 | tf_op jit(solution)/shard_map/ppermute | solution.py:252
  12.4 5.9 %copy-start = (s32[1,2,3]{2,1,0:T(2,128)S(1)}, s32[1,2,3]{2,1,0:T(2,128)}, u32[]{:S(2)}) copy-start(s32[1,2,3]{2,1,0:T(2,128)} %ghost.3) | copy-start | bytes 76
  21.2 8.1 %collective-permute-start.2 = (bf16[384,768]{1,0:T(8,128)(2,1)S(1)}, bf16[384,768]{1,0:T(8,128)(2,1)S(1)}, u32[]{:S(2)}, u32[]{:S(2)}) collective-permute-start(bf16[384,768]{1,0:T(8,128)(2,1)S(1)} %get-tuple-element.27), channel_id=1, source_target_pairs={{0,1},{1,0},{2,3},{3,2},{4,5},{5,4},{6,7},{7,6},{8,9},{9,8},{10,11... | collective-permute-start | bytes 1769480 | tf_op jit(solution)/shard_map/ppermute | solution.py:252
  21.3 15.5 %collective-permute-start.3 = (bf16[384,768]{1,0:T(8,128)(2,1)S(1)}, bf16[384,768]{1,0:T(8,128)(2,1)S(1)}, u32[]{:S(2)}, u32[]{:S(2)}) collective-permute-start(bf16[384,768]{1,0:T(8,128)(2,1)S(1)} %get-tuple-element.28.sent_x), channel_id=1, source_target_pairs={{1,2},{2,1},{3,4},{4,3},{5,6},{6,5},{7,8},{8,7},{9,10},{10,9},{11,... | collective-permute-start | bytes 1769480 | tf_op jit(solution)/shard_map/ppermute | solution.py:252
  29.7 16.8 %collective-permute-start.5 = (bf16[256,1408]{1,0:T(8,128)(2,1)S(1)}, bf16[256,1408]{1,0:T(8,128)(2,1)S(1)}, u32[]{:S(2)}, u32[]{:S(2)}) collective-permute-start(bf16[256,1408]{1,0:T(8,128)(2,1)S(1)} %shard_map.83), channel_id=1, source_target_pairs={{1,2},{2,1},{3,4},{4,3},{5,6},{6,5},{7,8},{8,7},{9,10},{10,9},{11,... | collective-permute-start | bytes 2162696 | tf_op jit(solution)/shard_map/ppermute | solution.py:252
  37.5 2.9 %collective-permute-start.4 = (bf16[256,1280]{1,0:T(8,128)(2,1)S(1)}, bf16[256,1280]{1,0:T(8,128)(2,1)S(1)}, u32[]{:S(2)}, u32[]{:S(2)}) collective-permute-start(bf16[256,1280]{1,0:T(8,128)(2,1)S(1)} %shard_map.79), channel_id=1, source_target_pairs={{0,1},{1,0},{2,3},{3,2},{4,5},{5,4},{6,7},{7,6},{8,9},{9,8},{10,11... | collective-permute-start | bytes 1966088 | tf_op jit(solution)/shard_map/ppermute | solution.py:252

commit v9 on v6

--- a/solution.py
+++ b/solution.py
@@ -162,14 +162,22 @@
             out[to, 2 * w :] = p_x[at, :]
 
 
-def cross_kernel(ahead, group, r, b, w, index, dense, p_s, p_own, p_x, *refs):
-    y, gal, flipped = refs[-3:]
-
-    opens = (lax.rem(index[0], group) == 0) & (index[0] > 0)
-
-    @pl.when(opens if ahead else jnp.logical_not(opens))
+def opens_group(index, group):
+    return (lax.rem(index[0], group) == 0) & (index[0] > 0)
+
+
+def ahead_kernel(group, r, b, index, dense, p_x, y, flipped):
+    @pl.when(opens_group(index, group))
     def _():
-        part_rows(r, b, w, dense, p_x, (p_s, p_own, p_x), y, gal, flipped)
+        left_product(r, b, dense, p_x, y, flipped)
+
+
+def cross_kernel(group, r, b, w, index, dense, p_s, p_own, p_x, y_in, y, gal, flipped):
+    @pl.when(jnp.logical_not(opens_group(index, group)))
+    def _():
+        left_product(r, b, dense, p_x, y, flipped)
+
+    right_product(r, b, w, (p_s, p_own, p_x), y, gal)
 
 
 def outer_kernel(w, span, gal, y, far_s, out):
@@ -188,17 +196,20 @@
         flipped[:, at] = p[at, :].T
 
 
-def part_rows(r, b, w, dense, p, parts, y, gal, flipped):
+def left_product(r, b, dense, p, y, flipped):
     flip(r, b, p, flipped)
     y[...] = dot(flipped[...], dense[...]).astype(BF16)
+
+
+def right_product(r, b, w, parts, y, gal):
     for d, other in enumerate(parts):
         gal[:, d * w : (d + 1) * w] = dot(y[:, : r * b], other[...])
 
 
-def rest_kernel(r, b, w, dense, p_s, p_own, p_x, y_s, gal_s, y_own, gal_own, flipped, flipped_own):
+def rest_kernel(which, r, b, w, dense, p_s, p_own, p_x, y, gal, flipped):
     parts = (p_s, p_own, p_x)
-    part_rows(r, b, w, dense, p_s, parts, y_s, gal_s, flipped)
-    part_rows(r, b, w, dense, p_own, parts, y_own, gal_own, flipped_own)
+    left_product(r, b, dense, parts[which], y, flipped)
+    right_product(r, b, w, parts, y, gal)
 
 
 def galerkin_rows(w, span, gal, y, far_s, far_x):
@@ -301,29 +312,33 @@
     shapes = [((w, total), BF16), ((w, 3 * w), F32)]
     scratch = [VMEM((w, r * b), BF16)]
     flops = 2 * r * b * r * b * 2 * w
-    ready = (index, dense, p_s, p_own, p_x)
+    (y_x,) = call(
+        functools.partial(ahead_kernel, group, r, b), (index, dense, p_x), "svv",
+        shapes[:1], scratch=scratch, flops=flops, limit=24 << 20,
+    )
     y_x, gal_x = call(
-        functools.partial(cross_kernel, True, group, r, b, w), ready, "svvvv",
-        shapes, scratch=scratch, flops=flops, limit=24 << 20,
-    )
-    y_x, gal_x = call(
-        functools.partial(cross_kernel, False, group, r, b, w), ready + (y_x, gal_x), "svvvvvv",
-        shapes, scratch=scratch, flops=flops, limit=24 << 20, aliases={5: 0, 6: 1},
+        functools.partial(cross_kernel, group, r, b, w), (index, dense, p_s, p_own, p_x, y_x), "svvvvv",
+        shapes, scratch=scratch, flops=flops, limit=24 << 20, aliases={5: 0},
     )
     (sum_x,) = call(
         functools.partial(outer_kernel, w, span), (gal_x, y_x, far_s), "vvv",
         [((w, 4 * w + span), BF16)], flops=2 * w * span * 3 * w, limit=16 << 20,
     )
     from_x = swap(sum_x, cross)
-    y_s, gal_s, y_own, gal_own = call(
-        functools.partial(rest_kernel, r, b, w), (dense, p_s, p_own, p_x), "vvvv",
-        shapes + shapes, scratch=scratch + scratch, flops=2 * flops, limit=24 << 20,
-    )
+
+    def rest(which):
+        return call(
+            functools.partial(rest_kernel, which, r, b, w), (dense, p_s, p_own, p_x), "vvvv",
+            shapes, scratch=scratch, flops=flops, limit=24 << 20,
+        )
+
+    y_s, gal_s = rest(0)
     (sum_s,) = call(
         functools.partial(chip_kernel, w, span), (gal_s, y_s, far_s, far_x), "vvvv",
         [((w, 5 * w), BF16)], flops=4 * w * span * 3 * w, limit=16 << 20,
     )
     from_s = swap(sum_s, chip)
+    y_own, gal_own = rest(1)
     (mine,) = call(
         functools.partial(inner_kernel, w, span), (gal_own, y_own, far_s, far_x, from_s), "vvvvv",
         [((w, 7 * w), F32)], flops=4 * w * span * 3 * w, limit=16 << 20,

time: 48.1 us -> 48.3 us (level)
    pallas_call x11 -> x12, Pallas kernels: 18.3 us -> 18.7 us  [call(): pl.pallas_call(kernel, out_shape=[jax.ShapeDtypeStruct(*o) for o in outs]...]
  transfers between devices with their start and end apart: 6 -> 6, of which waited for: 2 -> 1; matrix products, arithmetic and copies ran while one was open for 0% -> 0% of each run, Pallas kernels for 31% -> 31%
where the time goes in v9:
time: 48.3 us; the launch traced here: 48.1 us
  starting transfers between devices  20.8 us (43%)
  Pallas kernels  18.7 us (39%)
  waiting for transfers between devices  7.58 us (16%)
  between operations  0.99 us (2%)
    ppermute x6, starting transfers between devices, swap(): return lax.ppermute(x, AXES, route)  20.8 us
    pallas_call x12, Pallas kernels, call(): pl.pallas_call(kernel, out_shape=[jax.ShapeDtypeStruct(*o) for o in outs]...  18.7 us
    ppermute x6, waiting for transfers between devices, swap(): return lax.ppermute(x, AXES, route)  7.58 us
  transfers between devices with their start and end apart: 6, of which 1 were waited for; matrix products, arithmetic and copies ran while one was open for 0% of the time, Pallas kernels for 31%

profile of v9, /device:TPU:6, one launch (start us, length us, event | category | flops | bytes accessed | tf_op | source)
XLA Modules:
  0.0 48.1 jit_solution(3034427770441909710)
XLA Ops:
  0.0 1.0 %shard_map.73.pay = bf16[1568,128]{1,0:T(8,128)(2,1)S(1)} custom-call(s32[12]{0:T(128)} %agg_hbm.3, s32[1,2,3]{2,1,0:T(2,128)} %ghost.3, bf16[1536,128]{1,0:T(8,128)(2,1)} %bitcast.4), custom_call_target="tpu_custom_call" | custom-call | flops 1 | bytes 393288 | tf_op jit(solution)/shard_map/pallas_call | solution.py:25
  1.0 0.1 collective-permute-start
  1.1 10.6 %collective-permute-start.1 = (bf16[1568,128]{1,0:T(8,128)(2,1)S(1)}, bf16[1568,128]{1,0:T(8,128)(2,1)S(1)}, u32[]{:S(2)}, u32[]{:S(2)}) collective-permute-start(bf16[1568,128]{1,0:T(8,128)(2,1)S(1)} %shard_map.73.pay), channel_id=1, source_target_pairs={{1,2},{2,1},{3,4},{4,3},{5,6},{6,5},{7,8},{8,7},{9,10},{10,9},{11,... | collective-permute-start | bytes 1204232 | tf_op jit(solution)/shard_map/ppermute | solution.py:260
  12.4 0.0 copy-start
  12.4 3.9 %shard_map.74 = (bf16[1536,2304]{1,0:T(8,128)(2,1)S(1)}, bf16[1536,128]{1,0:T(8,128)(2,1)S(1)}, bf16[1536,256]{1,0:T(8,128)(2,1)S(1)}, f32[8,256]{1,0:T(8,128)S(1)}) custom-call(s32[1]{0:T(128)} %bitcast.index, f32[1]{0:T(128)S(6)} %copy.10.damp_in, s32[12]{0:T(128)} %agg_hbm.3, s32[12,9]{1,0:T(8,128)} %cols_hbm.1, bf16[1536,128]{1,0:T(8,128)(2,1)} %bitcast.5, ...), custom_call_target="tpu_custom_call" | custom-call | flops 1207959552 | bytes 4334056 | tf_op jit(solution)/shard_map/pallas_call | solution.py:25
  16.3 0.0 collective-permute-done.pay.pay_s
  16.3 0.0 copy-done
  16.3 1.4 %shard_map.75.p_s = bf16[1536,256]{1,0:T(8,128)(2,1)S(1)} custom-call(s32[1,2,3]{2,1,0:T(2,128)S(1)} %copy-done, s32[1]{0:T(128)} %bitcast.index, f32[8,256]{1,0:T(8,128)S(1)} %get-tuple-element.19.damp, bf16[1536,2304]{1,0:T(8,128)(2,1)S(1)} %get-tuple-element.18.dense, bf16[1536,128]{1,0:T(8,128)(2,1)S(1)} %get-tuple-element.20.inv, ...), custom_call_target="tpu_custom_call" | custom-call | flops 301989888 | bytes 7880732 | tf_op jit(solution)/shard_map/pallas_call | solution.py:25
  17.8 0.0 collective-permute-done.1.pay_x
  17.8 1.5 %shard_map.76 = (bf16[1536,256]{1,0:T(8,128)(2,1)S(1)}, bf16[384,768]{1,0:T(8,128)(2,1)S(1)}, bf16[384,768]{1,0:T(8,128)(2,1)S(1)}) custom-call(s32[1,2,3]{2,1,0:T(2,128)S(1)} %copy-done, s32[1]{0:T(128)} %bitcast.index, f32[8,256]{1,0:T(8,128)S(1)} %get-tuple-element.19.damp, bf16[1536,2304]{1,0:T(8,128)(2,1)S(1)} %get-tuple-element.18.dense, ...), custom_call_target="tpu_custom_call" | custom-call | flops 301989888 | bytes 9855004 | tf_op jit(solution)/shard_map/pallas_call | solution.py:25
  19.3 0.1 collective-permute-start.2
  19.4 7.3 %collective-permute-start.3 = (bf16[384,768]{1,0:T(8,128)(2,1)S(1)}, bf16[384,768]{1,0:T(8,128)(2,1)S(1)}, u32[]{:S(2)}, u32[]{:S(2)}) collective-permute-start(bf16[384,768]{1,0:T(8,128)(2,1)S(1)} %get-tuple-element.26.sent_x), channel_id=1, source_target_pairs={{1,2},{2,1},{3,4},{4,3},{5,6},{6,5},{7,8},{8,7},{9,10},{10,9},{11,... | collective-permute-start | bytes 1769480 | tf_op jit(solution)/shard_map/ppermute | solution.py:260
  26.7 2.1 %shard_map.81.y_in = bf16[256,2304]{1,0:T(8,128)(2,1)S(1)} custom-call(s32[1]{0:T(128)} %bitcast.index, bf16[1536,2304]{1,0:T(8,128)(2,1)S(1)} %get-tuple-element.18.dense, bf16[1536,256]{1,0:T(8,128)(2,1)S(1)} %get-tuple-element.22.p_x), custom_call_target="tpu_custom_call" | custom-call | flops 2415919104 | bytes 7864324 | tf_op jit(solution)/shard_map/pallas_call | solution.py:25
  28.8 0.8 %shard_map.82 = (bf16[256,2304]{1,0:T(8,128)(2,1)S(1)}, f32[256,768]{1,0:T(8,128)S(1)}) custom-call(s32[1]{0:T(128)} %bitcast.index, bf16[1536,2304]{1,0:T(8,128)(2,1)S(1)} %get-tuple-element.18.dense, bf16[1536,256]{1,0:T(8,128)(2,1)S(1)} %shard_map.75.p_s, bf16[1536,256]{1,0:T(8,128)(2,1)S(1)} %get-tuple-element.21.p_own, ...), custom_call_target="tpu_custom_call", output_to_operand_aliasing={{0}: (5, {})} | custom-call | flops 2415919104 | bytes 10616836 | tf_op jit(solution)/shard_map/pallas_call | solution.py:25
  29.6 0.0 collective-permute-done.2.far_s
  29.6 0.4 shard_map.83
  30.0 2.5 %collective-permute-start.5 = (bf16[256,1408]{1,0:T(8,128)(2,1)S(1)}, bf16[256,1408]{1,0:T(8,128)(2,1)S(1)}, u32[]{:S(2)}, u32[]{:S(2)}) collective-permute-start(bf16[256,1408]{1,0:T(8,128)(2,1)S(1)} %shard_map.83), channel_id=1, source_target_pairs={{1,2},{2,1},{3,4},{4,3},{5,6},{6,5},{7,8},{8,7},{9,10},{10,9},{11,... | collective-permute-start | bytes 2162696 | tf_op jit(solution)/shard_map/ppermute | solution.py:260
  32.4 2.6 %shard_map.78 = (bf16[256,2304]{1,0:T(8,128)(2,1)S(1)}, f32[256,768]{1,0:T(8,128)S(1)}) custom-call(bf16[1536,2304]{1,0:T(8,128)(2,1)S(1)} %get-tuple-element.18.dense, bf16[1536,256]{1,0:T(8,128)(2,1)S(1)} %shard_map.75.p_s, bf16[1536,256]{1,0:T(8,128)(2,1)S(1)} %get-tuple-element.21.p_own, bf16[1536,256]{1,0:T(8,128)(2,1)S(1)} %get-tuple-element.22.p_x), custom_call_target="tpu_custom_call" | custom-call | flops 2415919104 | bytes 9437184 | tf_op jit(solution)/shard_map/pallas_call | solution.py:25
  35.1 0.0 collective-permute-done.3.far_x
  35.1 0.6 %shard_map.79 = bf16[256,1280]{1,0:T(8,128)(2,1)S(1)} custom-call(f32[256,768]{1,0:T(8,128)S(1)} %get-tuple-element.27.gal, bf16[256,2304]{1,0:T(8,128)(2,1)S(1)} %get-tuple-element.28.y, bf16[384,768]{1,0:T(8,128)(2,1)S(1)} %collective-permute-done.2.far_s, bf16[384,768]{1,0:T(8,128)(2,1)S(1)} %collective-permute-done.3.far_x), custom_call_target="tpu_custom_call" | custom-call | flops 301989888 | bytes 3145728 | tf_op jit(solution)/shard_map/pallas_call | solution.py:25
  35.7 0.3 collective-permute-start.4
  36.0 2.7 %shard_map.77 = (bf16[256,2304]{1,0:T(8,128)(2,1)S(1)}, f32[256,768]{1,0:T(8,128)S(1)}) custom-call(bf16[1536,2304]{1,0:T(8,128)(2,1)S(1)} %get-tuple-element.18.dense, bf16[1536,256]{1,0:T(8,128)(2,1)S(1)} %shard_map.75.p_s, bf16[1536,256]{1,0:T(8,128)(2,1)S(1)} %get-tuple-element.21.p_own, bf16[1536,256]{1,0:T(8,128)(2,1)S(1)} %get-tuple-element.22.p_x), custom_call_target="tpu_custom_call" | custom-call | flops 2415919104 | bytes 9437184 | tf_op jit(solution)/shard_map/pallas_call | solution.py:25
  38.6 0.0 collective-permute-done.4.from_s
  38.6 0.6 %shard_map.80.mine = f32[256,1792]{1,0:T(8,128)S(1)} custom-call(f32[256,768]{1,0:T(8,128)S(1)} %get-tuple-element.23.gal, bf16[256,2304]{1,0:T(8,128)(2,1)S(1)} %get-tuple-element.24.y, bf16[384,768]{1,0:T(8,128)(2,1)S(1)} %collective-permute-done.2.far_s, bf16[384,768]{1,0:T(8,128)(2,1)S(1)} %collective-permute-done.3.far_x, ...), custom_call_target="tpu_custom_call" | custom-call | flops 301989888 | bytes 3801088 | tf_op jit(solution)/shard_map/pallas_call | solution.py:25
  39.2 7.6 %collective-permute-done.5.from_x = bf16[256,1408]{1,0:T(8,128)(2,1)S(1)} collective-permute-done((bf16[256,1408]{1,0:T(8,128)(2,1)S(1)}, bf16[256,1408]{1,0:T(8,128)(2,1)S(1)}, u32[]{:S(2)}, u32[]{:S(2)}) %collective-permute-start.5) | collective-permute-done | bytes 720928 | tf_op jit(solution)/shard_map/ppermute | solution.py:260
  46.8 1.2 %shard_map.84 = bf16[256,1792]{1,0:T(8,128)(2,1)} custom-call(s32[1]{0:T(128)} %bitcast.index, f32[256,1792]{1,0:T(8,128)S(1)} %shard_map.80.mine, bf16[384,768]{1,0:T(8,128)(2,1)S(1)} %get-tuple-element.26.sent_x, bf16[256,1408]{1,0:T(8,128)(2,1)S(1)} %collective-permute-done.5.from_x), custom_call_target="tpu_custom_call" | custom-call | flops 150994944 | bytes 3145732 | tf_op jit(solution)/shard_map/pallas_call | solution.py:25
Async XLA Ops:
  1.0 15.3 %collective-permute-start = (bf16[1568,128]{1,0:T(8,128)(2,1)S(1)}, bf16[1568,128]{1,0:T(8,128)(2,1)S(1)}, u32[]{:S(2)}, u32[]{:S(2)}) collective-permute-start(bf16[1568,128]{1,0:T(8,128)(2,1)S(1)} %shard_map.73.pay), channel_id=1, source_target_pairs={{0,1},{1,0},{2,3},{3,2},{4,5},{5,4},{6,7},{7,6},{8,9},{9,8},{10,11... | collective-permute-start | bytes 1204232 | tf_op jit(solution)/shard_map/ppermute | solution.py:260
  1.1 16.7 %collective-permute-start.1 = (bf16[1568,128]{1,0:T(8,128)(2,1)S(1)}, bf16[1568,128]{1,0:T(8,128)(2,1)S(1)}, u32[]{:S(2)}, u32[]{:S(2)}) collective-permute-start(bf16[1568,128]{1,0:T(8,128)(2,1)S(1)} %shard_map.73.pay), channel_id=1, source_target_pairs={{1,2},{2,1},{3,4},{4,3},{5,6},{6,5},{7,8},{8,7},{9,10},{10,9},{11,... | collective-permute-start | bytes 1204232 | tf_op jit(solution)/shard_map/ppermute | solution.py:260
  12.4 4.0 %copy-start = (s32[1,2,3]{2,1,0:T(2,128)S(1)}, s32[1,2,3]{2,1,0:T(2,128)}, u32[]{:S(2)}) copy-start(s32[1,2,3]{2,1,0:T(2,128)} %ghost.3) | copy-start | bytes 76
  19.3 10.3 %collective-permute-start.2 = (bf16[384,768]{1,0:T(8,128)(2,1)S(1)}, bf16[384,768]{1,0:T(8,128)(2,1)S(1)}, u32[]{:S(2)}, u32[]{:S(2)}) collective-permute-start(bf16[384,768]{1,0:T(8,128)(2,1)S(1)} %get-tuple-element.25), channel_id=1, source_target_pairs={{0,1},{1,0},{2,3},{3,2},{4,5},{5,4},{6,7},{7,6},{8,9},{9,8},{10,11... | collective-permute-start | bytes 1769480 | tf_op jit(solution)/shard_map/ppermute | solution.py:260
  19.4 15.7 %collective-permute-start.3 = (bf16[384,768]{1,0:T(8,128)(2,1)S(1)}, bf16[384,768]{1,0:T(8,128)(2,1)S(1)}, u32[]{:S(2)}, u32[]{:S(2)}) collective-permute-start(bf16[384,768]{1,0:T(8,128)(2,1)S(1)} %get-tuple-element.26.sent_x), channel_id=1, source_target_pairs={{1,2},{2,1},{3,4},{4,3},{5,6},{6,5},{7,8},{8,7},{9,10},{10,9},{11,... | collective-permute-start | bytes 1769480 | tf_op jit(solution)/shard_map/ppermute | solution.py:260
  30.0 16.8 %collective-permute-start.5 = (bf16[256,1408]{1,0:T(8,128)(2,1)S(1)}, bf16[256,1408]{1,0:T(8,128)(2,1)S(1)}, u32[]{:S(2)}, u32[]{:S(2)}) collective-permute-start(bf16[256,1408]{1,0:T(8,128)(2,1)S(1)} %shard_map.83), channel_id=1, source_target_pairs={{1,2},{2,1},{3,4},{4,3},{5,6},{6,5},{7,8},{8,7},{9,10},{10,9},{11,... | collective-permute-start | bytes 2162696 | tf_op jit(solution)/shard_map/ppermute | solution.py:260
  35.7 2.9 %collective-permute-start.4 = (bf16[256,1280]{1,0:T(8,128)(2,1)S(1)}, bf16[256,1280]{1,0:T(8,128)(2,1)S(1)}, u32[]{:S(2)}, u32[]{:S(2)}) collective-permute-start(bf16[256,1280]{1,0:T(8,128)(2,1)S(1)} %shard_map.79), channel_id=1, source_target_pairs={{0,1},{1,0},{2,3},{3,2},{4,5},{5,4},{6,7},{7,6},{8,9},{9,8},{10,11... | collective-permute-start | bytes 1966088 | tf_op jit(solution)/shard_map/ppermute | solution.py:260

commit v10 on v9

--- a/solution.py
+++ b/solution.py
@@ -77,10 +77,16 @@
         target[at, :] = value.astype(BF16)
 
 
+def to_row(line, r):
+    return jnp.clip(jnp.max(line).astype(jnp.int32), 0, r - 1)
+
+
 def place_ghosts(r, b, s, ghost, mine, pay, meta, placed):
     meta[...] = pay[r * b :, :].astype(F32)
+    line = ghost[0, pl.ds(mine, 1), :].astype(F32)
+    lane = lax.broadcasted_iota(jnp.int32, line.shape, 1)
     for j in range(s):
-        row = jnp.clip(ghost[0, mine, j], 0, r - 1)
+        row = to_row(jnp.where(lane == j, line, 0.0), r)
         block = pay[rows(row, b), :]
         here = jnp.broadcast_to(meta[pl.ds(row, 1), :], (b, b))
         for c in range(CA):
@@ -90,8 +96,7 @@
 def wanted_rows(r, s, theirs, meta):
     found = []
     for j in range(s):
-        value = jnp.max(meta[pl.ds(16 + 8 * theirs + j, 1), :])
-        found.append(jnp.clip(value.astype(jnp.int32), 0, r - 1))
+        found.append(to_row(meta[pl.ds(16 + 8 * theirs + j, 1), :], r))
     return found
 
 
@@ -241,14 +246,13 @@
 
 def final_kernel(w, index, mine, sent_x, from_x, out_hbm, out, sems):
     sign = 1 - 2 * (index[0] & 1)
-    back = dot(from_x[:, 4 * w :], sent_x[...])
     copies = []
     for u in (3, 2, -3, -2, -1, 0, 1):
         total = mine[:, (3 - u) * w : (4 - u) * w]
         if 0 <= 3 + u < 4:
             total = total + from_x[:, (3 + u) * w : (4 + u) * w].astype(F32)
         if abs(u) < 2:
-            total = total + back[:, (1 - u) * w : (2 - u) * w]
+            total = total + dot(from_x[:, 4 * w :], sent_x[:, (1 - u) * w : (2 - u) * w])
         out[u + 3, :, :] = total.astype(BF16)
         copies.append(pltpu.make_async_copy(out.at[u + 3], out_hbm.at[:, rows(3 + sign * u, w)], sems.at[u + 3]))
         copies[-1].start()
@@ -296,13 +300,13 @@
         flops=2 * r * b * r * b * w, limit=24 << 20,
     )
     (p_s,) = call(
-        functools.partial(near_kernel, r, b, s), (ghost_rows, index, damp, dense, inv, pay_s), "ssvvvv",
+        functools.partial(near_kernel, r, b, s), (ghost_rows, index, damp, dense, inv, pay_s), "vsvvvv",
         [((r * b, w), BF16)], scratch=[VMEM((META, b), F32), VMEM((span, w), BF16), VMEM((r * b, w), BF16)],
         flops=2 * r * b * span * w, limit=24 << 20,
     )
     p_x, out_x, out_s = call(
         functools.partial(far_kernel, r, b, s, w),
-        (ghost_rows, index, damp, dense, inv, p_s, p_own, pay_s, pay_x), "ssvvvvvvv",
+        (ghost_rows, index, damp, dense, inv, p_s, p_own, pay_s, pay_x), "vsvvvvvvv",
         [((r * b, w), BF16), ((span, 3 * w), BF16), ((span, 3 * w), BF16)],
         scratch=[VMEM((META, b), F32), VMEM((META, b), F32), VMEM((span, w), BF16), VMEM((r * b, w), BF16)],
         flops=2 * r * b * span * w, limit=24 << 20,

time: 48.3 us -> 47.9 us (level)
  Pallas kernels: 18.7 us -> 17.9 us
    pallas_call x12, Pallas kernels: 18.7 us -> 17.9 us  [call(): pl.pallas_call(kernel, out_shape=[jax.ShapeDtypeStruct(*o) for o in outs]...]
where the time goes in v10:
time: 47.9 us; the launch traced here: 47.7 us
  starting transfers between devices  20.8 us (43%)
  Pallas kernels  17.9 us (37%)
  waiting for transfers between devices  7.98 us (17%)
  between operations  0.99 us (2%)
    ppermute x6, starting transfers between devices, swap(): return lax.ppermute(x, AXES, route)  20.8 us
    pallas_call x12, Pallas kernels, call(): pl.pallas_call(kernel, out_shape=[jax.ShapeDtypeStruct(*o) for o in outs]...  17.9 us
    ppermute x6, waiting for transfers between devices, swap(): return lax.ppermute(x, AXES, route)  7.98 us
  transfers between devices with their start and end apart: 6, of which 1 were waited for; matrix products, arithmetic and copies ran while one was open for 0% of the time, Pallas kernels for 31%

profile of v10, /device:TPU:6, one launch (start us, length us, event | category | flops | bytes accessed | tf_op | source)
XLA Modules:
  0.0 47.7 jit_solution(17004748910583517432)
XLA Ops:
  0.0 1.0 %shard_map.73.pay = bf16[1568,128]{1,0:T(8,128)(2,1)S(1)} custom-call(s32[12]{0:T(128)} %agg_hbm.3, s32[1,2,3]{2,1,0:T(2,128)} %ghost.3, bf16[1536,128]{1,0:T(8,128)(2,1)} %bitcast.4), custom_call_target="tpu_custom_call" | custom-call | flops 1 | bytes 393288 | tf_op jit(solution)/shard_map/pallas_call | solution.py:25
  1.0 0.1 collective-permute-start
  1.1 10.6 %collective-permute-start.1 = (bf16[1568,128]{1,0:T(8,128)(2,1)S(1)}, bf16[1568,128]{1,0:T(8,128)(2,1)S(1)}, u32[]{:S(2)}, u32[]{:S(2)}) collective-permute-start(bf16[1568,128]{1,0:T(8,128)(2,1)S(1)} %shard_map.73.pay), channel_id=1, source_target_pairs={{1,2},{2,1},{3,4},{4,3},{5,6},{6,5},{7,8},{8,7},{9,10},{10,9},{11,... | collective-permute-start | bytes 1204232 | tf_op jit(solution)/shard_map/ppermute | solution.py:264
  12.4 0.0 copy-start
  12.4 3.9 %shard_map.74 = (bf16[1536,2304]{1,0:T(8,128)(2,1)S(1)}, bf16[1536,128]{1,0:T(8,128)(2,1)S(1)}, bf16[1536,256]{1,0:T(8,128)(2,1)S(1)}, f32[8,256]{1,0:T(8,128)S(1)}) custom-call(s32[1]{0:T(128)} %bitcast.index, f32[1]{0:T(128)S(6)} %copy.10.damp_in, s32[12]{0:T(128)} %agg_hbm.3, s32[12,9]{1,0:T(8,128)} %cols_hbm.1, bf16[1536,128]{1,0:T(8,128)(2,1)} %bitcast.5, ...), custom_call_target="tpu_custom_call" | custom-call | flops 1207959552 | bytes 4334056 | tf_op jit(solution)/shard_map/pallas_call | solution.py:25
  16.3 0.0 collective-permute-done.pay.pay_s
  16.3 0.0 copy-done
  16.3 1.0 %shard_map.75.p_s = bf16[1536,256]{1,0:T(8,128)(2,1)S(1)} custom-call(s32[1,2,3]{2,1,0:T(2,128)S(1)} %copy-done, s32[1]{0:T(128)} %bitcast.index, f32[8,256]{1,0:T(8,128)S(1)} %get-tuple-element.19.damp, bf16[1536,2304]{1,0:T(8,128)(2,1)S(1)} %get-tuple-element.18.dense, bf16[1536,128]{1,0:T(8,128)(2,1)S(1)} %get-tuple-element.20.inv, ...), custom_call_target="tpu_custom_call" | custom-call | flops 301989888 | bytes 7880732 | tf_op jit(solution)/shard_map/pallas_call | solution.py:25
  17.4 0.0 collective-permute-done.1.pay_x
  17.4 1.0 %shard_map.76 = (bf16[1536,256]{1,0:T(8,128)(2,1)S(1)}, bf16[384,768]{1,0:T(8,128)(2,1)S(1)}, bf16[384,768]{1,0:T(8,128)(2,1)S(1)}) custom-call(s32[1,2,3]{2,1,0:T(2,128)S(1)} %copy-done, s32[1]{0:T(128)} %bitcast.index, f32[8,256]{1,0:T(8,128)S(1)} %get-tuple-element.19.damp, bf16[1536,2304]{1,0:T(8,128)(2,1)S(1)} %get-tuple-element.18.dense, ...), custom_call_target="tpu_custom_call" | custom-call | flops 301989888 | bytes 9855004 | tf_op jit(solution)/shard_map/pallas_call | solution.py:25
  18.4 0.1 collective-permute-start.2
  18.5 7.7 %collective-permute-start.3 = (bf16[384,768]{1,0:T(8,128)(2,1)S(1)}, bf16[384,768]{1,0:T(8,128)(2,1)S(1)}, u32[]{:S(2)}, u32[]{:S(2)}) collective-permute-start(bf16[384,768]{1,0:T(8,128)(2,1)S(1)} %get-tuple-element.26.sent_x), channel_id=1, source_target_pairs={{1,2},{2,1},{3,4},{4,3},{5,6},{6,5},{7,8},{8,7},{9,10},{10,9},{11,... | collective-permute-start | bytes 1769480 | tf_op jit(solution)/shard_map/ppermute | solution.py:264
  26.3 2.1 %shard_map.81.y_in = bf16[256,2304]{1,0:T(8,128)(2,1)S(1)} custom-call(s32[1]{0:T(128)} %bitcast.index, bf16[1536,2304]{1,0:T(8,128)(2,1)S(1)} %get-tuple-element.18.dense, bf16[1536,256]{1,0:T(8,128)(2,1)S(1)} %get-tuple-element.22.p_x), custom_call_target="tpu_custom_call" | custom-call | flops 2415919104 | bytes 7864324 | tf_op jit(solution)/shard_map/pallas_call | solution.py:25
  28.4 0.8 %shard_map.82 = (bf16[256,2304]{1,0:T(8,128)(2,1)S(1)}, f32[256,768]{1,0:T(8,128)S(1)}) custom-call(s32[1]{0:T(128)} %bitcast.index, bf16[1536,2304]{1,0:T(8,128)(2,1)S(1)} %get-tuple-element.18.dense, bf16[1536,256]{1,0:T(8,128)(2,1)S(1)} %shard_map.75.p_s, bf16[1536,256]{1,0:T(8,128)(2,1)S(1)} %get-tuple-element.21.p_own, ...), custom_call_target="tpu_custom_call", output_to_operand_aliasing={{0}: (5, {})} | custom-call | flops 2415919104 | bytes 10616836 | tf_op jit(solution)/shard_map/pallas_call | solution.py:25
  29.2 0.0 collective-permute-done.2.far_s
  29.2 0.4 shard_map.83
  29.5 2.1 %collective-permute-start.5 = (bf16[256,1408]{1,0:T(8,128)(2,1)S(1)}, bf16[256,1408]{1,0:T(8,128)(2,1)S(1)}, u32[]{:S(2)}, u32[]{:S(2)}) collective-permute-start(bf16[256,1408]{1,0:T(8,128)(2,1)S(1)} %shard_map.83), channel_id=1, source_target_pairs={{1,2},{2,1},{3,4},{4,3},{5,6},{6,5},{7,8},{8,7},{9,10},{10,9},{11,... | collective-permute-start | bytes 2162696 | tf_op jit(solution)/shard_map/ppermute | solution.py:264
  31.6 2.7 %shard_map.78 = (bf16[256,2304]{1,0:T(8,128)(2,1)S(1)}, f32[256,768]{1,0:T(8,128)S(1)}) custom-call(bf16[1536,2304]{1,0:T(8,128)(2,1)S(1)} %get-tuple-element.18.dense, bf16[1536,256]{1,0:T(8,128)(2,1)S(1)} %shard_map.75.p_s, bf16[1536,256]{1,0:T(8,128)(2,1)S(1)} %get-tuple-element.21.p_own, bf16[1536,256]{1,0:T(8,128)(2,1)S(1)} %get-tuple-element.22.p_x), custom_call_target="tpu_custom_call" | custom-call | flops 2415919104 | bytes 9437184 | tf_op jit(solution)/shard_map/pallas_call | solution.py:25
  34.3 0.0 collective-permute-done.3.far_x
  34.3 0.6 %shard_map.79 = bf16[256,1280]{1,0:T(8,128)(2,1)S(1)} custom-call(f32[256,768]{1,0:T(8,128)S(1)} %get-tuple-element.27.gal, bf16[256,2304]{1,0:T(8,128)(2,1)S(1)} %get-tuple-element.28.y, bf16[384,768]{1,0:T(8,128)(2,1)S(1)} %collective-permute-done.2.far_s, bf16[384,768]{1,0:T(8,128)(2,1)S(1)} %collective-permute-done.3.far_x), custom_call_target="tpu_custom_call" | custom-call | flops 301989888 | bytes 3145728 | tf_op jit(solution)/shard_map/pallas_call | solution.py:25
  34.9 0.3 collective-permute-start.4
  35.1 2.7 %shard_map.77 = (bf16[256,2304]{1,0:T(8,128)(2,1)S(1)}, f32[256,768]{1,0:T(8,128)S(1)}) custom-call(bf16[1536,2304]{1,0:T(8,128)(2,1)S(1)} %get-tuple-element.18.dense, bf16[1536,256]{1,0:T(8,128)(2,1)S(1)} %shard_map.75.p_s, bf16[1536,256]{1,0:T(8,128)(2,1)S(1)} %get-tuple-element.21.p_own, bf16[1536,256]{1,0:T(8,128)(2,1)S(1)} %get-tuple-element.22.p_x), custom_call_target="tpu_custom_call" | custom-call | flops 2415919104 | bytes 9437184 | tf_op jit(solution)/shard_map/pallas_call | solution.py:25
  37.8 0.0 collective-permute-done.4.from_s
  37.8 0.6 %shard_map.80.mine = f32[256,1792]{1,0:T(8,128)S(1)} custom-call(f32[256,768]{1,0:T(8,128)S(1)} %get-tuple-element.23.gal, bf16[256,2304]{1,0:T(8,128)(2,1)S(1)} %get-tuple-element.24.y, bf16[384,768]{1,0:T(8,128)(2,1)S(1)} %collective-permute-done.2.far_s, bf16[384,768]{1,0:T(8,128)(2,1)S(1)} %collective-permute-done.3.far_x, ...), custom_call_target="tpu_custom_call" | custom-call | flops 301989888 | bytes 3801088 | tf_op jit(solution)/shard_map/pallas_call | solution.py:25
  38.4 8.0 %collective-permute-done.5.from_x = bf16[256,1408]{1,0:T(8,128)(2,1)S(1)} collective-permute-done((bf16[256,1408]{1,0:T(8,128)(2,1)S(1)}, bf16[256,1408]{1,0:T(8,128)(2,1)S(1)}, u32[]{:S(2)}, u32[]{:S(2)}) %collective-permute-start.5) | collective-permute-done | bytes 720928 | tf_op jit(solution)/shard_map/ppermute | solution.py:264
  46.4 1.2 %shard_map.84 = bf16[256,1792]{1,0:T(8,128)(2,1)} custom-call(s32[1]{0:T(128)} %bitcast.index, f32[256,1792]{1,0:T(8,128)S(1)} %shard_map.80.mine, bf16[384,768]{1,0:T(8,128)(2,1)S(1)} %get-tuple-element.26.sent_x, bf16[256,1408]{1,0:T(8,128)(2,1)S(1)} %collective-permute-done.5.from_x), custom_call_target="tpu_custom_call" | custom-call | flops 150994944 | bytes 3145732 | tf_op jit(solution)/shard_map/pallas_call | solution.py:25
Async XLA Ops:
  1.0 15.3 %collective-permute-start = (bf16[1568,128]{1,0:T(8,128)(2,1)S(1)}, bf16[1568,128]{1,0:T(8,128)(2,1)S(1)}, u32[]{:S(2)}, u32[]{:S(2)}) collective-permute-start(bf16[1568,128]{1,0:T(8,128)(2,1)S(1)} %shard_map.73.pay), channel_id=1, source_target_pairs={{0,1},{1,0},{2,3},{3,2},{4,5},{5,4},{6,7},{7,6},{8,9},{9,8},{10,11... | collective-permute-start | bytes 1204232 | tf_op jit(solution)/shard_map/ppermute | solution.py:264
  1.1 16.2 %collective-permute-start.1 = (bf16[1568,128]{1,0:T(8,128)(2,1)S(1)}, bf16[1568,128]{1,0:T(8,128)(2,1)S(1)}, u32[]{:S(2)}, u32[]{:S(2)}) collective-permute-start(bf16[1568,128]{1,0:T(8,128)(2,1)S(1)} %shard_map.73.pay), channel_id=1, source_target_pairs={{1,2},{2,1},{3,4},{4,3},{5,6},{6,5},{7,8},{8,7},{9,10},{10,9},{11,... | collective-permute-start | bytes 1204232 | tf_op jit(solution)/shard_map/ppermute | solution.py:264
  12.4 4.0 %copy-start = (s32[1,2,3]{2,1,0:T(2,128)S(1)}, s32[1,2,3]{2,1,0:T(2,128)}, u32[]{:S(2)}) copy-start(s32[1,2,3]{2,1,0:T(2,128)} %ghost.3) | copy-start | bytes 76
  18.4 10.7 %collective-permute-start.2 = (bf16[384,768]{1,0:T(8,128)(2,1)S(1)}, bf16[384,768]{1,0:T(8,128)(2,1)S(1)}, u32[]{:S(2)}, u32[]{:S(2)}) collective-permute-start(bf16[384,768]{1,0:T(8,128)(2,1)S(1)} %get-tuple-element.25), channel_id=1, source_target_pairs={{0,1},{1,0},{2,3},{3,2},{4,5},{5,4},{6,7},{7,6},{8,9},{9,8},{10,11... | collective-permute-start | bytes 1769480 | tf_op jit(solution)/shard_map/ppermute | solution.py:264
  18.5 15.8 %collective-permute-start.3 = (bf16[384,768]{1,0:T(8,128)(2,1)S(1)}, bf16[384,768]{1,0:T(8,128)(2,1)S(1)}, u32[]{:S(2)}, u32[]{:S(2)}) collective-permute-start(bf16[384,768]{1,0:T(8,128)(2,1)S(1)} %get-tuple-element.26.sent_x), channel_id=1, source_target_pairs={{1,2},{2,1},{3,4},{4,3},{5,6},{6,5},{7,8},{8,7},{9,10},{10,9},{11,... | collective-permute-start | bytes 1769480 | tf_op jit(solution)/shard_map/ppermute | solution.py:264
  29.5 16.8 %collective-permute-start.5 = (bf16[256,1408]{1,0:T(8,128)(2,1)S(1)}, bf16[256,1408]{1,0:T(8,128)(2,1)S(1)}, u32[]{:S(2)}, u32[]{:S(2)}) collective-permute-start(bf16[256,1408]{1,0:T(8,128)(2,1)S(1)} %shard_map.83), channel_id=1, source_target_pairs={{1,2},{2,1},{3,4},{4,3},{5,6},{6,5},{7,8},{8,7},{9,10},{10,9},{11,... | collective-permute-start | bytes 2162696 | tf_op jit(solution)/shard_map/ppermute | solution.py:264
  34.9 2.9 %collective-permute-start.4 = (bf16[256,1280]{1,0:T(8,128)(2,1)S(1)}, bf16[256,1280]{1,0:T(8,128)(2,1)S(1)}, u32[]{:S(2)}, u32[]{:S(2)}) collective-permute-start(bf16[256,1280]{1,0:T(8,128)(2,1)S(1)} %shard_map.79), channel_id=1, source_target_pairs={{0,1},{1,0},{2,3},{3,2},{4,5},{5,4},{6,7},{7,6},{8,9},{9,8},{10,11... | collective-permute-start | bytes 1966088 | tf_op jit(solution)/shard_map/ppermute | solution.py:264

commit v11 on v10

--- a/solution.py
+++ b/solution.py
@@ -171,18 +171,20 @@
     return (lax.rem(index[0], group) == 0) & (index[0] > 0)
 
 
-def ahead_kernel(group, r, b, index, dense, p_x, y, flipped):
+def ahead_kernel(group, r, b, w, index, dense, p_s, p_x, y, gal, flipped):
     @pl.when(opens_group(index, group))
     def _():
         left_product(r, b, dense, p_x, y, flipped)
-
-
-def cross_kernel(group, r, b, w, index, dense, p_s, p_own, p_x, y_in, y, gal, flipped):
+        right_product(r, b, w, (p_s,), y, gal)
+
+
+def cross_kernel(group, r, b, w, index, dense, p_s, p_own, p_x, y_in, gal_in, y, gal, flipped):
     @pl.when(jnp.logical_not(opens_group(index, group)))
     def _():
         left_product(r, b, dense, p_x, y, flipped)
-
-    right_product(r, b, w, (p_s, p_own, p_x), y, gal)
+        right_product(r, b, w, (p_s,), y, gal)
+
+    right_product(r, b, w, (p_own, p_x), y, gal, 1)
 
 
 def outer_kernel(w, span, gal, y, far_s, out):
@@ -206,8 +208,8 @@
     y[...] = dot(flipped[...], dense[...]).astype(BF16)
 
 
-def right_product(r, b, w, parts, y, gal):
-    for d, other in enumerate(parts):
+def right_product(r, b, w, parts, y, gal, first=0):
+    for d, other in enumerate(parts, first):
         gal[:, d * w : (d + 1) * w] = dot(y[:, : r * b], other[...])
 
 
@@ -246,13 +248,14 @@
 
 def final_kernel(w, index, mine, sent_x, from_x, out_hbm, out, sems):
     sign = 1 - 2 * (index[0] & 1)
+    back = dot(from_x[:, 4 * w :], sent_x[...])
     copies = []
     for u in (3, 2, -3, -2, -1, 0, 1):
         total = mine[:, (3 - u) * w : (4 - u) * w]
         if 0 <= 3 + u < 4:
             total = total + from_x[:, (3 + u) * w : (4 + u) * w].astype(F32)
         if abs(u) < 2:
-            total = total + dot(from_x[:, 4 * w :], sent_x[:, (1 - u) * w : (2 - u) * w])
+            total = total + back[:, (1 - u) * w : (2 - u) * w]
         out[u + 3, :, :] = total.astype(BF16)
         copies.append(pltpu.make_async_copy(out.at[u + 3], out_hbm.at[:, rows(3 + sign * u, w)], sems.at[u + 3]))
         copies[-1].start()
@@ -316,13 +319,13 @@
     shapes = [((w, total), BF16), ((w, 3 * w), F32)]
     scratch = [VMEM((w, r * b), BF16)]
     flops = 2 * r * b * r * b * 2 * w
-    (y_x,) = call(
-        functools.partial(ahead_kernel, group, r, b), (index, dense, p_x), "svv",
-        shapes[:1], scratch=scratch, flops=flops, limit=24 << 20,
-    )
     y_x, gal_x = call(
-        functools.partial(cross_kernel, group, r, b, w), (index, dense, p_s, p_own, p_x, y_x), "svvvvv",
-        shapes, scratch=scratch, flops=flops, limit=24 << 20, aliases={5: 0},
+        functools.partial(ahead_kernel, group, r, b, w), (index, dense, p_s, p_x), "svvv",
+        shapes, scratch=scratch, flops=flops, limit=24 << 20,
+    )
+    y_x, gal_x = call(
+        functools.partial(cross_kernel, group, r, b, w), (index, dense, p_s, p_own, p_x, y_x, gal_x), "svvvvvv",
+        shapes, scratch=scratch, flops=flops, limit=24 << 20, aliases={5: 0, 6: 1},
     )
     (sum_x,) = call(
         functools.partial(outer_kernel, w, span), (gal_x, y_x, far_s), "vvv",

time: 47.9 us -> 47.9 us (level)
  no operation moved by 1% of the time
where the time goes in v11:
time: 47.9 us; the launch traced here: 47.7 us
  starting transfers between devices  20.8 us (43%)
  Pallas kernels  17.9 us (37%)
  waiting for transfers between devices  7.99 us (17%)
  between operations  0.99 us (2%)
    ppermute x6, starting transfers between devices, swap(): return lax.ppermute(x, AXES, route)  20.8 us
    pallas_call x12, Pallas kernels, call(): pl.pallas_call(kernel, out_shape=[jax.ShapeDtypeStruct(*o) for o in outs]...  17.9 us
    ppermute x6, waiting for transfers between devices, swap(): return lax.ppermute(x, AXES, route)  7.99 us
  transfers between devices with their start and end apart: 6, of which 1 were waited for; matrix products, arithmetic and copies ran while one was open for 0% of the time, Pallas kernels for 31%

profile of v11, /device:TPU:6, one launch (start us, length us, event | category | flops | bytes accessed | tf_op | source)
XLA Modules:
  0.0 47.7 jit_solution(17384405827967469266)
XLA Ops:
  0.0 1.0 %shard_map.73.pay = bf16[1568,128]{1,0:T(8,128)(2,1)S(1)} custom-call(s32[12]{0:T(128)} %agg_hbm.3, s32[1,2,3]{2,1,0:T(2,128)} %ghost.3, bf16[1536,128]{1,0:T(8,128)(2,1)} %bitcast.4), custom_call_target="tpu_custom_call" | custom-call | flops 1 | bytes 393288 | tf_op jit(solution)/shard_map/pallas_call | solution.py:25
  1.0 0.1 collective-permute-start
  1.1 10.6 %collective-permute-start.1 = (bf16[1568,128]{1,0:T(8,128)(2,1)S(1)}, bf16[1568,128]{1,0:T(8,128)(2,1)S(1)}, u32[]{:S(2)}, u32[]{:S(2)}) collective-permute-start(bf16[1568,128]{1,0:T(8,128)(2,1)S(1)} %shard_map.73.pay), channel_id=1, source_target_pairs={{1,2},{2,1},{3,4},{4,3},{5,6},{6,5},{7,8},{8,7},{9,10},{10,9},{11,... | collective-permute-start | bytes 1204232 | tf_op jit(solution)/shard_map/ppermute | solution.py:267
  12.4 0.0 copy-start
  12.4 3.9 %shard_map.74 = (bf16[1536,2304]{1,0:T(8,128)(2,1)S(1)}, bf16[1536,128]{1,0:T(8,128)(2,1)S(1)}, bf16[1536,256]{1,0:T(8,128)(2,1)S(1)}, f32[8,256]{1,0:T(8,128)S(1)}) custom-call(s32[1]{0:T(128)} %bitcast.index, f32[1]{0:T(128)S(6)} %copy.12.damp_in, s32[12]{0:T(128)} %agg_hbm.3, s32[12,9]{1,0:T(8,128)} %cols_hbm.1, bf16[1536,128]{1,0:T(8,128)(2,1)} %bitcast.5, ...), custom_call_target="tpu_custom_call" | custom-call | flops 1207959552 | bytes 4334056 | tf_op jit(solution)/shard_map/pallas_call | solution.py:25
  16.3 0.0 collective-permute-done.pay.pay_s
  16.3 0.0 copy-done
  16.3 1.0 %shard_map.75.p_s = bf16[1536,256]{1,0:T(8,128)(2,1)S(1)} custom-call(s32[1,2,3]{2,1,0:T(2,128)S(1)} %copy-done, s32[1]{0:T(128)} %bitcast.index, f32[8,256]{1,0:T(8,128)S(1)} %get-tuple-element.21.damp, bf16[1536,2304]{1,0:T(8,128)(2,1)S(1)} %get-tuple-element.20.dense, bf16[1536,128]{1,0:T(8,128)(2,1)S(1)} %get-tuple-element.22.inv, ...), custom_call_target="tpu_custom_call" | custom-call | flops 301989888 | bytes 7880732 | tf_op jit(solution)/shard_map/pallas_call | solution.py:25
  17.4 0.0 collective-permute-done.1.pay_x
  17.4 1.0 %shard_map.76 = (bf16[1536,256]{1,0:T(8,128)(2,1)S(1)}, bf16[384,768]{1,0:T(8,128)(2,1)S(1)}, bf16[384,768]{1,0:T(8,128)(2,1)S(1)}) custom-call(s32[1,2,3]{2,1,0:T(2,128)S(1)} %copy-done, s32[1]{0:T(128)} %bitcast.index, f32[8,256]{1,0:T(8,128)S(1)} %get-tuple-element.21.damp, bf16[1536,2304]{1,0:T(8,128)(2,1)S(1)} %get-tuple-element.20.dense, ...), custom_call_target="tpu_custom_call" | custom-call | flops 301989888 | bytes 9855004 | tf_op jit(solution)/shard_map/pallas_call | solution.py:25
  18.4 0.1 collective-permute-start.2
  18.5 7.7 %collective-permute-start.3 = (bf16[384,768]{1,0:T(8,128)(2,1)S(1)}, bf16[384,768]{1,0:T(8,128)(2,1)S(1)}, u32[]{:S(2)}, u32[]{:S(2)}) collective-permute-start(bf16[384,768]{1,0:T(8,128)(2,1)S(1)} %get-tuple-element.28.sent_x), channel_id=1, source_target_pairs={{1,2},{2,1},{3,4},{4,3},{5,6},{6,5},{7,8},{8,7},{9,10},{10,9},{11,... | collective-permute-start | bytes 1769480 | tf_op jit(solution)/shard_map/ppermute | solution.py:267
  26.3 2.3 %shard_map.81 = (bf16[256,2304]{1,0:T(8,128)(2,1)S(1)}, f32[256,768]{1,0:T(8,128)S(1)}) custom-call(s32[1]{0:T(128)} %bitcast.index, bf16[1536,2304]{1,0:T(8,128)(2,1)S(1)} %get-tuple-element.20.dense, bf16[1536,256]{1,0:T(8,128)(2,1)S(1)} %shard_map.75.p_s, bf16[1536,256]{1,0:T(8,128)(2,1)S(1)} %get-tuple-element.24.p_x), custom_call_target="tpu_custom_call" | custom-call | flops 2415919104 | bytes 8650756 | tf_op jit(solution)/shard_map/pallas_call | solution.py:25
  28.5 0.6 %shard_map.82 = (bf16[256,2304]{1,0:T(8,128)(2,1)S(1)}, f32[256,768]{1,0:T(8,128)S(1)}) custom-call(s32[1]{0:T(128)} %bitcast.index, bf16[1536,2304]{1,0:T(8,128)(2,1)S(1)} %get-tuple-element.20.dense, bf16[1536,256]{1,0:T(8,128)(2,1)S(1)} %shard_map.75.p_s, ...), custom_call_target="tpu_custom_call", output_to_operand_aliasing={{0}: (5, {}), {1}: (6, {})} | custom-call | flops 2415919104 | bytes 11403268 | tf_op jit(solution)/shard_map/pallas_call | solution.py:25
  29.1 0.0 collective-permute-done.2.far_s
  29.1 0.4 shard_map.83
  29.5 2.1 %collective-permute-start.5 = (bf16[256,1408]{1,0:T(8,128)(2,1)S(1)}, bf16[256,1408]{1,0:T(8,128)(2,1)S(1)}, u32[]{:S(2)}, u32[]{:S(2)}) collective-permute-start(bf16[256,1408]{1,0:T(8,128)(2,1)S(1)} %shard_map.83), channel_id=1, source_target_pairs={{1,2},{2,1},{3,4},{4,3},{5,6},{6,5},{7,8},{8,7},{9,10},{10,9},{11,... | collective-permute-start | bytes 2162696 | tf_op jit(solution)/shard_map/ppermute | solution.py:267
  31.6 2.7 %shard_map.78 = (bf16[256,2304]{1,0:T(8,128)(2,1)S(1)}, f32[256,768]{1,0:T(8,128)S(1)}) custom-call(bf16[1536,2304]{1,0:T(8,128)(2,1)S(1)} %get-tuple-element.20.dense, bf16[1536,256]{1,0:T(8,128)(2,1)S(1)} %shard_map.75.p_s, bf16[1536,256]{1,0:T(8,128)(2,1)S(1)} %get-tuple-element.23.p_own, bf16[1536,256]{1,0:T(8,128)(2,1)S(1)} %get-tuple-element.24.p_x), custom_call_target="tpu_custom_call" | custom-call | flops 2415919104 | bytes 9437184 | tf_op jit(solution)/shard_map/pallas_call | solution.py:25
  34.2 0.0 collective-permute-done.3.far_x
  34.2 0.6 %shard_map.79 = bf16[256,1280]{1,0:T(8,128)(2,1)S(1)} custom-call(f32[256,768]{1,0:T(8,128)S(1)} %get-tuple-element.29.gal, bf16[256,2304]{1,0:T(8,128)(2,1)S(1)} %get-tuple-element.30.y, bf16[384,768]{1,0:T(8,128)(2,1)S(1)} %collective-permute-done.2.far_s, bf16[384,768]{1,0:T(8,128)(2,1)S(1)} %collective-permute-done.3.far_x), custom_call_target="tpu_custom_call" | custom-call | flops 301989888 | bytes 3145728 | tf_op jit(solution)/shard_map/pallas_call | solution.py:25
  34.8 0.3 collective-permute-start.4
  35.1 2.7 %shard_map.77 = (bf16[256,2304]{1,0:T(8,128)(2,1)S(1)}, f32[256,768]{1,0:T(8,128)S(1)}) custom-call(bf16[1536,2304]{1,0:T(8,128)(2,1)S(1)} %get-tuple-element.20.dense, bf16[1536,256]{1,0:T(8,128)(2,1)S(1)} %shard_map.75.p_s, bf16[1536,256]{1,0:T(8,128)(2,1)S(1)} %get-tuple-element.23.p_own, bf16[1536,256]{1,0:T(8,128)(2,1)S(1)} %get-tuple-element.24.p_x), custom_call_target="tpu_custom_call" | custom-call | flops 2415919104 | bytes 9437184 | tf_op jit(solution)/shard_map/pallas_call | solution.py:25
  37.8 0.0 collective-permute-done.4.from_s
  37.8 0.6 %shard_map.80.mine = f32[256,1792]{1,0:T(8,128)S(1)} custom-call(f32[256,768]{1,0:T(8,128)S(1)} %get-tuple-element.25.gal, bf16[256,2304]{1,0:T(8,128)(2,1)S(1)} %get-tuple-element.26.y, bf16[384,768]{1,0:T(8,128)(2,1)S(1)} %collective-permute-done.2.far_s, bf16[384,768]{1,0:T(8,128)(2,1)S(1)} %collective-permute-done.3.far_x, ...), custom_call_target="tpu_custom_call" | custom-call | flops 301989888 | bytes 3801088 | tf_op jit(solution)/shard_map/pallas_call | solution.py:25
  38.3 8.0 %collective-permute-done.5.from_x = bf16[256,1408]{1,0:T(8,128)(2,1)S(1)} collective-permute-done((bf16[256,1408]{1,0:T(8,128)(2,1)S(1)}, bf16[256,1408]{1,0:T(8,128)(2,1)S(1)}, u32[]{:S(2)}, u32[]{:S(2)}) %collective-permute-start.5) | collective-permute-done | bytes 720928 | tf_op jit(solution)/shard_map/ppermute | solution.py:267
  46.3 1.2 %shard_map.84 = bf16[256,1792]{1,0:T(8,128)(2,1)} custom-call(s32[1]{0:T(128)} %bitcast.index, f32[256,1792]{1,0:T(8,128)S(1)} %shard_map.80.mine, bf16[384,768]{1,0:T(8,128)(2,1)S(1)} %get-tuple-element.28.sent_x, bf16[256,1408]{1,0:T(8,128)(2,1)S(1)} %collective-permute-done.5.from_x), custom_call_target="tpu_custom_call" | custom-call | flops 150994944 | bytes 3145732 | tf_op jit(solution)/shard_map/pallas_call | solution.py:25
Async XLA Ops:
  1.0 15.3 %collective-permute-start = (bf16[1568,128]{1,0:T(8,128)(2,1)S(1)}, bf16[1568,128]{1,0:T(8,128)(2,1)S(1)}, u32[]{:S(2)}, u32[]{:S(2)}) collective-permute-start(bf16[1568,128]{1,0:T(8,128)(2,1)S(1)} %shard_map.73.pay), channel_id=1, source_target_pairs={{0,1},{1,0},{2,3},{3,2},{4,5},{5,4},{6,7},{7,6},{8,9},{9,8},{10,11... | collective-permute-start | bytes 1204232 | tf_op jit(solution)/shard_map/ppermute | solution.py:267
  1.1 16.2 %collective-permute-start.1 = (bf16[1568,128]{1,0:T(8,128)(2,1)S(1)}, bf16[1568,128]{1,0:T(8,128)(2,1)S(1)}, u32[]{:S(2)}, u32[]{:S(2)}) collective-permute-start(bf16[1568,128]{1,0:T(8,128)(2,1)S(1)} %shard_map.73.pay), channel_id=1, source_target_pairs={{1,2},{2,1},{3,4},{4,3},{5,6},{6,5},{7,8},{8,7},{9,10},{10,9},{11,... | collective-permute-start | bytes 1204232 | tf_op jit(solution)/shard_map/ppermute | solution.py:267
  12.4 4.0 %copy-start = (s32[1,2,3]{2,1,0:T(2,128)S(1)}, s32[1,2,3]{2,1,0:T(2,128)}, u32[]{:S(2)}) copy-start(s32[1,2,3]{2,1,0:T(2,128)} %ghost.3) | copy-start | bytes 76
  18.4 10.7 %collective-permute-start.2 = (bf16[384,768]{1,0:T(8,128)(2,1)S(1)}, bf16[384,768]{1,0:T(8,128)(2,1)S(1)}, u32[]{:S(2)}, u32[]{:S(2)}) collective-permute-start(bf16[384,768]{1,0:T(8,128)(2,1)S(1)} %get-tuple-element.27), channel_id=1, source_target_pairs={{0,1},{1,0},{2,3},{3,2},{4,5},{5,4},{6,7},{7,6},{8,9},{9,8},{10,11... | collective-permute-start | bytes 1769480 | tf_op jit(solution)/shard_map/ppermute | solution.py:267
  18.5 15.7 %collective-permute-start.3 = (bf16[384,768]{1,0:T(8,128)(2,1)S(1)}, bf16[384,768]{1,0:T(8,128)(2,1)S(1)}, u32[]{:S(2)}, u32[]{:S(2)}) collective-permute-start(bf16[384,768]{1,0:T(8,128)(2,1)S(1)} %get-tuple-element.28.sent_x), channel_id=1, source_target_pairs={{1,2},{2,1},{3,4},{4,3},{5,6},{6,5},{7,8},{8,7},{9,10},{10,9},{11,... | collective-permute-start | bytes 1769480 | tf_op jit(solution)/shard_map/ppermute | solution.py:267
  29.5 16.8 %collective-permute-start.5 = (bf16[256,1408]{1,0:T(8,128)(2,1)S(1)}, bf16[256,1408]{1,0:T(8,128)(2,1)S(1)}, u32[]{:S(2)}, u32[]{:S(2)}) collective-permute-start(bf16[256,1408]{1,0:T(8,128)(2,1)S(1)} %shard_map.83), channel_id=1, source_target_pairs={{1,2},{2,1},{3,4},{4,3},{5,6},{6,5},{7,8},{8,7},{9,10},{10,9},{11,... | collective-permute-start | bytes 2162696 | tf_op jit(solution)/shard_map/ppermute | solution.py:267
  34.8 2.9 %collective-permute-start.4 = (bf16[256,1280]{1,0:T(8,128)(2,1)S(1)}, bf16[256,1280]{1,0:T(8,128)(2,1)S(1)}, u32[]{:S(2)}, u32[]{:S(2)}) collective-permute-start(bf16[256,1280]{1,0:T(8,128)(2,1)S(1)} %shard_map.79), channel_id=1, source_target_pairs={{0,1},{1,0},{2,3},{3,2},{4,5},{5,4},{6,7},{7,6},{8,9},{9,8},{10,11... | collective-permute-start | bytes 1966088 | tf_op jit(solution)/shard_map/ppermute | solution.py:267
